TPU v7x, 32 devices: a whole 2x2x4 slice. The times are simulated.
32 devices in a mesh: dom: 32 (over z, y, x, core).
Axes of the slice: x: 2, y: 2, z: 4, core: 2. Of those that a mesh axis runs over, the one named last changes fastest.
Arguments:
- start_point: float32 [16384, 128], P('dom'), may hold values from -6 to 6
- residual: float32 [16384, 128], P('dom'), may hold values from -40 to 40
- direction: float32 [16384, 128], P('dom'), may hold values from -40 to 40
- send_list: int32 [32, 4, 3], P('dom'), may hold values from 0 to 3, as said below
- block_cols: int32 [128, 6], P('dom'), may hold values from 0 to 15, as said below
- block_vals: float32 [128, 6, 128, 128], P('dom'), may hold values from -0.2 to 8.1, as said below
Outputs:
- new_point: float32 [16384, 128], P('dom')
- new_residual: float32 [16384, 128], P('dom')
- new_direction: float32 [16384, 128], P('dom')
Inputs may be any that keep to these rules, and one draw needn't show every extreme that they name: send_list[t, m] lists, in its first entries, the distinct blocks of partition t that the partition at offset -off (off as in the first step) reads; between 1 and 3 of them are read for each pair, and some pair reads 3; the other entries are valid block numbers that are never read. `block_cols`: entry 0 of a block row names the row's own block; a block that couples two partitions appears in both partitions' rows, transposed; the assembled matrix is symmetric positive definite. `block_vals`: stored blocks that no coupling uses are zero.
All inputs are finite; a program needn't handle non-finite values.
Results may differ from a plain program's by a relative error of at most 0.0003.
Values sent between devices are 32-bit elements; how exact they have to be, the bound alone decides.
No kernel may reach another device: no remote copies, remote signals or barrier semaphores. Data moves between devices by JAX's collectives and lax.ppermute only.
A program may use at most 128 MiB of HBM per device.

v0:
```python
import jax
import jax.numpy as jnp
from jax import lax
from jax.sharding import PartitionSpec as P

STEPS = 6
BASIS = 13


center_value = 4.5
half_range = 4.5


def from_behind(shard, axis, by):
    peers = lax.axis_size(axis)
    return lax.ppermute(shard, axis, [(i, (i + by) % peers) for i in range(peers)])


def apply_blocks(blocked, send_rows, block_cols, block_vals):
    block_count, block_rows, width = blocked.shape
    highest = lax.Precision.HIGHEST
    flat_rows = blocked.reshape(block_count, block_rows * width)
    hop_count = send_rows.shape[0] // 2
    own_ids = jnp.arange(block_count, dtype=jnp.int32)
    pieces = [flat_rows]
    for slot_index in range(2 * hop_count):
        offset = slot_index + 1 if slot_index < hop_count else hop_count - 1 - slot_index
        chooser = (send_rows[slot_index][:, None] == own_ids[None, :]).astype(jnp.float32)
        outgoing = jnp.dot(chooser, flat_rows, precision=highest)
        pieces.append(from_behind(outgoing, "dom", -offset))
    ghost_table = jnp.concatenate(pieces, axis=0)
    ghost_ids = jnp.arange(ghost_table.shape[0], dtype=jnp.int32)
    running = jnp.zeros((block_count, block_rows, width), jnp.float32)
    for slot_index in range(block_cols.shape[1]):
        chooser = (block_cols[:, slot_index][:, None] == ghost_ids[None, :]).astype(jnp.float32)
        picked = jnp.dot(chooser, ghost_table, precision=highest).reshape(
            block_count, block_rows, width
        )
        running = running + jnp.einsum(
            "icb,ibw->icw", block_vals[:, slot_index], picked, precision=highest
        )
    return running


def next_vector(vector, send_rows, block_cols, block_vals):
    block_count = block_vals.shape[0]
    block_rows = block_vals.shape[2]
    blocked = vector.reshape(block_count, block_rows, vector.shape[1])
    image_part = apply_blocks(blocked, send_rows, block_cols, block_vals).reshape(vector.shape)
    return (image_part - center_value * vector) / half_range


def basis_change():
    positions = jnp.arange(BASIS)
    row_ids = positions[:, None]
    col_ids = positions[None, :]
    active = (col_ids < STEPS) | (col_ids > STEPS) & (col_ids < BASIS - 1)
    change_table = jnp.where(active & (row_ids == col_ids), center_value, 0.0)
    change_table = change_table + jnp.where(active & (row_ids == col_ids + 1), half_range, 0.0)
    return change_table.astype(jnp.float32)


def coefficient_steps(gram_matrix):
    change_table = basis_change()
    column_count = gram_matrix.shape[0]
    positions = jnp.arange(BASIS)
    point_c = jnp.zeros((column_count, BASIS), jnp.float32)
    resid_c = jnp.broadcast_to((positions == STEPS + 1).astype(jnp.float32), (column_count, BASIS))
    direc_c = jnp.broadcast_to((positions == 0).astype(jnp.float32), (column_count, BASIS))
    highest = lax.Precision.HIGHEST
    for step_index in range(STEPS):
        current = jnp.sum(
            resid_c * jnp.einsum("nab,nb->na", gram_matrix, resid_c, precision=highest), axis=1
        )
        moved_dir = jnp.einsum("ab,nb->na", change_table, direc_c, precision=highest)
        curvature = jnp.sum(
            direc_c * jnp.einsum("nab,nb->na", gram_matrix, moved_dir, precision=highest), axis=1
        )
        alpha_step = current / curvature
        point_c = point_c + alpha_step[:, None] * direc_c
        resid_c = resid_c - alpha_step[:, None] * moved_dir
        following = jnp.sum(
            resid_c * jnp.einsum("nab,nb->na", gram_matrix, resid_c, precision=highest), axis=1
        )
        direc_c = resid_c + (following / current)[:, None] * direc_c
    return (point_c, resid_c, direc_c)


def shards(start_point, residual, direction, send_list, block_cols, block_vals):
    send_rows = send_list[0]
    p_basis = [direction]
    r_basis = [residual]
    for power_step in range(STEPS):
        p_basis.append(next_vector(p_basis[-1], send_rows, block_cols, block_vals))
    for power_step in range(STEPS - 1):
        r_basis.append(next_vector(r_basis[-1], send_rows, block_cols, block_vals))
    basis_stack = jnp.stack(p_basis + r_basis)
    local_gram = jnp.einsum(
        "arn,brn->nab", basis_stack, basis_stack, precision=lax.Precision.HIGHEST
    )
    gram_matrix = lax.psum(local_gram, "dom")
    point_c, resid_c, direc_c = coefficient_steps(gram_matrix)
    highest = lax.Precision.HIGHEST
    new_point = start_point + jnp.einsum("na,arn->rn", point_c, basis_stack, precision=highest)
    new_residual = jnp.einsum("na,arn->rn", resid_c, basis_stack, precision=highest)
    new_direction = jnp.einsum("na,arn->rn", direc_c, basis_stack, precision=highest)
    return (new_point, new_residual, new_direction)


def solution(mesh):
    return jax.shard_map(
        shards,
        mesh=mesh,
        in_specs=(
            P("dom", None),
            P("dom", None),
            P("dom", None),
            P("dom", None, None),
            P("dom", None),
            P("dom", None, None, None),
        ),
        out_specs=(P("dom", None), P("dom", None), P("dom", None)),
        check_vma=False,
    )
```

profile of v0, /device:TPU:0, one launch (start us, length us, event | category | flops | bytes accessed | tf_op | source)
XLA Modules:
  0.0 516.2 jit_solution(13102410080200635533)
XLA Ops:
  7.2 1.2 slice_reduce_fusion.6
  9.9 6.5 %collective-permute-start.24 = (f32[3,16384]{1,0:T(4,128)S(1)}, f32[3,16384]{1,0:T(4,128)S(1)}, u32[]{:S(2)}, u32[]{:S(2)}) collective-permute-start(f32[3,16384]{1,0:T(4,128)S(1)} %fusion.361), channel_id=1, source_target_pairs={{0,31},{1,0},{2,1},{3,2},{4,3},{5,4},{6,5},{7,6},{8,7},{9,8},{10,9... | collective-permute-start | bytes 589832 | tf_op jit(solution)/shard_map/ppermute | solution.py:16
  18.6 1.3 collective-permute-start.27
  21.1 5.0 collective-permute-start
  32.6 7.7 %collective-permute-start.3 = (f32[3,16384]{1,0:T(4,128)}, f32[3,16384]{1,0:T(4,128)}, u32[]{:S(2)}, u32[]{:S(2)}) collective-permute-start(f32[3,16384]{1,0:T(4,128)} %fusion.334), channel_id=1, source_target_pairs={{0,2},{1,3},{2,4},{3,5},{4,6},{5,7},{6,8},{7,9},{8,10},{9,11},{10,... | collective-permute-start | bytes 589832 | tf_op jit(solution)/shard_map/ppermute | solution.py:16
  40.3 2.2 concatenate.39
  53.3 6.4 %concatenate.33 = f32[16,16384]{1,0:T(8,128)S(1)} concatenate(f32[4,16384]{1,0:T(4,128)S(1)} %reshape_reshape.33, f32[3,16384]{1,0:T(4,128)} %collective-permute-done, f32[3,16384]{1,0:T(4,128)} %collective-permute-done.1, f32[3,16384]{1,0:T(4,128)} %collective-permute-done.2, f32[3,16384]{1,0:T(4,128)} %collective-permute-done.3), dimensions={0} | concatenate | bytes 2097152 | tf_op jit(solution)/shard_map/concatenate | solution.py:31
  69.0 2.6 collective-permute-start.28
  71.7 1.9 collective-permute-start.31
  73.6 5.0 collective-permute-start.4
  81.7 1.9 collective-permute-start.5
  83.7 12.6 %collective-permute-start.7 = (f32[3,16384]{1,0:T(4,128)}, f32[3,16384]{1,0:T(4,128)}, u32[]{:S(2)}, u32[]{:S(2)}) collective-permute-start(f32[3,16384]{1,0:T(4,128)} %fusion.333), channel_id=1, source_target_pairs={{0,2},{1,3},{2,4},{3,5},{4,6},{5,7},{6,8},{7,9},{8,10},{9,11},{10,... | collective-permute-start | bytes 589832 | tf_op jit(solution)/shard_map/ppermute | solution.py:16
  96.2 6.5 %concatenate.40 = f32[16,16384]{1,0:T(8,128)S(1)} concatenate(f32[4,16384]{1,0:T(4,128)S(1)} %reshape_reshape.40, f32[3,16384]{1,0:T(4,128)} %copy-done.37, f32[3,16384]{1,0:T(4,128)} %copy-done.40, f32[3,16384]{1,0:T(4,128)} %copy-done.43, f32[3,16384]{1,0:T(4,128)} %collective-permute-done.31), dimensions={0} | concatenate | bytes 2097152 | tf_op jit(solution)/shard_map/concatenate | solution.py:31
  113.2 6.7 %concatenate.34 = f32[16,16384]{1,0:T(8,128)S(1)} concatenate(f32[4,16384]{1,0:T(4,128)S(1)} %reshape_reshape.34, f32[3,16384]{1,0:T(4,128)} %collective-permute-done.4, f32[3,16384]{1,0:T(4,128)} %collective-permute-done.5, f32[3,16384]{1,0:T(4,128)} %collective-permute-done.6, f32[3,16384]{1,0:T(4,128)} %collective-permute-done.7), dimensions={0} | concatenate | bytes 2097152 | tf_op jit(solution)/shard_map/concatenate | solution.py:31
  130.8 1.7 collective-permute-start.34
  132.9 4.6 collective-permute-start.32
  139.3 1.5 collective-permute-done.34
  140.8 10.1 %collective-permute-start.9 = (f32[3,16384]{1,0:T(4,128)}, f32[3,16384]{1,0:T(4,128)}, u32[]{:S(2)}, u32[]{:S(2)}) collective-permute-start(f32[3,16384]{1,0:T(4,128)} %fusion.354), channel_id=1, source_target_pairs={{0,30},{1,31},{2,0},{3,1},{4,2},{5,3},{6,4},{7,5},{8,6},{9,7},{10,... | collective-permute-start | bytes 589832 | tf_op jit(solution)/shard_map/ppermute | solution.py:16
  151.0 5.4 %collective-permute-start.8 = (f32[3,16384]{1,0:T(4,128)}, f32[3,16384]{1,0:T(4,128)}, u32[]{:S(2)}, u32[]{:S(2)}) collective-permute-start(f32[3,16384]{1,0:T(4,128)} %fusion.365), channel_id=1, source_target_pairs={{0,31},{1,0},{2,1},{3,2},{4,3},{5,4},{6,5},{7,6},{8,7},{9,8},{10,9... | collective-permute-start | bytes 589832 | tf_op jit(solution)/shard_map/ppermute | solution.py:16
  156.4 3.3 concatenate.41
  170.9 6.4 %concatenate.35 = f32[16,16384]{1,0:T(8,128)S(1)} concatenate(f32[4,16384]{1,0:T(4,128)S(1)} %reshape_reshape.35, f32[3,16384]{1,0:T(4,128)} %collective-permute-done.8, f32[3,16384]{1,0:T(4,128)} %collective-permute-done.9, f32[3,16384]{1,0:T(4,128)} %collective-permute-done.10, f32[3,16384]{1,0:T(4,128)} %collective-permute-done.11), dimensions={0} | concatenate | bytes 2097152 | tf_op jit(solution)/shard_map/concatenate | solution.py:31
  188.2 3.5 collective-permute-start.38
  191.7 2.6 collective-permute-start.39
  195.3 4.1 collective-permute-start.12
  201.6 4.5 collective-permute-done.37
  206.1 6.6 %collective-permute-start.15 = (f32[3,16384]{1,0:T(4,128)}, f32[3,16384]{1,0:T(4,128)}, u32[]{:S(2)}, u32[]{:S(2)}) collective-permute-start(f32[3,16384]{1,0:T(4,128)} %fusion.331), channel_id=1, source_target_pairs={{0,2},{1,3},{2,4},{3,5},{4,6},{5,7},{6,8},{7,9},{8,10},{9,11},{10,... | collective-permute-start | bytes 589832 | tf_op jit(solution)/shard_map/ppermute | solution.py:16
  212.7 6.5 %concatenate.42 = f32[16,16384]{1,0:T(8,128)S(1)} concatenate(f32[4,16384]{1,0:T(4,128)S(1)} %reshape_reshape.42, f32[3,16384]{1,0:T(4,128)} %copy-done.38, f32[3,16384]{1,0:T(4,128)} %copy-done.41, f32[3,16384]{1,0:T(4,128)} %copy-done.44, f32[3,16384]{1,0:T(4,128)} %collective-permute-done.39), dimensions={0} | concatenate | bytes 2097152 | tf_op jit(solution)/shard_map/concatenate | solution.py:31
  230.3 6.7 %concatenate.36 = f32[16,16384]{1,0:T(8,128)S(1)} concatenate(f32[4,16384]{1,0:T(4,128)S(1)} %reshape_reshape.36, f32[3,16384]{1,0:T(4,128)} %collective-permute-done.12, f32[3,16384]{1,0:T(4,128)} %collective-permute-done.13, f32[3,16384]{1,0:T(4,128)} %collective-permute-done.14, f32[3,16384]{1,0:T(4,128)} %collective-permute-done.15), dimensions={0} | concatenate | bytes 2097152 | tf_op jit(solution)/shard_map/concatenate | solution.py:31
  246.2 2.7 collective-permute-start.40
  249.2 1.7 collective-permute-start.43
  251.9 5.1 collective-permute-start.16
  259.1 1.4 collective-permute-start.17
  261.5 14.8 %collective-permute-start.19 = (f32[3,16384]{1,0:T(4,128)}, f32[3,16384]{1,0:T(4,128)}, u32[]{:S(2)}, u32[]{:S(2)}) collective-permute-start(f32[3,16384]{1,0:T(4,128)} %fusion.330), channel_id=1, source_target_pairs={{0,2},{1,3},{2,4},{3,5},{4,6},{5,7},{6,8},{7,9},{8,10},{9,11},{10,... | collective-permute-start | bytes 589832 | tf_op jit(solution)/shard_map/ppermute | solution.py:16
  276.4 6.2 %concatenate.43 = f32[16,16384]{1,0:T(8,128)S(1)} concatenate(f32[4,16384]{1,0:T(4,128)S(1)} %reshape_reshape.43, f32[3,16384]{1,0:T(4,128)} %copy-done.39, f32[3,16384]{1,0:T(4,128)} %copy-done.42, f32[3,16384]{1,0:T(4,128)} %copy-done.45, f32[3,16384]{1,0:T(4,128)} %collective-permute-done.43), dimensions={0} | concatenate | bytes 2097152 | tf_op jit(solution)/shard_map/concatenate | solution.py:31
  282.6 1.2 convolution_bitcast_fusion.5
  287.4 1.2 convolution_bitcast_fusion.1
  288.5 1.2 convolution_bitcast_fusion
  289.8 6.4 %concatenate.37 = f32[16,16384]{1,0:T(8,128)S(1)} concatenate(f32[4,16384]{1,0:T(4,128)S(1)} %reshape_reshape.37, f32[3,16384]{1,0:T(4,128)} %collective-permute-done.16, f32[3,16384]{1,0:T(4,128)} %collective-permute-done.17, f32[3,16384]{1,0:T(4,128)} %collective-permute-done.18, f32[3,16384]{1,0:T(4,128)} %collective-permute-done.19), dimensions={0} | concatenate | bytes 2097152 | tf_op jit(solution)/shard_map/concatenate | solution.py:31
  308.4 2.7 collective-permute-start.20
  311.3 1.8 collective-permute-start.23
  314.7 3.0 collective-permute-done.20
  317.6 5.8 %collective-permute-done.21 = f32[3,16384]{1,0:T(4,128)S(1)} collective-permute-done((f32[3,16384]{1,0:T(4,128)}, f32[3,16384]{1,0:T(4,128)S(1)}, u32[]{:S(2)}, u32[]{:S(2)}) %collective-permute-start.21) | collective-permute-done | bytes 196640 | tf_op jit(solution)/shard_map/ppermute | solution.py:16
  324.8 6.2 %concatenate.38 = f32[16,16384]{1,0:T(8,128)S(1)} concatenate(f32[4,16384]{1,0:T(4,128)S(1)} %reshape_reshape.38, f32[3,16384]{1,0:T(4,128)} %copy-done.47, f32[3,16384]{1,0:T(4,128)} %copy-done.49, f32[3,16384]{1,0:T(4,128)} %copy-done.50, f32[3,16384]{1,0:T(4,128)} %collective-permute-done.23), dimensions={0} | concatenate | bytes 2097152 | tf_op jit(solution)/shard_map/concatenate | solution.py:31
  338.0 9.0 %stack.55 = f32[13,512,128]{1,0,2:T(8,128)} concatenate(f32[1,512,128]{1,0,2:T(1,128)S(1)} %copy-done.27, f32[1,512,128]{1,0,2:T(1,128)S(1)} %copy-done.30, f32[1,512,128]{1,0,2:T(1,128)S(1)} %copy-done.32, f32[1,512,128]{1,0,2:T(1,128)S(1)} %copy-done.34, f32[1,512,128]{1,0,2:T(1,128)S(1)} %copy-done.35, f32[1,512,128]{1,0,2:T(1,128)S(1)} %copy.74, f32[1,512,128]{1,0,2:T(1,128)S(1)} %copy.75, ...), dimensions={0} | concatenate | bytes 6815744 | tf_op jit(solution)/shard_map/stack | solution.py:97
  347.0 10.0 %fusion.499 = f32[128,13,13]{2,1,0:T(8,128)} fusion(f32[13,512,128]{1,0,2:T(8,128)} %stack.55), kind=kOutput, calls=%fused_computation.689 | convolution fusion | flops 132907008 | bytes 3494400 | tf_op jit(solution)/shard_map/arn,brn->nab/dot_general | solution.py:98
  357.2 134.9 %all-reduce.2.cloned.1.call-done = f32[128,13,13]{2,1,0:T(8,128)} async-done(((f32[128,13,13]{2,1,0:T(8,128)}), f32[128,13,13]{2,1,0:T(8,128)}) %all-reduce.2.cloned.1.call-update) | async-done | bytes 86544 | tf_op jit(solution)/shard_map/psum | solution.py:101
  492.1 1.9 multiply_reduce_fusion.14
  502.3 4.3 multiply_reduce_fusion
  (496 shorter events, 142.8 us)
Async XLA Ops:
  7.2 484.9 %all-reduce.2.cloned.1.call-start = ((), (), s32[]{:S(2)}) async-start(), calls=%async_computation | async-start | bytes 2097152 | tf_op jit(solution)/shard_map/psum | solution.py:101
  9.9 22.1 %collective-permute-start.24 = (f32[3,16384]{1,0:T(4,128)S(1)}, f32[3,16384]{1,0:T(4,128)S(1)}, u32[]{:S(2)}, u32[]{:S(2)}) collective-permute-start(f32[3,16384]{1,0:T(4,128)S(1)} %fusion.361), channel_id=1, source_target_pairs={{0,31},{1,0},{2,1},{3,2},{4,3},{5,4},{6,5},{7,6},{8,7},{9,8},{10,9... | collective-permute-start | bytes 589832 | tf_op jit(solution)/shard_map/ppermute | solution.py:16
  16.8 15.8 %collective-permute-start.25 = (f32[3,16384]{1,0:T(4,128)S(1)}, f32[3,16384]{1,0:T(4,128)S(1)}, u32[]{:S(2)}, u32[]{:S(2)}) collective-permute-start(f32[3,16384]{1,0:T(4,128)S(1)} %fusion.350), channel_id=1, source_target_pairs={{0,30},{1,31},{2,0},{3,1},{4,2},{5,3},{6,4},{7,5},{8,6},{9,7},{10,... | collective-permute-start | bytes 589832 | tf_op jit(solution)/shard_map/ppermute | solution.py:16
  17.9 14.7 %collective-permute-start.26 = (f32[3,16384]{1,0:T(4,128)S(1)}, f32[3,16384]{1,0:T(4,128)S(1)}, u32[]{:S(2)}, u32[]{:S(2)}) collective-permute-start(f32[3,16384]{1,0:T(4,128)S(1)} %fusion.339), channel_id=1, source_target_pairs={{0,1},{1,2},{2,3},{3,4},{4,5},{5,6},{6,7},{7,8},{8,9},{9,10},{10,1... | collective-permute-start | bytes 589832 | tf_op jit(solution)/shard_map/ppermute | solution.py:16
  18.6 21.8 %collective-permute-start.27 = (f32[3,16384]{1,0:T(4,128)S(1)}, f32[3,16384]{1,0:T(4,128)}, u32[]{:S(2)}, u32[]{:S(2)}) collective-permute-start(f32[3,16384]{1,0:T(4,128)S(1)} %fusion.328), channel_id=1, source_target_pairs={{0,2},{1,3},{2,4},{3,5},{4,6},{5,7},{6,8},{7,9},{8,10},{9,11},{10,... | collective-permute-start | bytes 589832 | tf_op jit(solution)/shard_map/ppermute | solution.py:16
  21.1 32.2 %collective-permute-start = (f32[3,16384]{1,0:T(4,128)}, f32[3,16384]{1,0:T(4,128)}, u32[]{:S(2)}, u32[]{:S(2)}) collective-permute-start(f32[3,16384]{1,0:T(4,128)} %fusion.367), channel_id=1, source_target_pairs={{0,31},{1,0},{2,1},{3,2},{4,3},{5,4},{6,5},{7,6},{8,7},{9,8},{10,9... | collective-permute-start | bytes 589832 | tf_op jit(solution)/shard_map/ppermute | solution.py:16
  26.3 22.2 %copy-start.4 = (f32[512,128]{0,1:T(8,128)}, f32[512,128]{0,1:T(8,128)S(1)}, u32[]{:S(2)}) copy-start(f32[512,128]{0,1:T(8,128)S(1)} %copy.60) | copy-start | bytes 786436
  29.8 35.4 %copy-start.2 = (f32[512,128]{0,1:T(8,128)}, f32[512,128]{0,1:T(8,128)S(1)}, u32[]{:S(2)}) copy-start(f32[512,128]{0,1:T(8,128)S(1)} %copy.47) | copy-start | bytes 786436
  32.0 21.3 %collective-permute-start.1 = (f32[3,16384]{1,0:T(4,128)}, f32[3,16384]{1,0:T(4,128)}, u32[]{:S(2)}, u32[]{:S(2)}) collective-permute-start(f32[3,16384]{1,0:T(4,128)} %fusion.356), channel_id=1, source_target_pairs={{0,30},{1,31},{2,0},{3,1},{4,2},{5,3},{6,4},{7,5},{8,6},{9,7},{10,... | collective-permute-start | bytes 589832 | tf_op jit(solution)/shard_map/ppermute | solution.py:16
  32.6 20.7 %collective-permute-start.2 = (f32[3,16384]{1,0:T(4,128)}, f32[3,16384]{1,0:T(4,128)}, u32[]{:S(2)}, u32[]{:S(2)}) collective-permute-start(f32[3,16384]{1,0:T(4,128)} %fusion.345), channel_id=1, source_target_pairs={{0,1},{1,2},{2,3},{3,4},{4,5},{5,6},{6,7},{7,8},{8,9},{9,10},{10,1... | collective-permute-start | bytes 589832 | tf_op jit(solution)/shard_map/ppermute | solution.py:16
  32.6 20.7 %collective-permute-start.3 = (f32[3,16384]{1,0:T(4,128)}, f32[3,16384]{1,0:T(4,128)}, u32[]{:S(2)}, u32[]{:S(2)}) collective-permute-start(f32[3,16384]{1,0:T(4,128)} %fusion.334), channel_id=1, source_target_pairs={{0,2},{1,3},{2,4},{3,5},{4,6},{5,7},{6,8},{7,9},{8,10},{9,11},{10,... | collective-permute-start | bytes 589832 | tf_op jit(solution)/shard_map/ppermute | solution.py:16
  69.0 12.8 %collective-permute-start.28 = (f32[3,16384]{1,0:T(4,128)S(1)}, f32[3,16384]{1,0:T(4,128)S(1)}, u32[]{:S(2)}, u32[]{:S(2)}) collective-permute-start(f32[3,16384]{1,0:T(4,128)S(1)} %copy-done.56), channel_id=1, source_target_pairs={{0,31},{1,0},{2,1},{3,2},{4,3},{5,4},{6,5},{7,6},{8,7},{9,8},{10,9... | collective-permute-start | bytes 589832 | tf_op jit(solution)/shard_map/ppermute | solution.py:16
  71.5 12.1 %collective-permute-start.29 = (f32[3,16384]{1,0:T(4,128)S(1)}, f32[3,16384]{1,0:T(4,128)S(1)}, u32[]{:S(2)}, u32[]{:S(2)}) collective-permute-start(f32[3,16384]{1,0:T(4,128)S(1)} %copy-done.55), channel_id=1, source_target_pairs={{0,30},{1,31},{2,0},{3,1},{4,2},{5,3},{6,4},{7,5},{8,6},{9,7},{10,... | collective-permute-start | bytes 589832 | tf_op jit(solution)/shard_map/ppermute | solution.py:16
  71.6 12.1 %collective-permute-start.30 = (f32[3,16384]{1,0:T(4,128)S(1)}, f32[3,16384]{1,0:T(4,128)S(1)}, u32[]{:S(2)}, u32[]{:S(2)}) collective-permute-start(f32[3,16384]{1,0:T(4,128)S(1)} %copy-done.53), channel_id=1, source_target_pairs={{0,1},{1,2},{2,3},{3,4},{4,5},{5,6},{6,7},{7,8},{8,9},{9,10},{10,1... | collective-permute-start | bytes 589832 | tf_op jit(solution)/shard_map/ppermute | solution.py:16
  71.7 24.5 %collective-permute-start.31 = (f32[3,16384]{1,0:T(4,128)S(1)}, f32[3,16384]{1,0:T(4,128)}, u32[]{:S(2)}, u32[]{:S(2)}) collective-permute-start(f32[3,16384]{1,0:T(4,128)S(1)} %copy-done.51), channel_id=1, source_target_pairs={{0,2},{1,3},{2,4},{3,5},{4,6},{5,7},{6,8},{7,9},{8,10},{9,11},{10,... | collective-permute-start | bytes 589832 | tf_op jit(solution)/shard_map/ppermute | solution.py:16
  73.6 39.5 %collective-permute-start.4 = (f32[3,16384]{1,0:T(4,128)}, f32[3,16384]{1,0:T(4,128)}, u32[]{:S(2)}, u32[]{:S(2)}) collective-permute-start(f32[3,16384]{1,0:T(4,128)} %fusion.366), channel_id=1, source_target_pairs={{0,31},{1,0},{2,1},{3,2},{4,3},{5,4},{6,5},{7,6},{8,7},{9,8},{10,9... | collective-permute-start | bytes 589832 | tf_op jit(solution)/shard_map/ppermute | solution.py:16
  81.7 31.4 %collective-permute-start.5 = (f32[3,16384]{1,0:T(4,128)}, f32[3,16384]{1,0:T(4,128)}, u32[]{:S(2)}, u32[]{:S(2)}) collective-permute-start(f32[3,16384]{1,0:T(4,128)} %fusion.355), channel_id=1, source_target_pairs={{0,30},{1,31},{2,0},{3,1},{4,2},{5,3},{6,4},{7,5},{8,6},{9,7},{10,... | collective-permute-start | bytes 589832 | tf_op jit(solution)/shard_map/ppermute | solution.py:16
  83.6 29.5 %collective-permute-start.6 = (f32[3,16384]{1,0:T(4,128)}, f32[3,16384]{1,0:T(4,128)}, u32[]{:S(2)}, u32[]{:S(2)}) collective-permute-start(f32[3,16384]{1,0:T(4,128)} %fusion.344), channel_id=1, source_target_pairs={{0,1},{1,2},{2,3},{3,4},{4,5},{5,6},{6,7},{7,8},{8,9},{9,10},{10,1... | collective-permute-start | bytes 589832 | tf_op jit(solution)/shard_map/ppermute | solution.py:16
  83.7 29.5 %collective-permute-start.7 = (f32[3,16384]{1,0:T(4,128)}, f32[3,16384]{1,0:T(4,128)}, u32[]{:S(2)}, u32[]{:S(2)}) collective-permute-start(f32[3,16384]{1,0:T(4,128)} %fusion.333), channel_id=1, source_target_pairs={{0,2},{1,3},{2,4},{3,5},{4,6},{5,7},{6,8},{7,9},{8,10},{9,11},{10,... | collective-permute-start | bytes 589832 | tf_op jit(solution)/shard_map/ppermute | solution.py:16
  129.8 9.1 %collective-permute-start.33 = (f32[3,16384]{1,0:T(4,128)}, f32[3,16384]{1,0:T(4,128)S(1)}, u32[]{:S(2)}, u32[]{:S(2)}) collective-permute-start(f32[3,16384]{1,0:T(4,128)} %fusion.348), channel_id=1, source_target_pairs={{0,30},{1,31},{2,0},{3,1},{4,2},{5,3},{6,4},{7,5},{8,6},{9,7},{10,... | collective-permute-start | bytes 589832 | tf_op jit(solution)/shard_map/ppermute | solution.py:16
  130.8 10.0 %collective-permute-start.34 = (f32[3,16384]{1,0:T(4,128)S(1)}, f32[3,16384]{1,0:T(4,128)S(1)}, u32[]{:S(2)}, u32[]{:S(2)}) collective-permute-start(f32[3,16384]{1,0:T(4,128)S(1)} %copy-done.54), channel_id=1, source_target_pairs={{0,1},{1,2},{2,3},{3,4},{4,5},{5,6},{6,7},{7,8},{8,9},{9,10},{10,1... | collective-permute-start | bytes 589832 | tf_op jit(solution)/shard_map/ppermute | solution.py:16
  132.5 18.5 %collective-permute-start.35 = (f32[3,16384]{1,0:T(4,128)S(1)}, f32[3,16384]{1,0:T(4,128)S(1)}, u32[]{:S(2)}, u32[]{:S(2)}) collective-permute-start(f32[3,16384]{1,0:T(4,128)S(1)} %copy-done.52), channel_id=1, source_target_pairs={{0,2},{1,3},{2,4},{3,5},{4,6},{5,7},{6,8},{7,9},{8,10},{9,11},{10,... | collective-permute-start | bytes 589832 | tf_op jit(solution)/shard_map/ppermute | solution.py:16
  132.9 23.6 %collective-permute-start.32 = (f32[3,16384]{1,0:T(4,128)S(1)}, f32[3,16384]{1,0:T(4,128)}, u32[]{:S(2)}, u32[]{:S(2)}) collective-permute-start(f32[3,16384]{1,0:T(4,128)S(1)} %fusion.359), channel_id=1, source_target_pairs={{0,31},{1,0},{2,1},{3,2},{4,3},{5,4},{6,5},{7,6},{8,7},{9,8},{10,9... | collective-permute-start | bytes 589832 | tf_op jit(solution)/shard_map/ppermute | solution.py:16
  137.5 33.3 %collective-permute-start.10 = (f32[3,16384]{1,0:T(4,128)}, f32[3,16384]{1,0:T(4,128)}, u32[]{:S(2)}, u32[]{:S(2)}) collective-permute-start(f32[3,16384]{1,0:T(4,128)} %fusion.343), channel_id=1, source_target_pairs={{0,1},{1,2},{2,3},{3,4},{4,5},{5,6},{6,7},{7,8},{8,9},{9,10},{10,1... | collective-permute-start | bytes 589832 | tf_op jit(solution)/shard_map/ppermute | solution.py:16
  138.9 32.0 %collective-permute-start.11 = (f32[3,16384]{1,0:T(4,128)}, f32[3,16384]{1,0:T(4,128)}, u32[]{:S(2)}, u32[]{:S(2)}) collective-permute-start(f32[3,16384]{1,0:T(4,128)} %fusion.332), channel_id=1, source_target_pairs={{0,2},{1,3},{2,4},{3,5},{4,6},{5,7},{6,8},{7,9},{8,10},{9,11},{10,... | collective-permute-start | bytes 589832 | tf_op jit(solution)/shard_map/ppermute | solution.py:16
  140.8 30.0 %collective-permute-start.9 = (f32[3,16384]{1,0:T(4,128)}, f32[3,16384]{1,0:T(4,128)}, u32[]{:S(2)}, u32[]{:S(2)}) collective-permute-start(f32[3,16384]{1,0:T(4,128)} %fusion.354), channel_id=1, source_target_pairs={{0,30},{1,31},{2,0},{3,1},{4,2},{5,3},{6,4},{7,5},{8,6},{9,7},{10,... | collective-permute-start | bytes 589832 | tf_op jit(solution)/shard_map/ppermute | solution.py:16
  151.0 19.9 %collective-permute-start.8 = (f32[3,16384]{1,0:T(4,128)}, f32[3,16384]{1,0:T(4,128)}, u32[]{:S(2)}, u32[]{:S(2)}) collective-permute-start(f32[3,16384]{1,0:T(4,128)} %fusion.365), channel_id=1, source_target_pairs={{0,31},{1,0},{2,1},{3,2},{4,3},{5,4},{6,5},{7,6},{8,7},{9,8},{10,9... | collective-permute-start | bytes 589832 | tf_op jit(solution)/shard_map/ppermute | solution.py:16
  187.2 14.3 %collective-permute-start.36 = (f32[3,16384]{1,0:T(4,128)}, f32[3,16384]{1,0:T(4,128)S(1)}, u32[]{:S(2)}, u32[]{:S(2)}) collective-permute-start(f32[3,16384]{1,0:T(4,128)} %fusion.358), channel_id=1, source_target_pairs={{0,31},{1,0},{2,1},{3,2},{4,3},{5,4},{6,5},{7,6},{8,7},{9,8},{10,9... | collective-permute-start | bytes 589832 | tf_op jit(solution)/shard_map/ppermute | solution.py:16
  187.9 18.1 %collective-permute-start.37 = (f32[3,16384]{1,0:T(4,128)}, f32[3,16384]{1,0:T(4,128)S(1)}, u32[]{:S(2)}, u32[]{:S(2)}) collective-permute-start(f32[3,16384]{1,0:T(4,128)} %fusion.347), channel_id=1, source_target_pairs={{0,30},{1,31},{2,0},{3,1},{4,2},{5,3},{6,4},{7,5},{8,6},{9,7},{10,... | collective-permute-start | bytes 589832 | tf_op jit(solution)/shard_map/ppermute | solution.py:16
  188.2 17.9 %collective-permute-start.38 = (f32[3,16384]{1,0:T(4,128)}, f32[3,16384]{1,0:T(4,128)S(1)}, u32[]{:S(2)}, u32[]{:S(2)}) collective-permute-start(f32[3,16384]{1,0:T(4,128)} %fusion.336), channel_id=1, source_target_pairs={{0,1},{1,2},{2,3},{3,4},{4,5},{5,6},{6,7},{7,8},{8,9},{9,10},{10,1... | collective-permute-start | bytes 589832 | tf_op jit(solution)/shard_map/ppermute | solution.py:16
  191.7 20.9 %collective-permute-start.39 = (f32[3,16384]{1,0:T(4,128)}, f32[3,16384]{1,0:T(4,128)}, u32[]{:S(2)}, u32[]{:S(2)}) collective-permute-start(f32[3,16384]{1,0:T(4,128)} %fusion.325), channel_id=1, source_target_pairs={{0,2},{1,3},{2,4},{3,5},{4,6},{5,7},{6,8},{7,9},{8,10},{9,11},{10,... | collective-permute-start | bytes 589832 | tf_op jit(solution)/shard_map/ppermute | solution.py:16
  195.3 35.0 %collective-permute-start.12 = (f32[3,16384]{1,0:T(4,128)}, f32[3,16384]{1,0:T(4,128)}, u32[]{:S(2)}, u32[]{:S(2)}) collective-permute-start(f32[3,16384]{1,0:T(4,128)} %fusion.364), channel_id=1, source_target_pairs={{0,31},{1,0},{2,1},{3,2},{4,3},{5,4},{6,5},{7,6},{8,7},{9,8},{10,9... | collective-permute-start | bytes 589832 | tf_op jit(solution)/shard_map/ppermute | solution.py:16
  201.5 28.7 %collective-permute-start.13 = (f32[3,16384]{1,0:T(4,128)}, f32[3,16384]{1,0:T(4,128)}, u32[]{:S(2)}, u32[]{:S(2)}) collective-permute-start(f32[3,16384]{1,0:T(4,128)} %fusion.353), channel_id=1, source_target_pairs={{0,30},{1,31},{2,0},{3,1},{4,2},{5,3},{6,4},{7,5},{8,6},{9,7},{10,... | collective-permute-start | bytes 589832 | tf_op jit(solution)/shard_map/ppermute | solution.py:16
  206.1 24.2 %collective-permute-start.14 = (f32[3,16384]{1,0:T(4,128)}, f32[3,16384]{1,0:T(4,128)}, u32[]{:S(2)}, u32[]{:S(2)}) collective-permute-start(f32[3,16384]{1,0:T(4,128)} %fusion.342), channel_id=1, source_target_pairs={{0,1},{1,2},{2,3},{3,4},{4,5},{5,6},{6,7},{7,8},{8,9},{9,10},{10,1... | collective-permute-start | bytes 589832 | tf_op jit(solution)/shard_map/ppermute | solution.py:16
  206.1 24.2 %collective-permute-start.15 = (f32[3,16384]{1,0:T(4,128)}, f32[3,16384]{1,0:T(4,128)}, u32[]{:S(2)}, u32[]{:S(2)}) collective-permute-start(f32[3,16384]{1,0:T(4,128)} %fusion.331), channel_id=1, source_target_pairs={{0,2},{1,3},{2,4},{3,5},{4,6},{5,7},{6,8},{7,9},{8,10},{9,11},{10,... | collective-permute-start | bytes 589832 | tf_op jit(solution)/shard_map/ppermute | solution.py:16
  246.2 12.9 %collective-permute-start.40 = (f32[3,16384]{1,0:T(4,128)}, f32[3,16384]{1,0:T(4,128)S(1)}, u32[]{:S(2)}, u32[]{:S(2)}) collective-permute-start(f32[3,16384]{1,0:T(4,128)} %fusion.357), channel_id=1, source_target_pairs={{0,31},{1,0},{2,1},{3,2},{4,3},{5,4},{6,5},{7,6},{8,7},{9,8},{10,9... | collective-permute-start | bytes 589832 | tf_op jit(solution)/shard_map/ppermute | solution.py:16
  248.9 12.6 %collective-permute-start.41 = (f32[3,16384]{1,0:T(4,128)}, f32[3,16384]{1,0:T(4,128)S(1)}, u32[]{:S(2)}, u32[]{:S(2)}) collective-permute-start(f32[3,16384]{1,0:T(4,128)} %fusion.346), channel_id=1, source_target_pairs={{0,30},{1,31},{2,0},{3,1},{4,2},{5,3},{6,4},{7,5},{8,6},{9,7},{10,... | collective-permute-start | bytes 589832 | tf_op jit(solution)/shard_map/ppermute | solution.py:16
  248.9 12.6 %collective-permute-start.42 = (f32[3,16384]{1,0:T(4,128)}, f32[3,16384]{1,0:T(4,128)S(1)}, u32[]{:S(2)}, u32[]{:S(2)}) collective-permute-start(f32[3,16384]{1,0:T(4,128)} %fusion.335), channel_id=1, source_target_pairs={{0,1},{1,2},{2,3},{3,4},{4,5},{5,6},{6,7},{7,8},{8,9},{9,10},{10,1... | collective-permute-start | bytes 589832 | tf_op jit(solution)/shard_map/ppermute | solution.py:16
  249.2 27.2 %collective-permute-start.43 = (f32[3,16384]{1,0:T(4,128)}, f32[3,16384]{1,0:T(4,128)}, u32[]{:S(2)}, u32[]{:S(2)}) collective-permute-start(f32[3,16384]{1,0:T(4,128)} %fusion.324), channel_id=1, source_target_pairs={{0,2},{1,3},{2,4},{3,5},{4,6},{5,7},{6,8},{7,9},{8,10},{9,11},{10,... | collective-permute-start | bytes 589832 | tf_op jit(solution)/shard_map/ppermute | solution.py:16
  251.9 37.8 %collective-permute-start.16 = (f32[3,16384]{1,0:T(4,128)}, f32[3,16384]{1,0:T(4,128)}, u32[]{:S(2)}, u32[]{:S(2)}) collective-permute-start(f32[3,16384]{1,0:T(4,128)} %fusion.363), channel_id=1, source_target_pairs={{0,31},{1,0},{2,1},{3,2},{4,3},{5,4},{6,5},{7,6},{8,7},{9,8},{10,9... | collective-permute-start | bytes 589832 | tf_op jit(solution)/shard_map/ppermute | solution.py:16
  259.1 17.3 %copy-start.39 = (f32[3,16384]{1,0:T(4,128)}, f32[3,16384]{1,0:T(4,128)S(1)}, u32[]{:S(2)}) copy-start(f32[3,16384]{1,0:T(4,128)S(1)} %collective-permute-done.40) | copy-start | bytes 589828
  259.1 30.7 %collective-permute-start.17 = (f32[3,16384]{1,0:T(4,128)}, f32[3,16384]{1,0:T(4,128)}, u32[]{:S(2)}, u32[]{:S(2)}) collective-permute-start(f32[3,16384]{1,0:T(4,128)} %fusion.352), channel_id=1, source_target_pairs={{0,30},{1,31},{2,0},{3,1},{4,2},{5,3},{6,4},{7,5},{8,6},{9,7},{10,... | collective-permute-start | bytes 589832 | tf_op jit(solution)/shard_map/ppermute | solution.py:16
  261.5 28.2 %collective-permute-start.18 = (f32[3,16384]{1,0:T(4,128)}, f32[3,16384]{1,0:T(4,128)}, u32[]{:S(2)}, u32[]{:S(2)}) collective-permute-start(f32[3,16384]{1,0:T(4,128)} %fusion.341), channel_id=1, source_target_pairs={{0,1},{1,2},{2,3},{3,4},{4,5},{5,6},{6,7},{7,8},{8,9},{9,10},{10,1... | collective-permute-start | bytes 589832 | tf_op jit(solution)/shard_map/ppermute | solution.py:16
  261.5 28.2 %collective-permute-start.19 = (f32[3,16384]{1,0:T(4,128)}, f32[3,16384]{1,0:T(4,128)}, u32[]{:S(2)}, u32[]{:S(2)}) collective-permute-start(f32[3,16384]{1,0:T(4,128)} %fusion.330), channel_id=1, source_target_pairs={{0,2},{1,3},{2,4},{3,5},{4,6},{5,7},{6,8},{7,9},{8,10},{9,11},{10,... | collective-permute-start | bytes 589832 | tf_op jit(solution)/shard_map/ppermute | solution.py:16
  308.4 9.2 %collective-permute-start.20 = (f32[3,16384]{1,0:T(4,128)}, f32[3,16384]{1,0:T(4,128)S(1)}, u32[]{:S(2)}, u32[]{:S(2)}) collective-permute-start(f32[3,16384]{1,0:T(4,128)} %fusion.362), channel_id=1, source_target_pairs={{0,31},{1,0},{2,1},{3,2},{4,3},{5,4},{6,5},{7,6},{8,7},{9,8},{10,9... | collective-permute-start | bytes 589832 | tf_op jit(solution)/shard_map/ppermute | solution.py:16
  311.1 12.3 %collective-permute-start.21 = (f32[3,16384]{1,0:T(4,128)}, f32[3,16384]{1,0:T(4,128)S(1)}, u32[]{:S(2)}, u32[]{:S(2)}) collective-permute-start(f32[3,16384]{1,0:T(4,128)} %fusion.351), channel_id=1, source_target_pairs={{0,30},{1,31},{2,0},{3,1},{4,2},{5,3},{6,4},{7,5},{8,6},{9,7},{10,... | collective-permute-start | bytes 589832 | tf_op jit(solution)/shard_map/ppermute | solution.py:16
  311.1 12.3 %collective-permute-start.22 = (f32[3,16384]{1,0:T(4,128)S(1)}, f32[3,16384]{1,0:T(4,128)S(1)}, u32[]{:S(2)}, u32[]{:S(2)}) collective-permute-start(f32[3,16384]{1,0:T(4,128)S(1)} %fusion.340), channel_id=1, source_target_pairs={{0,1},{1,2},{2,3},{3,4},{4,5},{5,6},{6,7},{7,8},{8,9},{9,10},{10,1... | collective-permute-start | bytes 589832 | tf_op jit(solution)/shard_map/ppermute | solution.py:16
  311.3 13.5 %collective-permute-start.23 = (f32[3,16384]{1,0:T(4,128)S(1)}, f32[3,16384]{1,0:T(4,128)}, u32[]{:S(2)}, u32[]{:S(2)}) collective-permute-start(f32[3,16384]{1,0:T(4,128)S(1)} %fusion.329), channel_id=1, source_target_pairs={{0,2},{1,3},{2,4},{3,5},{4,6},{5,7},{6,8},{7,9},{8,10},{9,11},{10,... | collective-permute-start | bytes 589832 | tf_op jit(solution)/shard_map/ppermute | solution.py:16
  (55 other events, 281.2 us)
Sparse Core Ops, SparseCore 0:
  357.2 134.8 all-reduce.1
where the time goes:
time: 523 us; the launch traced here: 516 us
  waiting for transfers between devices  151 us (29%)
  starting transfers between devices  119 us (23%)
  matrix products  117 us (22%)
  local copies, waits for them, and re-layouts  95.6 us (18%)
  other arithmetic  17 us (3%)
  between operations  16.7 us (3%)
    psum x1, waiting for transfers between devices, shards(): gram_matrix = lax.psum(local_gram, 'dom')  135 us
    ppermute x44, starting transfers between devices, from_behind(): lax.ppermute(shard, axis, [(i, (i + by) % peers) for i in range(peers)])  118 us
    concatenate x11, local copies, waits for them, and re-layouts, apply_blocks(): ghost_table = jnp.concatenate(pieces, axis=0)  63.5 us
    dot_general x44, matrix products, apply_blocks(): outgoing = jnp.dot(chooser, flat_rows, precision=highest)  44.7 us
    dot_general x66, matrix products, apply_blocks(): jnp.dot(chooser, ghost_table, precision=highest)  36.4 us
    dot_general x66, matrix products, apply_blocks(): jnp.einsum('icb,ibw->icw', block_vals[:, slot_index], picked, precision=h...  25.2 us
    another operation x14, local copies, waits for them, and re-layouts, shards(): basis_stack = jnp.stack(p_basis + r_basis)  18.5 us
    ppermute x44, waiting for transfers between devices, from_behind(): lax.ppermute(shard, axis, [(i, (i + by) % peers) for i in range(peers)])  16 us
  transfers between devices with their start and end apart: 45, of which 7 were waited for; matrix products, arithmetic and copies ran while one was open for 18% of the time, Pallas kernels for 0%

commit v1 on v0

v1 whole, which is shorter than its diff:
```python
import functools
import jax
import jax.numpy as jnp
from jax import lax
from jax.experimental import pallas as pl
from jax.experimental.pallas import tpu as pltpu
from jax.sharding import PartitionSpec as P

STEPS = 6
CENTER = 4.5
HALF = 4.5
F32 = jnp.float32
BF16 = jnp.bfloat16
VM = pl.BlockSpec(memory_space=pltpu.VMEM)
SM = pl.BlockSpec(memory_space=pltpu.SMEM)


def call(body, out_shape, in_specs, out_specs, scratch=(), flops=0, bytes_=0, name=None, grid=None):
    extra = {} if grid is None else {"grid": grid}
    return pl.pallas_call(
        body,
        out_shape=out_shape,
        in_specs=in_specs,
        out_specs=out_specs,
        scratch_shapes=list(scratch),
        cost_estimate=pl.CostEstimate(flops=flops, bytes_accessed=bytes_, transcendentals=0),
        name=name,
        **extra,
    )


def pack_kernel(core, p_ref, r_ref, mine_ref, send_ref):
    half = p_ref.shape[1] // 2
    p, r = p_ref[...], r_ref[...]
    low = lax.broadcasted_iota(jnp.int32, p.shape, 1) < half
    first = jnp.where(low, p, pltpu.roll(r, half, 1))
    second = jnp.where(low, pltpu.roll(p, half, 1), r)
    is_first = core[0] == 0
    mine_ref[...] = jnp.where(is_first, first, second)
    send_ref[...] = jnp.where(is_first, second, first)


def copy_halo(core, lists, own, right_ref, left_ref):
    nb = right_ref.shape[0] - lists.shape[2]
    k = core[0]
    for target, whole, part, m in ((right_ref, 1, 0, 3), (left_ref, 0, 1, 1)):
        whole_slot = jnp.bitwise_xor(k, whole)
        part_slot = jnp.bitwise_xor(k, part)
        for b in range(nb):
            target[b] = own[whole_slot * nb + b]
        for e in range(lists.shape[2]):
            target[nb + e] = own[part_slot * nb + lists[part_slot, m, e]]


def first_kernel(core, lists, mine_ref, other_ref, own_ref, right_ref, left_ref):
    nb = mine_ref.shape[0]
    own_ref[:nb] = mine_ref[...]
    own_ref[nb:] = other_ref[...]
    copy_halo(core, lists, own_ref, right_ref, left_ref)


def index_kernel(core, lists, from_right, from_left, cols, out):
    k = core[0]
    cap = lists.shape[2]
    _, nb, slots = cols.shape
    right = 2 * nb
    left = 3 * nb + cap
    for s in range(2):
        t = jnp.bitwise_xor(k, s)
        is0 = t == 0
        other = 1 - s
        for b in range(nb):
            for j in range(slots):
                c = cols[s, b, j]
                place = s * nb + c
                for m in range(4):
                    for e in range(cap):
                        if m == 0:
                            v = jnp.where(is0, other * nb + lists[other, 0, e], right + from_right[k, 0, e])
                        elif m == 1:
                            v = jnp.where(is0, right + from_right[k, 1, e], right + nb + e)
                        elif m == 2:
                            v = jnp.where(is0, left + from_left[1 - k, 2, e], other * nb + lists[other, 2, e])
                        else:
                            v = jnp.where(is0, left + nb + e, left + from_left[1 - k, 3, e])
                        place = jnp.where(c == nb + m * cap + e, v, place)
                out[s * nb + b, j] = place


def matrix_kernel(a_ref, hi_ref, lo_ref):
    slots, rows, cols = a_ref.shape[1:]
    diag = lax.broadcasted_iota(jnp.int32, (rows, cols), 0) == lax.broadcasted_iota(
        jnp.int32, (rows, cols), 1
    )
    for j in range(slots):
        a = a_ref[0, j]
        if j == 0:
            a = a - jnp.where(diag, F32(CENTER), F32(0.0))
        a = a * F32(1.0 / HALF)
        hi = a.astype(BF16)
        hi_ref[0, :, j * cols : (j + 1) * cols] = hi
        lo_ref[0, :, j * cols : (j + 1) * cols] = (a - hi.astype(F32)).astype(BF16)


def step_kernel(last, core, lists, index, own_ref, fr_ref, fl_ref, h0, l0, h1, l1, new_ref, *rest):
    if last:
        (table,) = rest
    else:
        right_ref, left_ref, table = rest
    n_own, rows, width = own_ref.shape
    place = 0
    for ref in (own_ref, fr_ref, fl_ref):
        for b in range(ref.shape[0]):
            v = ref[b]
            hi = v.astype(BF16)
            table[place, :, :width] = hi
            table[place, :, width:] = (v - hi.astype(F32)).astype(BF16)
            place += 1
    half = n_own // 2
    slots = index.shape[1]
    for i in range(n_own):
        h, l = (h0, l0) if i < half else (h1, l1)
        acc = None
        for j in range(0, slots, 2):
            cols = [table[index[i, q]] for q in range(j, min(j + 2, slots))]
            tile = jnp.concatenate(cols, axis=0) if len(cols) > 1 else cols[0]
            span = slice(j * rows, (j + len(cols)) * rows)
            for part in (h, l):
                d = jnp.dot(part[i % half, :, span], tile, preferred_element_type=F32)
                acc = d if acc is None else acc + d
        new_ref[i] = acc[:, :width] + acc[:, width:]
    if not last:
        copy_halo(core, lists, new_ref, right_ref, left_ref)


def fold(x):
    return jnp.sum(x.reshape(-1, 8, x.shape[-1]), axis=0)


def moment_kernel(first, *refs):
    if first:
        now_ref, out = refs
        prev_ref = None
    else:
        now_ref, prev_ref, out = refs
    blocks, rows, width = now_ref.shape
    half = width // 2
    acc = [jnp.zeros((8, width), F32) for _ in range(4)]
    for b in range(blocks):
        s = now_ref[b]
        turned = pltpu.roll(s, half, 1)
        acc[1] += fold(s * s)
        acc[3] += fold(s * turned)
        if prev_ref is not None:
            q = prev_ref[b]
            acc[0] += fold(s * q)
            acc[2] += fold(s * pltpu.roll(q, half, 1))
    for i in range(4):
        out[i : i + 1, :] = jnp.sum(acc[i], axis=0, keepdims=True)
    out[4:8, :] = jnp.zeros((4, width), F32)


def coefficient_kernel(m_ref, out_ref, gram_ref):
    width = m_ref.shape[1]
    half = width // 2
    count = STEPS + 1

    def row(j, i):
        return m_ref[8 * j + i : 8 * j + i + 1, :]

    def moment(n):
        j = (n + 1) // 2
        return row(j, 0 if n % 2 else 1)

    def cross(n):
        j = (n + 1) // 2
        return row(j, 2 if n % 2 else 3)

    size = gram_ref.shape[1]
    gram_ref[...] = jnp.zeros(gram_ref.shape, F32)
    for a in range(count):
        for b in range(count):
            gram_ref[a, b : b + 1, :] = moment(a + b)
            if b < STEPS:
                gram_ref[a, count + b : count + b + 1, :] = cross(a + b)
            if a < STEPS:
                gram_ref[count + a, b : b + 1, :] = cross(a + b)
            if a < STEPS and b < STEPS:
                gram_ref[count + a, count + b : count + b + 1, :] = pltpu.roll(moment(a + b), half, 1)
    ids = lax.broadcasted_iota(jnp.int32, (size, width), 0)
    active = (ids < STEPS) | ((ids > STEPS) & (ids < 2 * STEPS))

    def change(v):
        v = jnp.where(active, v, F32(0.0))
        return F32(CENTER) * v + F32(HALF) * pltpu.roll(v, 1, 0)

    def times(v):
        out = None
        for a in range(2 * STEPS + 1):
            t = gram_ref[a] * v[a : a + 1, :]
            out = t if out is None else out + t
        return out

    def dot(u, v):
        return jnp.sum(u * v, axis=0, keepdims=True)

    x = jnp.zeros((size, width), F32)
    r = jnp.where(ids == STEPS + 1, F32(1.0), F32(0.0))
    d = jnp.where(ids == 0, F32(1.0), F32(0.0))
    current = dot(r, times(r))
    for _ in range(STEPS):
        moved = change(d)
        alpha = current / dot(d, times(moved))
        x = x + alpha * d
        r = r - alpha * moved
        following = dot(r, times(r))
        d = r + (following / current) * d
        current = following
    low = lax.broadcasted_iota(jnp.int32, (8, width), 1) < half
    sub = lax.broadcasted_iota(jnp.int32, (8, width), 0)
    for q, v in enumerate((x, r, d)):
        lows = v[:8]
        lows = jnp.where(sub < count, lows, F32(0.0))
        highs = pltpu.roll(v, size - count, 0)[:8]
        highs = jnp.where(sub < STEPS, pltpu.roll(highs, half, 1), F32(0.0))
        out_ref[8 * q : 8 * q + 8, :] = jnp.where(low, lows, highs)


def combine_kernel(*refs):
    basis, (w_ref, mine_ref, send_ref) = refs[:-3], refs[-3:]
    blocks, rows, width = basis[0].shape
    half = width // 2
    nb = blocks // 2
    for b in range(blocks):
        vs = [s[b] for s in basis]
        for q in range(3):
            out = None
            for j, v in enumerate(vs):
                t = v * w_ref[8 * q + j : 8 * q + j + 1, :]
                out = t if out is None else out + t
            out = out + pltpu.roll(out, half, 1)
            if b < nb:
                mine_ref[q * nb + b] = out
            else:
                send_ref[q * nb + b - nb] = out


def shards(devices, start_point, residual, direction, send_list, block_cols, block_vals):
    nb, slots, rows, _ = block_vals.shape
    cap = send_list.shape[2]
    width = direction.shape[1]
    half = width // 2
    ghosts = nb + cap
    sds = jax.ShapeDtypeStruct
    vec = lambda n: sds((n, rows, width), F32)
    core = (lax.axis_index("dom") % 2).astype(jnp.int32).reshape(1)
    swap = [(i, i ^ 1) for i in range(devices)]
    to_right = [(i, (i + 2) % devices) for i in range(devices)]
    to_left = [(i, (i - 2) % devices) for i in range(devices)]
    permute = lambda v, pairs: lax.ppermute(v, "dom", pairs)

    mine, send = call(
        pack_kernel,
        [sds(direction.shape, F32)] * 2,
        [SM, VM, VM],
        [VM, VM],
        bytes_=4 * direction.size * 4,
        flops=direction.size,
        name="pack",
    )(core, direction, residual)
    other = permute(send, swap)
    lists = jnp.stack([send_list[0], permute(send_list[0], swap)])
    own, right, left = call(
        first_kernel,
        [vec(2 * nb), vec(ghosts), vec(ghosts)],
        [SM, SM, VM, VM],
        [VM, VM, VM],
        bytes_=6 * direction.size * 4,
        flops=direction.size,
        name="first",
    )(core, lists, mine.reshape(nb, rows, width), other.reshape(nb, rows, width))
    fr, fl = permute(left, to_left), permute(right, to_right)
    vals_other = permute(block_vals, swap)
    cols = jnp.stack([block_cols, permute(block_cols, swap)])
    lists_right, lists_left = permute(lists, to_left), permute(lists, to_right)
    index = call(
        index_kernel,
        sds((2 * nb, slots), jnp.int32),
        [SM] * 5,
        SM,
        flops=1000,
        name="index",
    )(core, lists, lists_right, lists_left, cols)

    def split(vals):
        spec = pl.BlockSpec((1, rows, slots * rows), lambda i: (i, 0, 0))
        return call(
            matrix_kernel,
            [sds((nb, rows, slots * rows), BF16)] * 2,
            [pl.BlockSpec((1, slots, rows, rows), lambda i: (i, 0, 0, 0))],
            [spec, spec],
            grid=(nb,),
            flops=4 * vals.size,
            bytes_=8 * vals.size,
            name="matrix",
        )(vals)

    parts = split(block_vals) + split(vals_other)
    basis = [own]
    moments = []

    def moment(j):
        args = basis[j : j + 1] + basis[j - 1 : j] if j else basis[:1]
        moments.append(
            call(
                functools.partial(moment_kernel, j == 0),
                sds((8, width), F32),
                [VM] * len(args),
                VM,
                flops=8 * own.size,
                bytes_=8 * own.size,
                name="moment",
            )(*args)
        )

    for j in range(STEPS):
        last = j == STEPS - 1
        out = [vec(2 * nb)] + ([] if last else [vec(ghosts), vec(ghosts)])
        res = call(
            functools.partial(step_kernel, last),
            out,
            [SM] * 3 + [VM] * 7,
            [VM] * len(out),
            scratch=[pltpu.VMEM((2 * nb + 2 * ghosts, rows, 2 * width), BF16)],
            flops=2 * 4 * 2 * nb * slots * rows * rows * width,
            bytes_=8 * 2 * nb * slots * rows * rows,
            name="step",
        )(core, lists, index, basis[-1], fr, fl, *parts)
        moment(j)
        basis.append(res[0])
        if not last:
            fr, fl = permute(res[2], to_left), permute(res[1], to_right)
    moment(STEPS)
    total = reduce_moments(jnp.concatenate(moments, axis=0), devices)
    weights = call(
        coefficient_kernel,
        sds((24, width), F32),
        [VM],
        VM,
        scratch=[pltpu.VMEM((2 * STEPS + 1, 16, width), F32)],
        flops=100000,
        name="coefficients",
    )(total)
    mine, send = call(
        combine_kernel,
        [vec(3 * nb), vec(3 * nb)],
        [VM] * (STEPS + 2),
        [VM, VM],
        flops=6 * (STEPS + 1) * own.size,
        bytes_=(STEPS + 1 + 3) * own.size * 4,
        name="combine",
    )(*basis, weights)
    other = permute(send, swap)
    own_half = (lax.broadcasted_iota(jnp.int32, (1, width), 1) // half) == core[0]
    whole = jnp.where(own_half[None], mine, other).reshape(3, nb * rows, width)
    return start_point + whole[0], whole[1], whole[2]


def reduce_moments(local, devices):
    pairs = devices // 2
    if pairs & (pairs - 1):
        index = lax.axis_index("dom")
        slot = (lax.broadcasted_iota(jnp.int32, (2, 1, 1), 0) == index % 2).astype(F32)
        both = lax.psum(local[None] * slot, "dom")
        return jnp.where(index % 2 == 0, both[0], both[1])
    bit = 2
    while bit < devices:
        masks = [bit, 2 * bit, 3 * bit] if 2 * bit < devices else [bit]
        parts = [lax.ppermute(local, "dom", [(i, i ^ m) for i in range(devices)]) for m in masks]
        for part in parts:
            local = local + part
        bit *= 4
    return local


def solution(mesh):
    devices = mesh.shape["dom"]
    return jax.shard_map(
        functools.partial(shards, devices),
        mesh=mesh,
        in_specs=(
            P("dom", None),
            P("dom", None),
            P("dom", None),
            P("dom", None, None),
            P("dom", None),
            P("dom", None, None, None),
        ),
        out_specs=(P("dom", None), P("dom", None), P("dom", None)),
        check_vma=False,
    )
```

time: 523 us -> 217 us (0.41); the launches traced: 516 us -> 217 us
  matrix products: 117 us -> 0 us
  local copies, waits for them, and re-layouts: 95.6 us -> 13 us
  starting transfers between devices: 119 us -> 39.7 us
  Pallas kernels: 0 us -> 62.1 us
  waiting for transfers between devices: 151 us -> 97.2 us
  between operations: 16.7 us -> 0.75 us
  other arithmetic: 17 us -> 3.81 us
    psum x1 -> x0, waiting for transfers between devices: 135 us -> none  [shards(): gram_matrix = lax.psum(local_gram, 'dom')]
    dot_general x183 -> x0, matrix products: 117 us -> none  [the longest x44 44.7 us: apply_blocks(): outgoing = jnp.dot(chooser, flat_rows, precision=highest)]
    ppermute x44 -> x25, waiting for transfers between devices: 16 us -> 97.2 us  [the longest x19 90.3 us: shards(): permute = lambda v, pairs: lax.ppermute(v, 'dom', pairs)]
    ppermute x44 -> x25, starting transfers between devices: 118 us -> 39.7 us  [the longest x19 31 us: shards(): permute = lambda v, pairs: lax.ppermute(v, 'dom', pairs)]
    concatenate x11 -> x1, local copies, waits for them, and re-layouts: 63.5 us -> 0.69 us  [shards(): total = reduce_moments(jnp.concatenate(moments, axis=0), devices)]
    pallas_call x0 -> x20, Pallas kernels: none -> 62.1 us  [the longest x6 27.8 us: shards(): call(functools.partial(step_kernel, last), out, [SM] * 3 + [VM] * 7, [VM]...]
    another operation x25 -> x0, local copies, waits for them, and re-layouts: 20.7 us -> none  [the longest x14 18.5 us: shards(): basis_stack = jnp.stack(p_basis + r_basis)]
    unnamed x13 -> x0, other arithmetic: 10.1 us -> none
  transfers between devices with their start and end apart: 45 -> 25, of which waited for: 7 -> 17; matrix products, arithmetic and copies ran while one was open for 18% -> 2% of each run, Pallas kernels for 0% -> 12%
where the time goes in v1:
time: 217 us
  waiting for transfers between devices  97.2 us (45%)
  Pallas kernels  62.1 us (29%)
  starting transfers between devices  39.7 us (18%)
  local copies, waits for them, and re-layouts  13 us (6%)
  other arithmetic  3.81 us (2%)
    ppermute x19, waiting for transfers between devices, shards(): permute = lambda v, pairs: lax.ppermute(v, 'dom', pairs)  90.3 us
    ppermute x19, starting transfers between devices, shards(): permute = lambda v, pairs: lax.ppermute(v, 'dom', pairs)  31 us
    pallas_call x6, Pallas kernels, shards(): call(functools.partial(step_kernel, last), out, [SM] * 3 + [VM] * 7, [VM]...  27.8 us
    pallas_call x7, Pallas kernels, moment(): call(functools.partial(moment_kernel, j == 0), sds((8, width), F32), [VM]...  14.7 us
    unnamed x47, local copies, waits for them, and re-layouts  11.5 us
    ppermute x6, starting transfers between devices, reduce_moments(): lax.ppermute(local, 'dom', [(i, i ^ m) for i in range(devices)])  8.72 us
    pallas_call x2, Pallas kernels, split(): call(matrix_kernel, [sds((nb, rows, slots * rows), BF16)] * 2, [pl.BlockS...  7.38 us
    ppermute x6, waiting for transfers between devices, reduce_moments(): lax.ppermute(local, 'dom', [(i, i ^ m) for i in range(devices)])  6.91 us
  transfers between devices with their start and end apart: 25, of which 17 were waited for; matrix products, arithmetic and copies ran while one was open for 2% of the time, Pallas kernels for 12%

profile of v1, /device:TPU:0, one launch (start us, length us, event | category | flops | bytes accessed | tf_op | source)
XLA Modules:
  0.0 216.6 jit_solution(1251759268629476738)
XLA Ops:
  1.2 2.0 pack.1
  6.6 2.2 %first.1 = (f32[8,128,128]{2,1,0:T(8,128)}, f32[7,128,128]{2,1,0:T(8,128)}, f32[7,128,128]{2,1,0:T(8,128)}) custom-call(s32[1]{0:T(128)} %bitcast.core, s32[2,4,3]{2,1,0:T(4,128)} %pad_add_fusion.lists, f32[4,128,128]{2,1,0:T(8,128)} %bitcast.11, f32[4,128,128]{2,1,0:T(8,128)} %bitcast.12), custom_call_target="tpu_custom_call" | custom-call | flops 65536 | bytes 1572864 | tf_op jit(solution)/shard_map/first/pallas_call | solution.py:273
  8.8 6.8 %collective-permute-start.5 = (f32[7,128,128]{2,1,0:T(8,128)}, f32[7,128,128]{2,1,0:T(8,128)S(1)}, u32[]{:S(2)}, u32[]{:S(2)}) collective-permute-start(f32[7,128,128]{2,1,0:T(8,128)} %get-tuple-element.32), channel_id=1, source_target_pairs={{0,30},{1,31},{2,0},{3,1},{4,2},{5,3},{6,4},{7,5},{8,6},{9,7},{10,... | collective-permute-start | bytes 1376264 | tf_op jit(solution)/shard_map/ppermute | solution.py:260
  15.6 3.7 %matrix.2 = (bf16[4,128,768]{2,1,0:T(8,128)(2,1)}, bf16[4,128,768]{2,1,0:T(8,128)(2,1)}) custom-call(f32[4,6,128,128]{3,2,1,0:T(8,128)} %a_ref.1), custom_call_target="tpu_custom_call" | custom-call | flops 1572864 | bytes 3145728 | tf_op jit(solution)/shard_map/matrix/pallas_call | solution.py:297
  19.3 5.6 %collective-permute-start.2 = (s32[2,4,3]{2,1,0:T(4,128)S(1)}, s32[2,4,3]{2,1,0:T(4,128)S(1)}, u32[]{:S(2)}, u32[]{:S(2)}) collective-permute-start(s32[2,4,3]{2,1,0:T(4,128)S(1)} %copy-done.13), channel_id=1, source_target_pairs={{0,30},{1,31},{2,0},{3,1},{4,2},{5,3},{6,4},{7,5},{8,6},{9,7},{10,... | collective-permute-start | bytes 296 | tf_op jit(solution)/shard_map/ppermute | solution.py:260
  25.5 7.1 %collective-permute-done.2.from_right = s32[2,4,3]{2,1,0:T(4,128)S(1)} collective-permute-done((s32[2,4,3]{2,1,0:T(4,128)S(1)}, s32[2,4,3]{2,1,0:T(4,128)S(1)}, u32[]{:S(2)}, u32[]{:S(2)}) %collective-permute-start.2) | collective-permute-done | bytes 128 | tf_op jit(solution)/shard_map/ppermute | solution.py:260
  32.7 1.2 collective-permute-done.3.from_left
  34.5 2.4 %index.1 = s32[8,6]{1,0:T(8,128)} custom-call(s32[1]{0:T(128)} %bitcast.core, s32[2,4,3]{2,1,0:T(4,128)} %pad_add_fusion.lists, s32[2,4,3]{2,1,0:T(4,128)} %copy-done.17, s32[2,4,3]{2,1,0:T(4,128)} %copy-done.18, s32[2,4,6]{2,1,0:T(4,128)} %pad_add_fusion.1.cols), custom_call_target="tpu_custom_call" | custom-call | flops 1000 | tf_op jit(solution)/shard_map/index/pallas_call | solution.py:286
  36.9 1.2 copy-done
  38.1 3.7 %matrix.3 = (bf16[4,128,768]{2,1,0:T(8,128)(2,1)}, bf16[4,128,768]{2,1,0:T(8,128)(2,1)}) custom-call(f32[4,6,128,128]{3,2,1,0:T(8,128)} %copy-done), custom_call_target="tpu_custom_call" | custom-call | flops 1572864 | bytes 3145728 | tf_op jit(solution)/shard_map/matrix/pallas_call | solution.py:297
  42.7 4.6 %step.6 = (f32[8,128,128]{2,1,0:T(8,128)}, f32[7,128,128]{2,1,0:T(8,128)}, f32[7,128,128]{2,1,0:T(8,128)}) custom-call(s32[1]{0:T(128)} %bitcast.core, s32[2,4,3]{2,1,0:T(4,128)} %pad_add_fusion.lists, s32[8,6]{1,0:T(8,128)} %index.1, f32[8,128,128]{2,1,0:T(8,128)} %get-tuple-element.31.own_ref.refs_0_.refs_1_, f32[7,128,128]{2,1,0:T(8,128)} %copy-done.1, ...), custom_call_target="tpu_custom_call" | custom-call | flops 805306368 | bytes 6291456 | tf_op jit(solution)/shard_map/step/pallas_call | solution.py:329
  47.4 4.5 %collective-permute-start.8 = (f32[7,128,128]{2,1,0:T(8,128)}, f32[7,128,128]{2,1,0:T(8,128)S(1)}, u32[]{:S(2)}, u32[]{:S(2)}) collective-permute-start(f32[7,128,128]{2,1,0:T(8,128)} %get-tuple-element.39), channel_id=1, source_target_pairs={{0,30},{1,31},{2,0},{3,1},{4,2},{5,3},{6,4},{7,5},{8,6},{9,7},{10,... | collective-permute-start | bytes 1376264 | tf_op jit(solution)/shard_map/ppermute | solution.py:260
  51.9 9.6 %collective-permute-done.8.fr_ref = f32[7,128,128]{2,1,0:T(8,128)S(1)} collective-permute-done((f32[7,128,128]{2,1,0:T(8,128)}, f32[7,128,128]{2,1,0:T(8,128)S(1)}, u32[]{:S(2)}, u32[]{:S(2)}) %collective-permute-start.8) | collective-permute-done | bytes 458784 | tf_op jit(solution)/shard_map/ppermute | solution.py:260
  61.4 7.7 %collective-permute-done.9.fl_ref = f32[7,128,128]{2,1,0:T(8,128)S(1)} collective-permute-done((f32[7,128,128]{2,1,0:T(8,128)}, f32[7,128,128]{2,1,0:T(8,128)S(1)}, u32[]{:S(2)}, u32[]{:S(2)}) %collective-permute-start.9) | collective-permute-done | bytes 458784 | tf_op jit(solution)/shard_map/ppermute | solution.py:260
  69.9 4.6 %step.7 = (f32[8,128,128]{2,1,0:T(8,128)}, f32[7,128,128]{2,1,0:T(8,128)}, f32[7,128,128]{2,1,0:T(8,128)}) custom-call(s32[1]{0:T(128)} %bitcast.core, s32[2,4,3]{2,1,0:T(4,128)} %pad_add_fusion.lists, s32[8,6]{1,0:T(8,128)} %index.1, f32[8,128,128]{2,1,0:T(8,128)} %get-tuple-element.38.own_ref.refs_0_.refs_1_, f32[7,128,128]{2,1,0:T(8,128)} %copy-done.5, ...), custom_call_target="tpu_custom_call" | custom-call | flops 805306368 | bytes 6291456 | tf_op jit(solution)/shard_map/step/pallas_call | solution.py:329
  74.5 5.6 %collective-permute-start.10 = (f32[7,128,128]{2,1,0:T(8,128)}, f32[7,128,128]{2,1,0:T(8,128)S(1)}, u32[]{:S(2)}, u32[]{:S(2)}) collective-permute-start(f32[7,128,128]{2,1,0:T(8,128)} %get-tuple-element.42), channel_id=1, source_target_pairs={{0,30},{1,31},{2,0},{3,1},{4,2},{5,3},{6,4},{7,5},{8,6},{9,7},{10,... | collective-permute-start | bytes 1376264 | tf_op jit(solution)/shard_map/ppermute | solution.py:260
  80.2 8.4 %collective-permute-done.10.fr_ref = f32[7,128,128]{2,1,0:T(8,128)S(1)} collective-permute-done((f32[7,128,128]{2,1,0:T(8,128)}, f32[7,128,128]{2,1,0:T(8,128)S(1)}, u32[]{:S(2)}, u32[]{:S(2)}) %collective-permute-start.10) | collective-permute-done | bytes 458784 | tf_op jit(solution)/shard_map/ppermute | solution.py:260
  88.5 9.8 %collective-permute-done.11.fl_ref = f32[7,128,128]{2,1,0:T(8,128)S(1)} collective-permute-done((f32[7,128,128]{2,1,0:T(8,128)}, f32[7,128,128]{2,1,0:T(8,128)S(1)}, u32[]{:S(2)}, u32[]{:S(2)}) %collective-permute-start.11) | collective-permute-done | bytes 458784 | tf_op jit(solution)/shard_map/ppermute | solution.py:260
  99.2 4.7 %step.8 = (f32[8,128,128]{2,1,0:T(8,128)}, f32[7,128,128]{2,1,0:T(8,128)}, f32[7,128,128]{2,1,0:T(8,128)}) custom-call(s32[1]{0:T(128)} %bitcast.core, s32[2,4,3]{2,1,0:T(4,128)} %pad_add_fusion.lists, s32[8,6]{1,0:T(8,128)} %index.1, f32[8,128,128]{2,1,0:T(8,128)} %get-tuple-element.41.own_ref.refs_0_.refs_1_.refs_2_, f32[7,128,128]{2,1,0:T(8,128)} %copy-done.6, ...), custom_call_target="tpu_custom_call" | custom-call | flops 805306368 | bytes 6291456 | tf_op jit(solution)/shard_map/step/pallas_call | solution.py:329
  103.8 2.4 %collective-permute-start.12 = (f32[7,128,128]{2,1,0:T(8,128)}, f32[7,128,128]{2,1,0:T(8,128)S(1)}, u32[]{:S(2)}, u32[]{:S(2)}) collective-permute-start(f32[7,128,128]{2,1,0:T(8,128)} %get-tuple-element.45), channel_id=1, source_target_pairs={{0,30},{1,31},{2,0},{3,1},{4,2},{5,3},{6,4},{7,5},{8,6},{9,7},{10,... | collective-permute-start | bytes 1376264 | tf_op jit(solution)/shard_map/ppermute | solution.py:260
  106.2 11.6 %collective-permute-done.12.fr_ref = f32[7,128,128]{2,1,0:T(8,128)S(1)} collective-permute-done((f32[7,128,128]{2,1,0:T(8,128)}, f32[7,128,128]{2,1,0:T(8,128)S(1)}, u32[]{:S(2)}, u32[]{:S(2)}) %collective-permute-start.12) | collective-permute-done | bytes 458784 | tf_op jit(solution)/shard_map/ppermute | solution.py:260
  117.8 8.1 %collective-permute-done.13.fl_ref = f32[7,128,128]{2,1,0:T(8,128)S(1)} collective-permute-done((f32[7,128,128]{2,1,0:T(8,128)}, f32[7,128,128]{2,1,0:T(8,128)S(1)}, u32[]{:S(2)}, u32[]{:S(2)}) %collective-permute-start.13) | collective-permute-done | bytes 458784 | tf_op jit(solution)/shard_map/ppermute | solution.py:260
  126.7 4.7 %step.9 = (f32[8,128,128]{2,1,0:T(8,128)}, f32[7,128,128]{2,1,0:T(8,128)}, f32[7,128,128]{2,1,0:T(8,128)}) custom-call(s32[1]{0:T(128)} %bitcast.core, s32[2,4,3]{2,1,0:T(4,128)} %pad_add_fusion.lists, s32[8,6]{1,0:T(8,128)} %index.1, f32[8,128,128]{2,1,0:T(8,128)} %get-tuple-element.44.own_ref.refs_0_.refs_1_.refs_3_, f32[7,128,128]{2,1,0:T(8,128)} %copy-done.7, ...), custom_call_target="tpu_custom_call" | custom-call | flops 805306368 | bytes 6291456 | tf_op jit(solution)/shard_map/step/pallas_call | solution.py:329
  132.2 1.5 collective-permute-start.15
  133.8 1.8 moment.7
  136.3 2.1 moment.8
  138.5 6.9 %collective-permute-done.14.fr_ref = f32[7,128,128]{2,1,0:T(8,128)S(1)} collective-permute-done((f32[7,128,128]{2,1,0:T(8,128)}, f32[7,128,128]{2,1,0:T(8,128)S(1)}, u32[]{:S(2)}, u32[]{:S(2)}) %collective-permute-start.14) | collective-permute-done | bytes 458784 | tf_op jit(solution)/shard_map/ppermute | solution.py:260
  145.4 8.5 %collective-permute-done.15.fl_ref = f32[7,128,128]{2,1,0:T(8,128)S(1)} collective-permute-done((f32[7,128,128]{2,1,0:T(8,128)}, f32[7,128,128]{2,1,0:T(8,128)S(1)}, u32[]{:S(2)}, u32[]{:S(2)}) %collective-permute-start.15) | collective-permute-done | bytes 458784 | tf_op jit(solution)/shard_map/ppermute | solution.py:260
  154.7 4.7 %step.10 = (f32[8,128,128]{2,1,0:T(8,128)}, f32[7,128,128]{2,1,0:T(8,128)}, f32[7,128,128]{2,1,0:T(8,128)}) custom-call(s32[1]{0:T(128)} %bitcast.core, s32[2,4,3]{2,1,0:T(4,128)} %pad_add_fusion.lists, s32[8,6]{1,0:T(8,128)} %index.1, f32[8,128,128]{2,1,0:T(8,128)} %get-tuple-element.47.own_ref.refs_0_.refs_1_.refs_4_, f32[7,128,128]{2,1,0:T(8,128)} %copy-done.3, ...), custom_call_target="tpu_custom_call" | custom-call | flops 805306368 | bytes 6291456 | tf_op jit(solution)/shard_map/step/pallas_call | solution.py:329
  159.4 2.6 %collective-permute-start.16 = (f32[7,128,128]{2,1,0:T(8,128)}, f32[7,128,128]{2,1,0:T(8,128)S(1)}, u32[]{:S(2)}, u32[]{:S(2)}) collective-permute-start(f32[7,128,128]{2,1,0:T(8,128)} %get-tuple-element.51), channel_id=1, source_target_pairs={{0,30},{1,31},{2,0},{3,1},{4,2},{5,3},{6,4},{7,5},{8,6},{9,7},{10,... | collective-permute-start | bytes 1376264 | tf_op jit(solution)/shard_map/ppermute | solution.py:260
  162.0 2.1 moment.9
  164.8 2.1 moment.10
  167.7 2.1 moment.11
  170.5 2.1 moment.12
  173.3 8.0 %collective-permute-done.17.fl_ref = f32[7,128,128]{2,1,0:T(8,128)S(1)} collective-permute-done((f32[7,128,128]{2,1,0:T(8,128)}, f32[7,128,128]{2,1,0:T(8,128)S(1)}, u32[]{:S(2)}, u32[]{:S(2)}) %collective-permute-start.17) | collective-permute-done | bytes 458784 | tf_op jit(solution)/shard_map/ppermute | solution.py:260
  182.2 4.4 %step.11.refs_0_.refs_6_ = f32[8,128,128]{2,1,0:T(8,128)} custom-call(s32[1]{0:T(128)} %bitcast.core, s32[2,4,3]{2,1,0:T(4,128)} %pad_add_fusion.lists, s32[8,6]{1,0:T(8,128)} %index.1, f32[8,128,128]{2,1,0:T(8,128)} %get-tuple-element.50.own_ref.refs_0_.refs_1_.refs_5_, f32[7,128,128]{2,1,0:T(8,128)} %copy-done.11, f32[7,128,128]{2,1,0:T(8,128)} %copy-done.12, ...), custom_call_target="tpu_custom_call" | custom-call | flops 805306368 | bytes 6291456 | tf_op jit(solution)/shard_map/step/pallas_call | solution.py:329
  186.5 2.1 moment.13
  189.4 2.4 %collective-permute-start.18 = (f32[56,128]{1,0:T(8,128)S(1)}, f32[56,128]{1,0:T(8,128)S(1)}, u32[]{:S(2)}, u32[]{:S(2)}) collective-permute-start(f32[56,128]{1,0:T(8,128)S(1)} %constant_dynamic-update-slice_fusion), channel_id=1, source_target_pairs={{0,2},{1,3},{2,0},{3,1},{4,6},{5,7},{6,4},{7,5},{8,10},{9,11},{10,... | collective-permute-start | bytes 86024 | tf_op jit(solution)/shard_map/ppermute | solution.py:379
  191.7 1.4 collective-permute-start.19
  193.6 2.0 collective-permute-done.19
  195.6 2.3 %collective-permute-done.20 = f32[56,128]{1,0:T(8,128)S(1)} collective-permute-done((f32[56,128]{1,0:T(8,128)S(1)}, f32[56,128]{1,0:T(8,128)S(1)}, u32[]{:S(2)}, u32[]{:S(2)}) %collective-permute-start.20) | collective-permute-done | bytes 28704 | tf_op jit(solution)/shard_map/ppermute | solution.py:379
  198.0 1.4 collective-permute-start.21
  199.3 3.1 %collective-permute-start.23 = (f32[56,128]{1,0:T(8,128)S(1)}, f32[56,128]{1,0:T(8,128)S(1)}, u32[]{:S(2)}, u32[]{:S(2)}) collective-permute-start(f32[56,128]{1,0:T(8,128)S(1)} %add_add_fusion.1), channel_id=1, source_target_pairs={{0,24},{1,25},{2,26},{3,27},{4,28},{5,29},{6,30},{7,31},{8,16},{9,... | collective-permute-start | bytes 86024 | tf_op jit(solution)/shard_map/ppermute | solution.py:379
  202.4 2.0 collective-permute-done.22
  205.6 1.9 coefficients.1.refs_7_
  207.5 3.7 %combine.1 = (f32[12,128,128]{2,1,0:T(8,128)}, f32[12,128,128]{2,1,0:T(8,128)}) custom-call(f32[8,128,128]{2,1,0:T(8,128)} %get-tuple-element.31.own_ref.refs_0_.refs_1_, f32[8,128,128]{2,1,0:T(8,128)} %get-tuple-element.38.own_ref.refs_0_.refs_1_, f32[8,128,128]{2,1,0:T(8,128)} %get-tuple-element.41.own_ref.refs_0_.refs_1_.refs_2_, ...), custom_call_target="tpu_custom_call" | custom-call | flops 5505024 | bytes 5242880 | tf_op jit(solution)/shard_map/combine/pallas_call | solution.py:354
  211.3 2.5 %collective-permute-done.24 = f32[12,128,128]{2,1,0:T(8,128)S(1)} collective-permute-done((f32[12,128,128]{2,1,0:T(8,128)}, f32[12,128,128]{2,1,0:T(8,128)S(1)}, u32[]{:S(2)}, u32[]{:S(2)}) %collective-permute-start.24) | collective-permute-done | bytes 786464 | tf_op jit(solution)/shard_map/ppermute | solution.py:260
  213.8 1.3 broadcast_select_fusion
  (78 shorter events, 18.3 us)
Async XLA Ops:
  0.6 24.3 %copy-start.19 = (s32[4,6]{1,0:T(4,128)S(1)}, s32[4,6]{1,0:T(4,128)}, u32[]{:S(2)}) copy-start(s32[4,6]{1,0:T(4,128)} %param.10) | copy-start | bytes 292
  0.6 36.3 %collective-permute-start.7 = (f32[4,6,128,128]{3,2,1,0:T(8,128)}, f32[4,6,128,128]{3,2,1,0:T(8,128)S(1)}, u32[]{:S(2)}, u32[]{:S(2)}) collective-permute-start(f32[4,6,128,128]{3,2,1,0:T(8,128)} %a_ref.1), channel_id=1, source_target_pairs={{0,1},{1,0},{2,3},{3,2},{4,5},{5,4},{6,7},{7,6},{8,9},{9,8},{10,11... | collective-permute-start | bytes 4718600 | tf_op jit(solution)/shard_map/ppermute | solution.py:260
  3.2 2.7 %collective-permute-start.1 = (f32[512,128]{1,0:T(8,128)}, f32[512,128]{1,0:T(8,128)S(1)}, u32[]{:S(2)}, u32[]{:S(2)}) collective-permute-start(f32[512,128]{1,0:T(8,128)} %get-tuple-element.30), channel_id=1, source_target_pairs={{0,1},{1,0},{2,3},{3,2},{4,5},{5,4},{6,7},{7,6},{8,9},{9,8},{10,11... | collective-permute-start | bytes 786440 | tf_op jit(solution)/shard_map/ppermute | solution.py:260
  4.0 1.3 collective-permute-start
  5.9 13.4 %copy-start.13 = (s32[2,4,3]{2,1,0:T(4,128)S(1)}, s32[2,4,3]{2,1,0:T(4,128)}, u32[]{:S(2)}) copy-start(s32[2,4,3]{2,1,0:T(4,128)} %pad_add_fusion.lists) | copy-start | bytes 292
  5.9 0.7 copy-start.15
  8.8 33.0 %collective-permute-start.5 = (f32[7,128,128]{2,1,0:T(8,128)}, f32[7,128,128]{2,1,0:T(8,128)S(1)}, u32[]{:S(2)}, u32[]{:S(2)}) collective-permute-start(f32[7,128,128]{2,1,0:T(8,128)} %get-tuple-element.32), channel_id=1, source_target_pairs={{0,30},{1,31},{2,0},{3,1},{4,2},{5,3},{6,4},{7,5},{8,6},{9,7},{10,... | collective-permute-start | bytes 1376264 | tf_op jit(solution)/shard_map/ppermute | solution.py:260
  15.6 26.2 %collective-permute-start.6 = (f32[7,128,128]{2,1,0:T(8,128)}, f32[7,128,128]{2,1,0:T(8,128)S(1)}, u32[]{:S(2)}, u32[]{:S(2)}) collective-permute-start(f32[7,128,128]{2,1,0:T(8,128)} %get-tuple-element.33), channel_id=1, source_target_pairs={{0,2},{1,3},{2,4},{3,5},{4,6},{5,7},{6,8},{7,9},{8,10},{9,11},{10,... | collective-permute-start | bytes 1376264 | tf_op jit(solution)/shard_map/ppermute | solution.py:260
  15.6 9.3 %collective-permute-start.4 = (s32[4,6]{1,0:T(4,128)}, s32[4,6]{1,0:T(4,128)S(1)}, u32[]{:S(2)}, u32[]{:S(2)}) collective-permute-start(s32[4,6]{1,0:T(4,128)} %param.10), channel_id=1, source_target_pairs={{0,1},{1,0},{2,3},{3,2},{4,5},{5,4},{6,7},{7,6},{8,9},{9,8},{10,11... | collective-permute-start | bytes 296 | tf_op jit(solution)/shard_map/ppermute | solution.py:260
  19.3 13.3 %collective-permute-start.2 = (s32[2,4,3]{2,1,0:T(4,128)S(1)}, s32[2,4,3]{2,1,0:T(4,128)S(1)}, u32[]{:S(2)}, u32[]{:S(2)}) collective-permute-start(s32[2,4,3]{2,1,0:T(4,128)S(1)} %copy-done.13), channel_id=1, source_target_pairs={{0,30},{1,31},{2,0},{3,1},{4,2},{5,3},{6,4},{7,5},{8,6},{9,7},{10,... | collective-permute-start | bytes 296 | tf_op jit(solution)/shard_map/ppermute | solution.py:260
  24.9 8.9 %collective-permute-start.3 = (s32[2,4,3]{2,1,0:T(4,128)S(1)}, s32[2,4,3]{2,1,0:T(4,128)S(1)}, u32[]{:S(2)}, u32[]{:S(2)}) collective-permute-start(s32[2,4,3]{2,1,0:T(4,128)S(1)} %copy-done.13), channel_id=1, source_target_pairs={{0,2},{1,3},{2,4},{3,5},{4,6},{5,7},{6,8},{7,9},{8,10},{9,11},{10,... | collective-permute-start | bytes 296 | tf_op jit(solution)/shard_map/ppermute | solution.py:260
  32.7 1.2 copy-start.17
  33.9 0.6 copy-start.18
  36.9 1.2 copy-start
  41.8 0.8 copy-start.1
  41.8 0.9 copy-start.2
  47.4 14.1 %collective-permute-start.8 = (f32[7,128,128]{2,1,0:T(8,128)}, f32[7,128,128]{2,1,0:T(8,128)S(1)}, u32[]{:S(2)}, u32[]{:S(2)}) collective-permute-start(f32[7,128,128]{2,1,0:T(8,128)} %get-tuple-element.39), channel_id=1, source_target_pairs={{0,30},{1,31},{2,0},{3,1},{4,2},{5,3},{6,4},{7,5},{8,6},{9,7},{10,... | collective-permute-start | bytes 1376264 | tf_op jit(solution)/shard_map/ppermute | solution.py:260
  51.9 17.3 %collective-permute-start.9 = (f32[7,128,128]{2,1,0:T(8,128)}, f32[7,128,128]{2,1,0:T(8,128)S(1)}, u32[]{:S(2)}, u32[]{:S(2)}) collective-permute-start(f32[7,128,128]{2,1,0:T(8,128)} %get-tuple-element.40), channel_id=1, source_target_pairs={{0,2},{1,3},{2,4},{3,5},{4,6},{5,7},{6,8},{7,9},{8,10},{9,11},{10,... | collective-permute-start | bytes 1376264 | tf_op jit(solution)/shard_map/ppermute | solution.py:260
  61.4 7.7 %copy-start.5 = (f32[7,128,128]{2,1,0:T(8,128)}, f32[7,128,128]{2,1,0:T(8,128)S(1)}, u32[]{:S(2)}) copy-start(f32[7,128,128]{2,1,0:T(8,128)S(1)} %collective-permute-done.8.fr_ref) | copy-start | bytes 1376260
  69.1 0.8 copy-start.8
  74.5 14.0 %collective-permute-start.10 = (f32[7,128,128]{2,1,0:T(8,128)}, f32[7,128,128]{2,1,0:T(8,128)S(1)}, u32[]{:S(2)}, u32[]{:S(2)}) collective-permute-start(f32[7,128,128]{2,1,0:T(8,128)} %get-tuple-element.42), channel_id=1, source_target_pairs={{0,30},{1,31},{2,0},{3,1},{4,2},{5,3},{6,4},{7,5},{8,6},{9,7},{10,... | collective-permute-start | bytes 1376264 | tf_op jit(solution)/shard_map/ppermute | solution.py:260
  80.2 18.2 %collective-permute-start.11 = (f32[7,128,128]{2,1,0:T(8,128)}, f32[7,128,128]{2,1,0:T(8,128)S(1)}, u32[]{:S(2)}, u32[]{:S(2)}) collective-permute-start(f32[7,128,128]{2,1,0:T(8,128)} %get-tuple-element.43), channel_id=1, source_target_pairs={{0,2},{1,3},{2,4},{3,5},{4,6},{5,7},{6,8},{7,9},{8,10},{9,11},{10,... | collective-permute-start | bytes 1376264 | tf_op jit(solution)/shard_map/ppermute | solution.py:260
  88.5 9.8 %copy-start.6 = (f32[7,128,128]{2,1,0:T(8,128)}, f32[7,128,128]{2,1,0:T(8,128)S(1)}, u32[]{:S(2)}) copy-start(f32[7,128,128]{2,1,0:T(8,128)S(1)} %collective-permute-done.10.fr_ref) | copy-start | bytes 1376260
  98.4 0.8 copy-start.9
  103.8 14.0 %collective-permute-start.12 = (f32[7,128,128]{2,1,0:T(8,128)}, f32[7,128,128]{2,1,0:T(8,128)S(1)}, u32[]{:S(2)}, u32[]{:S(2)}) collective-permute-start(f32[7,128,128]{2,1,0:T(8,128)} %get-tuple-element.45), channel_id=1, source_target_pairs={{0,30},{1,31},{2,0},{3,1},{4,2},{5,3},{6,4},{7,5},{8,6},{9,7},{10,... | collective-permute-start | bytes 1376264 | tf_op jit(solution)/shard_map/ppermute | solution.py:260
  106.2 19.7 %collective-permute-start.13 = (f32[7,128,128]{2,1,0:T(8,128)}, f32[7,128,128]{2,1,0:T(8,128)S(1)}, u32[]{:S(2)}, u32[]{:S(2)}) collective-permute-start(f32[7,128,128]{2,1,0:T(8,128)} %get-tuple-element.46), channel_id=1, source_target_pairs={{0,2},{1,3},{2,4},{3,5},{4,6},{5,7},{6,8},{7,9},{8,10},{9,11},{10,... | collective-permute-start | bytes 1376264 | tf_op jit(solution)/shard_map/ppermute | solution.py:260
  117.8 8.1 %copy-start.7 = (f32[7,128,128]{2,1,0:T(8,128)}, f32[7,128,128]{2,1,0:T(8,128)S(1)}, u32[]{:S(2)}) copy-start(f32[7,128,128]{2,1,0:T(8,128)S(1)} %collective-permute-done.12.fr_ref) | copy-start | bytes 1376260
  125.9 0.8 copy-start.10
  131.4 14.0 %collective-permute-start.14 = (f32[7,128,128]{2,1,0:T(8,128)}, f32[7,128,128]{2,1,0:T(8,128)S(1)}, u32[]{:S(2)}, u32[]{:S(2)}) collective-permute-start(f32[7,128,128]{2,1,0:T(8,128)} %get-tuple-element.48), channel_id=1, source_target_pairs={{0,30},{1,31},{2,0},{3,1},{4,2},{5,3},{6,4},{7,5},{8,6},{9,7},{10,... | collective-permute-start | bytes 1376264 | tf_op jit(solution)/shard_map/ppermute | solution.py:260
  132.2 21.7 %collective-permute-start.15 = (f32[7,128,128]{2,1,0:T(8,128)}, f32[7,128,128]{2,1,0:T(8,128)S(1)}, u32[]{:S(2)}, u32[]{:S(2)}) collective-permute-start(f32[7,128,128]{2,1,0:T(8,128)} %get-tuple-element.49), channel_id=1, source_target_pairs={{0,2},{1,3},{2,4},{3,5},{4,6},{5,7},{6,8},{7,9},{8,10},{9,11},{10,... | collective-permute-start | bytes 1376264 | tf_op jit(solution)/shard_map/ppermute | solution.py:260
  145.4 8.5 %copy-start.3 = (f32[7,128,128]{2,1,0:T(8,128)}, f32[7,128,128]{2,1,0:T(8,128)S(1)}, u32[]{:S(2)}) copy-start(f32[7,128,128]{2,1,0:T(8,128)S(1)} %collective-permute-done.14.fr_ref) | copy-start | bytes 1376260
  153.9 0.8 copy-start.4
  154.7 7.3 %copy-start.16 = (f32[8,128]{1,0:T(8,128)S(1)}, f32[8,128]{1,0:T(8,128)}, u32[]{:S(2)}) copy-start(f32[8,128]{1,0:T(8,128)} %moment.8) | copy-start | bytes 12292
  159.4 14.0 %collective-permute-start.16 = (f32[7,128,128]{2,1,0:T(8,128)}, f32[7,128,128]{2,1,0:T(8,128)S(1)}, u32[]{:S(2)}, u32[]{:S(2)}) collective-permute-start(f32[7,128,128]{2,1,0:T(8,128)} %get-tuple-element.51), channel_id=1, source_target_pairs={{0,30},{1,31},{2,0},{3,1},{4,2},{5,3},{6,4},{7,5},{8,6},{9,7},{10,... | collective-permute-start | bytes 1376264 | tf_op jit(solution)/shard_map/ppermute | solution.py:260
  162.0 19.4 %collective-permute-start.17 = (f32[7,128,128]{2,1,0:T(8,128)}, f32[7,128,128]{2,1,0:T(8,128)S(1)}, u32[]{:S(2)}, u32[]{:S(2)}) collective-permute-start(f32[7,128,128]{2,1,0:T(8,128)} %get-tuple-element.52), channel_id=1, source_target_pairs={{0,2},{1,3},{2,4},{3,5},{4,6},{5,7},{6,8},{7,9},{8,10},{9,11},{10,... | collective-permute-start | bytes 1376264 | tf_op jit(solution)/shard_map/ppermute | solution.py:260
  173.3 8.0 %copy-start.11 = (f32[7,128,128]{2,1,0:T(8,128)}, f32[7,128,128]{2,1,0:T(8,128)S(1)}, u32[]{:S(2)}) copy-start(f32[7,128,128]{2,1,0:T(8,128)S(1)} %collective-permute-done.16.fr_ref) | copy-start | bytes 1376260
  181.4 0.8 copy-start.12
  189.4 4.3 %collective-permute-start.18 = (f32[56,128]{1,0:T(8,128)S(1)}, f32[56,128]{1,0:T(8,128)S(1)}, u32[]{:S(2)}, u32[]{:S(2)}) collective-permute-start(f32[56,128]{1,0:T(8,128)S(1)} %constant_dynamic-update-slice_fusion), channel_id=1, source_target_pairs={{0,2},{1,3},{2,0},{3,1},{4,6},{5,7},{6,4},{7,5},{8,10},{9,11},{10,... | collective-permute-start | bytes 86024 | tf_op jit(solution)/shard_map/ppermute | solution.py:379
  191.7 3.9 %collective-permute-start.19 = (f32[56,128]{1,0:T(8,128)S(1)}, f32[56,128]{1,0:T(8,128)S(1)}, u32[]{:S(2)}, u32[]{:S(2)}) collective-permute-start(f32[56,128]{1,0:T(8,128)S(1)} %constant_dynamic-update-slice_fusion), channel_id=1, source_target_pairs={{0,4},{1,5},{2,6},{3,7},{4,0},{5,1},{6,2},{7,3},{8,12},{9,13},{10,... | collective-permute-start | bytes 86024 | tf_op jit(solution)/shard_map/ppermute | solution.py:379
  193.2 4.8 %collective-permute-start.20 = (f32[56,128]{1,0:T(8,128)S(1)}, f32[56,128]{1,0:T(8,128)S(1)}, u32[]{:S(2)}, u32[]{:S(2)}) collective-permute-start(f32[56,128]{1,0:T(8,128)S(1)} %constant_dynamic-update-slice_fusion), channel_id=1, source_target_pairs={{0,6},{1,7},{2,4},{3,5},{4,2},{5,3},{6,0},{7,1},{8,14},{9,15},{10,... | collective-permute-start | bytes 86024 | tf_op jit(solution)/shard_map/ppermute | solution.py:379
  198.0 4.5 %collective-permute-start.21 = (f32[56,128]{1,0:T(8,128)S(1)}, f32[56,128]{1,0:T(8,128)S(1)}, u32[]{:S(2)}, u32[]{:S(2)}) collective-permute-start(f32[56,128]{1,0:T(8,128)S(1)} %add_add_fusion.1), channel_id=1, source_target_pairs={{0,8},{1,9},{2,10},{3,11},{4,12},{5,13},{6,14},{7,15},{8,0},{9,1},... | collective-permute-start | bytes 86024 | tf_op jit(solution)/shard_map/ppermute | solution.py:379
  199.3 5.1 %collective-permute-start.22 = (f32[56,128]{1,0:T(8,128)S(1)}, f32[56,128]{1,0:T(8,128)S(1)}, u32[]{:S(2)}, u32[]{:S(2)}) collective-permute-start(f32[56,128]{1,0:T(8,128)S(1)} %add_add_fusion.1), channel_id=1, source_target_pairs={{0,16},{1,17},{2,18},{3,19},{4,20},{5,21},{6,22},{7,23},{8,24},{9,... | collective-permute-start | bytes 86024 | tf_op jit(solution)/shard_map/ppermute | solution.py:379
  199.3 5.7 %collective-permute-start.23 = (f32[56,128]{1,0:T(8,128)S(1)}, f32[56,128]{1,0:T(8,128)S(1)}, u32[]{:S(2)}, u32[]{:S(2)}) collective-permute-start(f32[56,128]{1,0:T(8,128)S(1)} %add_add_fusion.1), channel_id=1, source_target_pairs={{0,24},{1,25},{2,26},{3,27},{4,28},{5,29},{6,30},{7,31},{8,16},{9,... | collective-permute-start | bytes 86024 | tf_op jit(solution)/shard_map/ppermute | solution.py:379
  211.3 2.5 %collective-permute-start.24 = (f32[12,128,128]{2,1,0:T(8,128)}, f32[12,128,128]{2,1,0:T(8,128)S(1)}, u32[]{:S(2)}, u32[]{:S(2)}) collective-permute-start(f32[12,128,128]{2,1,0:T(8,128)} %get-tuple-element.54), channel_id=1, source_target_pairs={{0,1},{1,0},{2,3},{3,2},{4,5},{5,4},{6,7},{7,6},{8,9},{9,8},{10,11... | collective-permute-start | bytes 2359304 | tf_op jit(solution)/shard_map/ppermute | solution.py:260
  213.8 2.1 copy-start.14

commit v2 on v1

--- a/solution.py
+++ b/solution.py
@@ -25,6 +25,7 @@
         scratch_shapes=list(scratch),
         cost_estimate=pl.CostEstimate(flops=flops, bytes_accessed=bytes_, transcendentals=0),
         name=name,
+        compiler_params=pltpu.CompilerParams(vmem_limit_bytes=12 * 2**20),
         **extra,
     )
 

time: 217 us -> 179 us (0.82)
  Pallas kernels: 62.1 us -> 19.5 us
  waiting for transfers between devices: 97.2 us -> 112 us
  local copies, waits for them, and re-layouts: 13 us -> 4.96 us
  other arithmetic: 3.81 us -> 0.85 us
    pallas_call x6, Pallas kernels: 27.8 us -> 11.6 us  [shards(): call(functools.partial(step_kernel, last), out, [SM] * 3 + [VM] * 7, [VM]...]
    ppermute x19, waiting for transfers between devices: 90.3 us -> 105 us  [shards(): permute = lambda v, pairs: lax.ppermute(v, 'dom', pairs)]
    pallas_call x7, Pallas kernels: 14.7 us -> 2.37 us  [moment(): call(functools.partial(moment_kernel, j == 0), sds((8, width), F32), [VM]...]
    unnamed x47 -> x17, local copies, waits for them, and re-layouts: 11.5 us -> 4.12 us
    pallas_call x2, Pallas kernels: 7.38 us -> 0.76 us  [split(): call(matrix_kernel, [sds((nb, rows, slots * rows), BF16)] * 2, [pl.BlockS...]
    pallas_call x1, Pallas kernels: 3.74 us -> 0.94 us  [shards(): call(combine_kernel, [vec(3 * nb), vec(3 * nb)], [VM] * (STEPS + 2), [VM,...]
  transfers between devices with their start and end apart: 25 -> 25, of which waited for: 17 -> 19; matrix products, arithmetic and copies ran while one was open for 2% -> 0% of each run, Pallas kernels for 12% -> 3%
where the time goes in v2:
time: 179 us
  waiting for transfers between devices  112 us (63%)
  starting transfers between devices  40.4 us (23%)
  Pallas kernels  19.5 us (11%)
  local copies, waits for them, and re-layouts  4.96 us (3%)
    ppermute x19, waiting for transfers between devices, shards(): permute = lambda v, pairs: lax.ppermute(v, 'dom', pairs)  105 us
    ppermute x19, starting transfers between devices, shards(): permute = lambda v, pairs: lax.ppermute(v, 'dom', pairs)  31.8 us
    pallas_call x6, Pallas kernels, shards(): call(functools.partial(step_kernel, last), out, [SM] * 3 + [VM] * 7, [VM]...  11.6 us
    ppermute x6, starting transfers between devices, reduce_moments(): lax.ppermute(local, 'dom', [(i, i ^ m) for i in range(devices)])  8.54 us
    ppermute x6, waiting for transfers between devices, reduce_moments(): lax.ppermute(local, 'dom', [(i, i ^ m) for i in range(devices)])  7.2 us
    unnamed x17, local copies, waits for them, and re-layouts  4.12 us
  transfers between devices with their start and end apart: 25, of which 19 were waited for; matrix products, arithmetic and copies ran while one was open for 0% of the time, Pallas kernels for 3%

profile of v2, /device:TPU:0, one launch (start us, length us, event | category | flops | bytes accessed | tf_op | source)
XLA Modules:
  0.0 178.6 jit_solution(16088253179744135856)
XLA Ops:
  0.6 0.6 collective-permute-start.7
  1.2 0.9 copy-done.1
  2.2 0.9 copy-done.2
  3.4 0.8 copy.10
  4.7 0.8 collective-permute-done
  5.5 0.7 first.1
  6.2 6.9 %collective-permute-start.5 = (f32[7,128,128]{2,1,0:T(8,128)S(1)}, f32[7,128,128]{2,1,0:T(8,128)S(1)}, u32[]{:S(2)}, u32[]{:S(2)}) collective-permute-start(f32[7,128,128]{2,1,0:T(8,128)S(1)} %get-tuple-element.32), channel_id=1, source_target_pairs={{0,30},{1,31},{2,0},{3,1},{4,2},{5,3},{6,4},{7,5},{8,6},{9,7},{10,... | collective-permute-start | bytes 1376264 | tf_op jit(solution)/shard_map/ppermute | solution.py:261
  13.1 1.4 copy-done
  14.8 5.7 %collective-permute-start.2 = (s32[2,4,3]{2,1,0:T(4,128)S(1)}, s32[2,4,3]{2,1,0:T(4,128)S(1)}, u32[]{:S(2)}, u32[]{:S(2)}) collective-permute-start(s32[2,4,3]{2,1,0:T(4,128)S(1)} %pad_add_fusion.lists), channel_id=1, source_target_pairs={{0,30},{1,31},{2,0},{3,1},{4,2},{5,3},{6,4},{7,5},{8,6},{9,7},{10,... | collective-permute-start | bytes 296 | tf_op jit(solution)/shard_map/ppermute | solution.py:261
  20.5 9.3 %collective-permute-done.2.from_right = s32[2,4,3]{2,1,0:T(4,128)S(1)} collective-permute-done((s32[2,4,3]{2,1,0:T(4,128)S(1)}, s32[2,4,3]{2,1,0:T(4,128)S(1)}, u32[]{:S(2)}, u32[]{:S(2)}) %collective-permute-start.2) | collective-permute-done | bytes 128 | tf_op jit(solution)/shard_map/ppermute | solution.py:261
  29.9 1.2 collective-permute-done.3.from_left
  31.0 2.4 %index.1 = s32[8,6]{1,0:T(8,128)S(1)} custom-call(s32[1]{0:T(128)} %bitcast.core, s32[2,4,3]{2,1,0:T(4,128)S(1)} %pad_add_fusion.lists, s32[2,4,3]{2,1,0:T(4,128)S(1)} %collective-permute-done.2.from_right, s32[2,4,3]{2,1,0:T(4,128)S(1)} %collective-permute-done.3.from_left, s32[2,4,6]{2,1,0:T(4,128)S(1)} %pad_add_fusion.1.cols), custom_call_target="tpu_custom_call" | custom-call | flops 1000 | tf_op jit(solution)/shard_map/index/pallas_call | solution.py:287
  33.8 2.0 %step.6 = (f32[8,128,128]{2,1,0:T(8,128)S(1)}, f32[7,128,128]{2,1,0:T(8,128)S(1)}, f32[7,128,128]{2,1,0:T(8,128)S(1)}) custom-call(s32[1]{0:T(128)} %bitcast.core, s32[2,4,3]{2,1,0:T(4,128)S(1)} %pad_add_fusion.lists, s32[8,6]{1,0:T(8,128)S(1)} %index.1, f32[8,128,128]{2,1,0:T(8,128)S(1)} %get-tuple-element.31.own_ref.refs_0_.refs_1_, ...), custom_call_target="tpu_custom_call" | custom-call | flops 805306368 | bytes 6291456 | tf_op jit(solution)/shard_map/step/pallas_call | solution.py:330
  35.8 4.6 %collective-permute-start.8 = (f32[7,128,128]{2,1,0:T(8,128)S(1)}, f32[7,128,128]{2,1,0:T(8,128)S(1)}, u32[]{:S(2)}, u32[]{:S(2)}) collective-permute-start(f32[7,128,128]{2,1,0:T(8,128)S(1)} %get-tuple-element.39), channel_id=1, source_target_pairs={{0,30},{1,31},{2,0},{3,1},{4,2},{5,3},{6,4},{7,5},{8,6},{9,7},{10,... | collective-permute-start | bytes 1376264 | tf_op jit(solution)/shard_map/ppermute | solution.py:261
  40.4 9.3 %collective-permute-done.8.fr_ref = f32[7,128,128]{2,1,0:T(8,128)S(1)} collective-permute-done((f32[7,128,128]{2,1,0:T(8,128)S(1)}, f32[7,128,128]{2,1,0:T(8,128)S(1)}, u32[]{:S(2)}, u32[]{:S(2)}) %collective-permute-start.8) | collective-permute-done | bytes 458784 | tf_op jit(solution)/shard_map/ppermute | solution.py:261
  49.7 7.7 %collective-permute-done.9.fl_ref = f32[7,128,128]{2,1,0:T(8,128)S(1)} collective-permute-done((f32[7,128,128]{2,1,0:T(8,128)S(1)}, f32[7,128,128]{2,1,0:T(8,128)S(1)}, u32[]{:S(2)}, u32[]{:S(2)}) %collective-permute-start.9) | collective-permute-done | bytes 458784 | tf_op jit(solution)/shard_map/ppermute | solution.py:261
  57.3 1.9 %step.7 = (f32[8,128,128]{2,1,0:T(8,128)S(1)}, f32[7,128,128]{2,1,0:T(8,128)S(1)}, f32[7,128,128]{2,1,0:T(8,128)S(1)}) custom-call(s32[1]{0:T(128)} %bitcast.core, s32[2,4,3]{2,1,0:T(4,128)S(1)} %pad_add_fusion.lists, s32[8,6]{1,0:T(8,128)S(1)} %index.1, f32[8,128,128]{2,1,0:T(8,128)S(1)} %get-tuple-element.38.own_ref.refs_0_.refs_1_, ...), custom_call_target="tpu_custom_call" | custom-call | flops 805306368 | bytes 6291456 | tf_op jit(solution)/shard_map/step/pallas_call | solution.py:330
  59.3 5.5 %collective-permute-start.10 = (f32[7,128,128]{2,1,0:T(8,128)S(1)}, f32[7,128,128]{2,1,0:T(8,128)S(1)}, u32[]{:S(2)}, u32[]{:S(2)}) collective-permute-start(f32[7,128,128]{2,1,0:T(8,128)S(1)} %get-tuple-element.42), channel_id=1, source_target_pairs={{0,30},{1,31},{2,0},{3,1},{4,2},{5,3},{6,4},{7,5},{8,6},{9,7},{10,... | collective-permute-start | bytes 1376264 | tf_op jit(solution)/shard_map/ppermute | solution.py:261
  64.8 8.4 %collective-permute-done.10.fr_ref = f32[7,128,128]{2,1,0:T(8,128)S(1)} collective-permute-done((f32[7,128,128]{2,1,0:T(8,128)S(1)}, f32[7,128,128]{2,1,0:T(8,128)S(1)}, u32[]{:S(2)}, u32[]{:S(2)}) %collective-permute-start.10) | collective-permute-done | bytes 458784 | tf_op jit(solution)/shard_map/ppermute | solution.py:261
  73.2 9.8 %collective-permute-done.11.fl_ref = f32[7,128,128]{2,1,0:T(8,128)S(1)} collective-permute-done((f32[7,128,128]{2,1,0:T(8,128)S(1)}, f32[7,128,128]{2,1,0:T(8,128)S(1)}, u32[]{:S(2)}, u32[]{:S(2)}) %collective-permute-start.11) | collective-permute-done | bytes 458784 | tf_op jit(solution)/shard_map/ppermute | solution.py:261
  83.0 1.9 %step.8 = (f32[8,128,128]{2,1,0:T(8,128)S(1)}, f32[7,128,128]{2,1,0:T(8,128)S(1)}, f32[7,128,128]{2,1,0:T(8,128)S(1)}) custom-call(s32[1]{0:T(128)} %bitcast.core, s32[2,4,3]{2,1,0:T(4,128)S(1)} %pad_add_fusion.lists, s32[8,6]{1,0:T(8,128)S(1)} %index.1, f32[8,128,128]{2,1,0:T(8,128)S(1)} %get-tuple-element.41.own_ref.refs_0_.refs_1_.refs_2_, ...), custom_call_target="tpu_custom_call" | custom-call | flops 805306368 | bytes 6291456 | tf_op jit(solution)/shard_map/step/pallas_call | solution.py:330
  85.0 2.6 %collective-permute-start.12 = (f32[7,128,128]{2,1,0:T(8,128)S(1)}, f32[7,128,128]{2,1,0:T(8,128)S(1)}, u32[]{:S(2)}, u32[]{:S(2)}) collective-permute-start(f32[7,128,128]{2,1,0:T(8,128)S(1)} %get-tuple-element.45), channel_id=1, source_target_pairs={{0,30},{1,31},{2,0},{3,1},{4,2},{5,3},{6,4},{7,5},{8,6},{9,7},{10,... | collective-permute-start | bytes 1376264 | tf_op jit(solution)/shard_map/ppermute | solution.py:261
  87.6 11.3 %collective-permute-done.12.fr_ref = f32[7,128,128]{2,1,0:T(8,128)S(1)} collective-permute-done((f32[7,128,128]{2,1,0:T(8,128)S(1)}, f32[7,128,128]{2,1,0:T(8,128)S(1)}, u32[]{:S(2)}, u32[]{:S(2)}) %collective-permute-start.12) | collective-permute-done | bytes 458784 | tf_op jit(solution)/shard_map/ppermute | solution.py:261
  98.9 7.9 %collective-permute-done.13.fl_ref = f32[7,128,128]{2,1,0:T(8,128)S(1)} collective-permute-done((f32[7,128,128]{2,1,0:T(8,128)S(1)}, f32[7,128,128]{2,1,0:T(8,128)S(1)}, u32[]{:S(2)}, u32[]{:S(2)}) %collective-permute-start.13) | collective-permute-done | bytes 458784 | tf_op jit(solution)/shard_map/ppermute | solution.py:261
  106.8 1.9 %step.9 = (f32[8,128,128]{2,1,0:T(8,128)S(1)}, f32[7,128,128]{2,1,0:T(8,128)S(1)}, f32[7,128,128]{2,1,0:T(8,128)S(1)}) custom-call(s32[1]{0:T(128)} %bitcast.core, s32[2,4,3]{2,1,0:T(4,128)S(1)} %pad_add_fusion.lists, s32[8,6]{1,0:T(8,128)S(1)} %index.1, f32[8,128,128]{2,1,0:T(8,128)S(1)} %get-tuple-element.44.own_ref.refs_0_.refs_1_.refs_3_, ...), custom_call_target="tpu_custom_call" | custom-call | flops 805306368 | bytes 6291456 | tf_op jit(solution)/shard_map/step/pallas_call | solution.py:330
  108.8 1.4 collective-permute-start.14
  110.1 1.2 collective-permute-start.15
  112.0 10.7 %collective-permute-done.14.fr_ref = f32[7,128,128]{2,1,0:T(8,128)S(1)} collective-permute-done((f32[7,128,128]{2,1,0:T(8,128)S(1)}, f32[7,128,128]{2,1,0:T(8,128)S(1)}, u32[]{:S(2)}, u32[]{:S(2)}) %collective-permute-start.14) | collective-permute-done | bytes 458784 | tf_op jit(solution)/shard_map/ppermute | solution.py:261
  122.7 8.5 %collective-permute-done.15.fl_ref = f32[7,128,128]{2,1,0:T(8,128)S(1)} collective-permute-done((f32[7,128,128]{2,1,0:T(8,128)S(1)}, f32[7,128,128]{2,1,0:T(8,128)S(1)}, u32[]{:S(2)}, u32[]{:S(2)}) %collective-permute-start.15) | collective-permute-done | bytes 458784 | tf_op jit(solution)/shard_map/ppermute | solution.py:261
  131.2 1.9 %step.10 = (f32[8,128,128]{2,1,0:T(8,128)S(1)}, f32[7,128,128]{2,1,0:T(8,128)S(1)}, f32[7,128,128]{2,1,0:T(8,128)S(1)}) custom-call(s32[1]{0:T(128)} %bitcast.core, s32[2,4,3]{2,1,0:T(4,128)S(1)} %pad_add_fusion.lists, s32[8,6]{1,0:T(8,128)S(1)} %index.1, f32[8,128,128]{2,1,0:T(8,128)S(1)} %get-tuple-element.47.own_ref.refs_0_.refs_1_.refs_4_, ...), custom_call_target="tpu_custom_call" | custom-call | flops 805306368 | bytes 6291456 | tf_op jit(solution)/shard_map/step/pallas_call | solution.py:330
  133.1 1.3 collective-permute-start.16
  134.4 1.5 collective-permute-start.17
  137.4 9.6 %collective-permute-done.16.fr_ref = f32[7,128,128]{2,1,0:T(8,128)S(1)} collective-permute-done((f32[7,128,128]{2,1,0:T(8,128)S(1)}, f32[7,128,128]{2,1,0:T(8,128)S(1)}, u32[]{:S(2)}, u32[]{:S(2)}) %collective-permute-start.16) | collective-permute-done | bytes 458784 | tf_op jit(solution)/shard_map/ppermute | solution.py:261
  147.0 8.0 %collective-permute-done.17.fl_ref = f32[7,128,128]{2,1,0:T(8,128)S(1)} collective-permute-done((f32[7,128,128]{2,1,0:T(8,128)S(1)}, f32[7,128,128]{2,1,0:T(8,128)S(1)}, u32[]{:S(2)}, u32[]{:S(2)}) %collective-permute-start.17) | collective-permute-done | bytes 458784 | tf_op jit(solution)/shard_map/ppermute | solution.py:261
  155.0 1.9 %step.11.refs_0_.refs_6_ = f32[8,128,128]{2,1,0:T(8,128)S(1)} custom-call(s32[1]{0:T(128)} %bitcast.core, s32[2,4,3]{2,1,0:T(4,128)S(1)} %pad_add_fusion.lists, s32[8,6]{1,0:T(8,128)S(1)} %index.1, f32[8,128,128]{2,1,0:T(8,128)S(1)} %get-tuple-element.50.own_ref.refs_0_.refs_1_.refs_5_, f32[7,128,128]{2,1,0:T(8,128)S(1)} %collective-permute-done.16.fr_ref, ...), custom_call_target="tpu_custom_call" | custom-call | flops 805306368 | bytes 6291456 | tf_op jit(solution)/shard_map/step/pallas_call | solution.py:330
  157.3 2.5 %collective-permute-start.18 = (f32[56,128]{1,0:T(8,128)S(1)}, f32[56,128]{1,0:T(8,128)S(1)}, u32[]{:S(2)}, u32[]{:S(2)}) collective-permute-start(f32[56,128]{1,0:T(8,128)S(1)} %constant_dynamic-update-slice_fusion), channel_id=1, source_target_pairs={{0,2},{1,3},{2,0},{3,1},{4,6},{5,7},{6,4},{7,5},{8,10},{9,11},{10,... | collective-permute-start | bytes 86024 | tf_op jit(solution)/shard_map/ppermute | solution.py:380
  159.8 1.2 collective-permute-start.19
  161.7 2.0 %collective-permute-done.19 = f32[56,128]{1,0:T(8,128)S(1)} collective-permute-done((f32[56,128]{1,0:T(8,128)S(1)}, f32[56,128]{1,0:T(8,128)S(1)}, u32[]{:S(2)}, u32[]{:S(2)}) %collective-permute-start.19) | collective-permute-done | bytes 28704 | tf_op jit(solution)/shard_map/ppermute | solution.py:380
  163.7 2.1 %collective-permute-done.20 = f32[56,128]{1,0:T(8,128)S(1)} collective-permute-done((f32[56,128]{1,0:T(8,128)S(1)}, f32[56,128]{1,0:T(8,128)S(1)}, u32[]{:S(2)}, u32[]{:S(2)}) %collective-permute-start.20) | collective-permute-done | bytes 28704 | tf_op jit(solution)/shard_map/ppermute | solution.py:380
  165.8 1.5 collective-permute-start.21
  167.3 2.9 %collective-permute-start.23 = (f32[56,128]{1,0:T(8,128)S(1)}, f32[56,128]{1,0:T(8,128)S(1)}, u32[]{:S(2)}, u32[]{:S(2)}) collective-permute-start(f32[56,128]{1,0:T(8,128)S(1)} %add_add_fusion.1), channel_id=1, source_target_pairs={{0,24},{1,25},{2,26},{3,27},{4,28},{5,29},{6,30},{7,31},{8,16},{9,... | collective-permute-start | bytes 86024 | tf_op jit(solution)/shard_map/ppermute | solution.py:380
  170.3 2.1 %collective-permute-done.22 = f32[56,128]{1,0:T(8,128)S(1)} collective-permute-done((f32[56,128]{1,0:T(8,128)S(1)}, f32[56,128]{1,0:T(8,128)S(1)}, u32[]{:S(2)}, u32[]{:S(2)}) %collective-permute-start.22) | collective-permute-done | bytes 28704 | tf_op jit(solution)/shard_map/ppermute | solution.py:380
  172.4 0.6 collective-permute-done.23
  173.1 0.5 coefficients.1.refs_7_
  173.6 0.9 combine.1
  174.6 2.3 %collective-permute-done.24 = f32[12,128,128]{2,1,0:T(8,128)S(1)} collective-permute-done((f32[12,128,128]{2,1,0:T(8,128)S(1)}, f32[12,128,128]{2,1,0:T(8,128)S(1)}, u32[]{:S(2)}, u32[]{:S(2)}) %collective-permute-start.24) | collective-permute-done | bytes 786464 | tf_op jit(solution)/shard_map/ppermute | solution.py:261
  177.0 0.8 fusion.1
  177.8 0.7 bitcast_add_fusion
  (48 shorter events, 4.8 us)
Async XLA Ops:
  0.6 19.9 %copy-start.4 = (s32[4,6]{1,0:T(4,128)S(1)}, s32[4,6]{1,0:T(4,128)}, u32[]{:S(2)}) copy-start(s32[4,6]{1,0:T(4,128)} %param.10) | copy-start | bytes 292
  0.6 32.8 %collective-permute-start.7 = (f32[4,6,128,128]{3,2,1,0:T(8,128)}, f32[4,6,128,128]{3,2,1,0:T(8,128)S(1)}, u32[]{:S(2)}, u32[]{:S(2)}) collective-permute-start(f32[4,6,128,128]{3,2,1,0:T(8,128)} %a_ref.1), channel_id=1, source_target_pairs={{0,1},{1,0},{2,3},{3,2},{4,5},{5,4},{6,7},{7,6},{8,9},{9,8},{10,11... | collective-permute-start | bytes 4718600 | tf_op jit(solution)/shard_map/ppermute | solution.py:261
  1.2 0.9 copy-start.1
  2.2 0.9 copy-start.2
  3.3 2.2 %collective-permute-start.1 = (f32[512,128]{1,0:T(8,128)S(1)}, f32[512,128]{1,0:T(8,128)S(1)}, u32[]{:S(2)}, u32[]{:S(2)}) collective-permute-start(f32[512,128]{1,0:T(8,128)S(1)} %get-tuple-element.30), channel_id=1, source_target_pairs={{0,1},{1,0},{2,3},{3,2},{4,5},{5,4},{6,7},{7,6},{8,9},{9,8},{10,11... | collective-permute-start | bytes 786440 | tf_op jit(solution)/shard_map/ppermute | solution.py:261
  4.2 1.3 collective-permute-start
  6.2 27.6 %collective-permute-start.5 = (f32[7,128,128]{2,1,0:T(8,128)S(1)}, f32[7,128,128]{2,1,0:T(8,128)S(1)}, u32[]{:S(2)}, u32[]{:S(2)}) collective-permute-start(f32[7,128,128]{2,1,0:T(8,128)S(1)} %get-tuple-element.32), channel_id=1, source_target_pairs={{0,30},{1,31},{2,0},{3,1},{4,2},{5,3},{6,4},{7,5},{8,6},{9,7},{10,... | collective-permute-start | bytes 1376264 | tf_op jit(solution)/shard_map/ppermute | solution.py:261
  13.0 20.8 %collective-permute-start.6 = (f32[7,128,128]{2,1,0:T(8,128)S(1)}, f32[7,128,128]{2,1,0:T(8,128)S(1)}, u32[]{:S(2)}, u32[]{:S(2)}) collective-permute-start(f32[7,128,128]{2,1,0:T(8,128)S(1)} %get-tuple-element.33), channel_id=1, source_target_pairs={{0,2},{1,3},{2,4},{3,5},{4,6},{5,7},{6,8},{7,9},{8,10},{9,11},{10,... | collective-permute-start | bytes 1376264 | tf_op jit(solution)/shard_map/ppermute | solution.py:261
  13.1 7.5 %collective-permute-start.4 = (s32[4,6]{1,0:T(4,128)}, s32[4,6]{1,0:T(4,128)S(1)}, u32[]{:S(2)}, u32[]{:S(2)}) collective-permute-start(s32[4,6]{1,0:T(4,128)} %param.10), channel_id=1, source_target_pairs={{0,1},{1,0},{2,3},{3,2},{4,5},{5,4},{6,7},{7,6},{8,9},{9,8},{10,11... | collective-permute-start | bytes 296 | tf_op jit(solution)/shard_map/ppermute | solution.py:261
  13.1 1.4 copy-start
  14.8 15.0 %collective-permute-start.2 = (s32[2,4,3]{2,1,0:T(4,128)S(1)}, s32[2,4,3]{2,1,0:T(4,128)S(1)}, u32[]{:S(2)}, u32[]{:S(2)}) collective-permute-start(s32[2,4,3]{2,1,0:T(4,128)S(1)} %pad_add_fusion.lists), channel_id=1, source_target_pairs={{0,30},{1,31},{2,0},{3,1},{4,2},{5,3},{6,4},{7,5},{8,6},{9,7},{10,... | collective-permute-start | bytes 296 | tf_op jit(solution)/shard_map/ppermute | solution.py:261
  20.5 10.5 %collective-permute-start.3 = (s32[2,4,3]{2,1,0:T(4,128)S(1)}, s32[2,4,3]{2,1,0:T(4,128)S(1)}, u32[]{:S(2)}, u32[]{:S(2)}) collective-permute-start(s32[2,4,3]{2,1,0:T(4,128)S(1)} %pad_add_fusion.lists), channel_id=1, source_target_pairs={{0,2},{1,3},{2,4},{3,5},{4,6},{5,7},{6,8},{7,9},{8,10},{9,11},{10,... | collective-permute-start | bytes 296 | tf_op jit(solution)/shard_map/ppermute | solution.py:261
  35.8 13.9 %collective-permute-start.8 = (f32[7,128,128]{2,1,0:T(8,128)S(1)}, f32[7,128,128]{2,1,0:T(8,128)S(1)}, u32[]{:S(2)}, u32[]{:S(2)}) collective-permute-start(f32[7,128,128]{2,1,0:T(8,128)S(1)} %get-tuple-element.39), channel_id=1, source_target_pairs={{0,30},{1,31},{2,0},{3,1},{4,2},{5,3},{6,4},{7,5},{8,6},{9,7},{10,... | collective-permute-start | bytes 1376264 | tf_op jit(solution)/shard_map/ppermute | solution.py:261
  40.4 16.9 %collective-permute-start.9 = (f32[7,128,128]{2,1,0:T(8,128)S(1)}, f32[7,128,128]{2,1,0:T(8,128)S(1)}, u32[]{:S(2)}, u32[]{:S(2)}) collective-permute-start(f32[7,128,128]{2,1,0:T(8,128)S(1)} %get-tuple-element.40), channel_id=1, source_target_pairs={{0,2},{1,3},{2,4},{3,5},{4,6},{5,7},{6,8},{7,9},{8,10},{9,11},{10,... | collective-permute-start | bytes 1376264 | tf_op jit(solution)/shard_map/ppermute | solution.py:261
  59.3 13.9 %collective-permute-start.10 = (f32[7,128,128]{2,1,0:T(8,128)S(1)}, f32[7,128,128]{2,1,0:T(8,128)S(1)}, u32[]{:S(2)}, u32[]{:S(2)}) collective-permute-start(f32[7,128,128]{2,1,0:T(8,128)S(1)} %get-tuple-element.42), channel_id=1, source_target_pairs={{0,30},{1,31},{2,0},{3,1},{4,2},{5,3},{6,4},{7,5},{8,6},{9,7},{10,... | collective-permute-start | bytes 1376264 | tf_op jit(solution)/shard_map/ppermute | solution.py:261
  64.8 18.2 %collective-permute-start.11 = (f32[7,128,128]{2,1,0:T(8,128)S(1)}, f32[7,128,128]{2,1,0:T(8,128)S(1)}, u32[]{:S(2)}, u32[]{:S(2)}) collective-permute-start(f32[7,128,128]{2,1,0:T(8,128)S(1)} %get-tuple-element.43), channel_id=1, source_target_pairs={{0,2},{1,3},{2,4},{3,5},{4,6},{5,7},{6,8},{7,9},{8,10},{9,11},{10,... | collective-permute-start | bytes 1376264 | tf_op jit(solution)/shard_map/ppermute | solution.py:261
  85.0 13.9 %collective-permute-start.12 = (f32[7,128,128]{2,1,0:T(8,128)S(1)}, f32[7,128,128]{2,1,0:T(8,128)S(1)}, u32[]{:S(2)}, u32[]{:S(2)}) collective-permute-start(f32[7,128,128]{2,1,0:T(8,128)S(1)} %get-tuple-element.45), channel_id=1, source_target_pairs={{0,30},{1,31},{2,0},{3,1},{4,2},{5,3},{6,4},{7,5},{8,6},{9,7},{10,... | collective-permute-start | bytes 1376264 | tf_op jit(solution)/shard_map/ppermute | solution.py:261
  87.6 19.2 %collective-permute-start.13 = (f32[7,128,128]{2,1,0:T(8,128)S(1)}, f32[7,128,128]{2,1,0:T(8,128)S(1)}, u32[]{:S(2)}, u32[]{:S(2)}) collective-permute-start(f32[7,128,128]{2,1,0:T(8,128)S(1)} %get-tuple-element.46), channel_id=1, source_target_pairs={{0,2},{1,3},{2,4},{3,5},{4,6},{5,7},{6,8},{7,9},{8,10},{9,11},{10,... | collective-permute-start | bytes 1376264 | tf_op jit(solution)/shard_map/ppermute | solution.py:261
  108.8 13.9 %collective-permute-start.14 = (f32[7,128,128]{2,1,0:T(8,128)S(1)}, f32[7,128,128]{2,1,0:T(8,128)S(1)}, u32[]{:S(2)}, u32[]{:S(2)}) collective-permute-start(f32[7,128,128]{2,1,0:T(8,128)S(1)} %get-tuple-element.48), channel_id=1, source_target_pairs={{0,30},{1,31},{2,0},{3,1},{4,2},{5,3},{6,4},{7,5},{8,6},{9,7},{10,... | collective-permute-start | bytes 1376264 | tf_op jit(solution)/shard_map/ppermute | solution.py:261
  110.1 21.0 %collective-permute-start.15 = (f32[7,128,128]{2,1,0:T(8,128)S(1)}, f32[7,128,128]{2,1,0:T(8,128)S(1)}, u32[]{:S(2)}, u32[]{:S(2)}) collective-permute-start(f32[7,128,128]{2,1,0:T(8,128)S(1)} %get-tuple-element.49), channel_id=1, source_target_pairs={{0,2},{1,3},{2,4},{3,5},{4,6},{5,7},{6,8},{7,9},{8,10},{9,11},{10,... | collective-permute-start | bytes 1376264 | tf_op jit(solution)/shard_map/ppermute | solution.py:261
  133.1 13.9 %collective-permute-start.16 = (f32[7,128,128]{2,1,0:T(8,128)S(1)}, f32[7,128,128]{2,1,0:T(8,128)S(1)}, u32[]{:S(2)}, u32[]{:S(2)}) collective-permute-start(f32[7,128,128]{2,1,0:T(8,128)S(1)} %get-tuple-element.51), channel_id=1, source_target_pairs={{0,30},{1,31},{2,0},{3,1},{4,2},{5,3},{6,4},{7,5},{8,6},{9,7},{10,... | collective-permute-start | bytes 1376264 | tf_op jit(solution)/shard_map/ppermute | solution.py:261
  134.4 20.6 %collective-permute-start.17 = (f32[7,128,128]{2,1,0:T(8,128)S(1)}, f32[7,128,128]{2,1,0:T(8,128)S(1)}, u32[]{:S(2)}, u32[]{:S(2)}) collective-permute-start(f32[7,128,128]{2,1,0:T(8,128)S(1)} %get-tuple-element.52), channel_id=1, source_target_pairs={{0,2},{1,3},{2,4},{3,5},{4,6},{5,7},{6,8},{7,9},{8,10},{9,11},{10,... | collective-permute-start | bytes 1376264 | tf_op jit(solution)/shard_map/ppermute | solution.py:261
  157.3 4.4 %collective-permute-start.18 = (f32[56,128]{1,0:T(8,128)S(1)}, f32[56,128]{1,0:T(8,128)S(1)}, u32[]{:S(2)}, u32[]{:S(2)}) collective-permute-start(f32[56,128]{1,0:T(8,128)S(1)} %constant_dynamic-update-slice_fusion), channel_id=1, source_target_pairs={{0,2},{1,3},{2,0},{3,1},{4,6},{5,7},{6,4},{7,5},{8,10},{9,11},{10,... | collective-permute-start | bytes 86024 | tf_op jit(solution)/shard_map/ppermute | solution.py:380
  159.8 3.9 %collective-permute-start.19 = (f32[56,128]{1,0:T(8,128)S(1)}, f32[56,128]{1,0:T(8,128)S(1)}, u32[]{:S(2)}, u32[]{:S(2)}) collective-permute-start(f32[56,128]{1,0:T(8,128)S(1)} %constant_dynamic-update-slice_fusion), channel_id=1, source_target_pairs={{0,4},{1,5},{2,6},{3,7},{4,0},{5,1},{6,2},{7,3},{8,12},{9,13},{10,... | collective-permute-start | bytes 86024 | tf_op jit(solution)/shard_map/ppermute | solution.py:380
  161.0 4.8 %collective-permute-start.20 = (f32[56,128]{1,0:T(8,128)S(1)}, f32[56,128]{1,0:T(8,128)S(1)}, u32[]{:S(2)}, u32[]{:S(2)}) collective-permute-start(f32[56,128]{1,0:T(8,128)S(1)} %constant_dynamic-update-slice_fusion), channel_id=1, source_target_pairs={{0,6},{1,7},{2,4},{3,5},{4,2},{5,3},{6,0},{7,1},{8,14},{9,15},{10,... | collective-permute-start | bytes 86024 | tf_op jit(solution)/shard_map/ppermute | solution.py:380
  165.8 4.5 %collective-permute-start.21 = (f32[56,128]{1,0:T(8,128)S(1)}, f32[56,128]{1,0:T(8,128)S(1)}, u32[]{:S(2)}, u32[]{:S(2)}) collective-permute-start(f32[56,128]{1,0:T(8,128)S(1)} %add_add_fusion.1), channel_id=1, source_target_pairs={{0,8},{1,9},{2,10},{3,11},{4,12},{5,13},{6,14},{7,15},{8,0},{9,1},... | collective-permute-start | bytes 86024 | tf_op jit(solution)/shard_map/ppermute | solution.py:380
  167.3 5.1 %collective-permute-start.22 = (f32[56,128]{1,0:T(8,128)S(1)}, f32[56,128]{1,0:T(8,128)S(1)}, u32[]{:S(2)}, u32[]{:S(2)}) collective-permute-start(f32[56,128]{1,0:T(8,128)S(1)} %add_add_fusion.1), channel_id=1, source_target_pairs={{0,16},{1,17},{2,18},{3,19},{4,20},{5,21},{6,22},{7,23},{8,24},{9,... | collective-permute-start | bytes 86024 | tf_op jit(solution)/shard_map/ppermute | solution.py:380
  167.3 5.7 %collective-permute-start.23 = (f32[56,128]{1,0:T(8,128)S(1)}, f32[56,128]{1,0:T(8,128)S(1)}, u32[]{:S(2)}, u32[]{:S(2)}) collective-permute-start(f32[56,128]{1,0:T(8,128)S(1)} %add_add_fusion.1), channel_id=1, source_target_pairs={{0,24},{1,25},{2,26},{3,27},{4,28},{5,29},{6,30},{7,31},{8,16},{9,... | collective-permute-start | bytes 86024 | tf_op jit(solution)/shard_map/ppermute | solution.py:380
  174.5 2.4 %collective-permute-start.24 = (f32[12,128,128]{2,1,0:T(8,128)S(1)}, f32[12,128,128]{2,1,0:T(8,128)S(1)}, u32[]{:S(2)}, u32[]{:S(2)}) collective-permute-start(f32[12,128,128]{2,1,0:T(8,128)S(1)} %get-tuple-element.54), channel_id=1, source_target_pairs={{0,1},{1,0},{2,3},{3,2},{4,5},{5,4},{6,7},{7,6},{8,9},{9,8},{10,11... | collective-permute-start | bytes 2359304 | tf_op jit(solution)/shard_map/ppermute | solution.py:261
  176.9 1.0 copy-start.3

commit v3 on v2

v3 whole, which is shorter than its diff:
```python
import functools
import jax
import jax.numpy as jnp
from jax import lax
from jax.experimental import pallas as pl
from jax.experimental.pallas import tpu as pltpu
from jax.sharding import PartitionSpec as P

STEPS = 6
CENTER = 4.5
HALF = 4.5
F32 = jnp.float32
BF16 = jnp.bfloat16
VM = pl.BlockSpec(memory_space=pltpu.VMEM)
SM = pl.BlockSpec(memory_space=pltpu.SMEM)


def call(body, out_shape, in_specs, out_specs, scratch=(), flops=0, bytes_=0, name=None, grid=None):
    extra = {} if grid is None else {"grid": grid}
    return pl.pallas_call(
        body,
        out_shape=out_shape,
        in_specs=in_specs,
        out_specs=out_specs,
        scratch_shapes=list(scratch),
        cost_estimate=pl.CostEstimate(flops=flops, bytes_accessed=bytes_, transcendentals=0),
        name=name,
        compiler_params=pltpu.CompilerParams(vmem_limit_bytes=12 * 2**20),
        **extra,
    )


def halves(shape):
    return lax.broadcasted_iota(jnp.int32, shape, len(shape) - 1) < shape[-1] // 2


def pack_kernel(core, v_ref, mine_ref, send_ref):
    rows, width = v_ref.shape[1:]
    top, bottom = v_ref[:, : rows // 2], v_ref[:, rows // 2 :]
    low = halves(top.shape)
    first = jnp.where(low, top, pltpu.roll(bottom, width // 2, 2))
    second = jnp.where(low, pltpu.roll(top, width // 2, 2), bottom)
    is_first = core[0] == 0
    mine_ref[...] = jnp.where(is_first, first, second)
    send_ref[...] = jnp.where(is_first, second, first)


def copy_halo(core, lists, own, right_ref, left_ref):
    nb = right_ref.shape[0] - lists.shape[2]
    k = core[0]
    for target, whole, part, m in ((right_ref, 1, 0, 3), (left_ref, 0, 1, 1)):
        whole_slot = jnp.bitwise_xor(k, whole)
        part_slot = jnp.bitwise_xor(k, part)
        for b in range(nb):
            target[b] = own[whole_slot * nb + b]
        for e in range(lists.shape[2]):
            target[nb + e] = own[part_slot * nb + lists[part_slot, m, e]]


def first_kernel(core, lists, mine_ref, other_ref, own_ref, right_ref, left_ref):
    nb = mine_ref.shape[0]
    own_ref[:nb] = mine_ref[...]
    own_ref[nb:] = other_ref[...]
    copy_halo(core, lists, own_ref, right_ref, left_ref)


def index_kernel(core, lists, from_right, from_left, cols, out, place):
    k = core[0]
    cap = lists.shape[2]
    _, nb, slots = cols.shape
    right = 2 * nb
    left = 3 * nb + cap
    for s in range(2):
        is0 = jnp.bitwise_xor(k, s) == 0
        other = 1 - s
        for b in range(nb):
            place[b] = s * nb + b
        for e in range(cap):
            place[nb + e] = jnp.where(is0, other * nb + lists[other, 0, e], right + from_right[k, 0, e])
            place[nb + cap + e] = jnp.where(is0, right + from_right[k, 1, e], right + nb + e)
            place[nb + 2 * cap + e] = jnp.where(
                is0, left + from_left[1 - k, 2, e], other * nb + lists[other, 2, e]
            )
            place[nb + 3 * cap + e] = jnp.where(is0, left + nb + e, left + from_left[1 - k, 3, e])
        for b in range(nb):
            for j in range(slots):
                out[s * nb + b, j] = place[cols[s, b, j]]


def matrix_kernel(a_ref, hi_ref, lo_ref):
    slots, rows, cols = a_ref.shape[1:]
    diag = lax.broadcasted_iota(jnp.int32, (rows, cols), 0) == lax.broadcasted_iota(
        jnp.int32, (rows, cols), 1
    )
    for j in range(slots):
        a = a_ref[0, j]
        if j == 0:
            a = a - jnp.where(diag, F32(CENTER), F32(0.0))
        a = a * F32(1.0 / HALF)
        hi = a.astype(BF16)
        hi_ref[0, :, j * cols : (j + 1) * cols] = hi
        lo_ref[0, :, j * cols : (j + 1) * cols] = (a - hi.astype(F32)).astype(BF16)


def step_kernel(last, core, lists, index, own_ref, fr_ref, fl_ref, h0, l0, h1, l1, new_ref, *rest):
    if last:
        (table,) = rest
    else:
        right_ref, left_ref, table = rest
    n_own, cut, width = own_ref.shape
    rows, half = 2 * cut, width // 2
    low = halves((cut, width))
    place = 0
    for ref in (own_ref, fr_ref, fl_ref):
        for b in range(ref.shape[0]):
            v = ref[b]
            hi = v.astype(BF16).astype(F32)
            lo = v - hi
            table[place, :cut] = jnp.where(low, hi, pltpu.roll(lo, half, 1)).astype(BF16)
            table[place, cut:] = jnp.where(low, pltpu.roll(hi, half, 1), lo).astype(BF16)
            place += 1
    slots = index.shape[1]
    for i in range(n_own):
        h, l = (h0, l0) if i < n_own // 2 else (h1, l1)
        acc = None
        for j in range(0, slots, 2):
            cols = [table[index[i, q]] for q in range(j, min(j + 2, slots))]
            tile = jnp.concatenate(cols, axis=0) if len(cols) > 1 else cols[0]
            span = slice(j * rows, (j + len(cols)) * rows)
            for part in (h, l):
                d = jnp.dot(part[i % (n_own // 2), :, span], tile, preferred_element_type=F32)
                acc = d if acc is None else acc + d
        acc = acc + pltpu.roll(acc, half, 1)
        new_ref[i] = jnp.where(low, acc[:cut], acc[cut:])
    if not last:
        copy_halo(core, lists, new_ref, right_ref, left_ref)


def fold(x):
    return jnp.sum(x.reshape(-1, 8, x.shape[-1]), axis=0)


def moment_kernel(pairs, *refs):
    out = refs[-1]
    blocks, _, width = refs[0].shape
    acc = [None] * 8
    for b in range(blocks):
        v = [ref[b] for ref in refs[:-1]]
        for i, pair in enumerate(pairs):
            if pair is not None:
                t = fold(v[pair[0]] * v[pair[1]])
                acc[i] = t if acc[i] is None else acc[i] + t
    for i in range(8):
        if acc[i] is None:
            out[i : i + 1, :] = jnp.zeros((1, width), F32)
        else:
            out[i : i + 1, :] = jnp.sum(acc[i], axis=0, keepdims=True)


def coefficient_kernel(m_ref, out_ref, gram_ref, sum_ref):
    width = m_ref.shape[1]
    count = STEPS + 1
    sum_ref[...] = m_ref[...] + pltpu.roll(m_ref[...], width // 2, 1)

    def moment(kind, n):
        at = 8 * ((n + 1) // 2) + 2 * kind + (0 if n % 2 else 1)
        return sum_ref[at : at + 1, :]

    size = gram_ref.shape[1]
    gram_ref[...] = jnp.zeros(gram_ref.shape, F32)
    for a in range(count):
        for b in range(count):
            gram_ref[a, b : b + 1, :] = moment(0, a + b)
            if b < STEPS:
                gram_ref[a, count + b : count + b + 1, :] = moment(1, a + b)
            if a < STEPS:
                gram_ref[count + a, b : b + 1, :] = moment(1, a + b)
            if a < STEPS and b < STEPS:
                gram_ref[count + a, count + b : count + b + 1, :] = moment(2, a + b)
    ids = lax.broadcasted_iota(jnp.int32, (size, width), 0)
    active = (ids < STEPS) | ((ids > STEPS) & (ids < 2 * STEPS))

    def change(v):
        v = jnp.where(active, v, F32(0.0))
        return F32(CENTER) * v + F32(HALF) * pltpu.roll(v, 1, 0)

    def times(v):
        out = None
        for a in range(2 * STEPS + 1):
            t = gram_ref[a] * v[a : a + 1, :]
            out = t if out is None else out + t
        return out

    def dot(u, v):
        return jnp.sum(u * v, axis=0, keepdims=True)

    x = jnp.zeros((size, width), F32)
    r = jnp.where(ids == STEPS + 1, F32(1.0), F32(0.0))
    d = jnp.where(ids == 0, F32(1.0), F32(0.0))
    current = dot(r, times(r))
    for _ in range(STEPS):
        moved = change(d)
        alpha = current / dot(d, times(moved))
        x = x + alpha * d
        r = r - alpha * moved
        following = dot(r, times(r))
        d = r + (following / current) * d
        current = following
    for q, v in enumerate((x, r, d)):
        out_ref[size * q : size * (q + 1), :] = v


def combine_kernel(second, *refs):
    basis, (w_ref, out_ref) = refs[:-2], refs[-2:]
    nb = basis[0].shape[0] // 2
    size = w_ref.shape[0] // 3
    for b in range(nb):
        vs = [s[second * nb + b] for s in basis]
        for q in range(3):
            out = None
            for j, v in enumerate(vs):
                t = v * w_ref[size * q + j : size * q + j + 1, :]
                out = t if out is None else out + t
            out_ref[q * nb + b] = out


def unpack_kernel(core, start_ref, mine_ref, other_ref, *out_refs):
    nb, rows, width = start_ref.shape
    cut, half = rows // 2, width // 2
    is_first = core[0] == 0
    low = halves((cut, width))
    for q, out_ref in enumerate(out_refs):
        for b in range(nb):
            mine, other = mine_ref[q * nb + b], other_ref[q * nb + b]
            first = jnp.where(is_first, mine, other)
            second = jnp.where(is_first, other, mine)
            top = jnp.where(low, first, pltpu.roll(second, half, 1))
            bottom = jnp.where(low, pltpu.roll(first, half, 1), second)
            if q == 0:
                top = top + start_ref[b, :cut]
                bottom = bottom + start_ref[b, cut:]
            out_ref[b, :cut] = top
            out_ref[b, cut:] = bottom


def shards(devices, start_point, residual, direction, send_list, block_cols, block_vals):
    nb, slots, rows, _ = block_vals.shape
    cap = send_list.shape[2]
    width = direction.shape[1]
    cut = rows // 2
    ghosts = nb + cap
    sds = jax.ShapeDtypeStruct
    vec = lambda n: sds((n, cut, width), F32)
    core = (lax.axis_index("dom") % 2).astype(jnp.int32).reshape(1)
    swap = [(i, i ^ 1) for i in range(devices)]
    to_right = [(i, (i + 2) % devices) for i in range(devices)]
    to_left = [(i, (i - 2) % devices) for i in range(devices)]
    permute = lambda v, pairs: lax.ppermute(v, "dom", pairs)
    blocked = lambda v: v.reshape(nb, rows, width)
    size = direction.size

    lists = jnp.stack([send_list[0], permute(send_list[0], swap)])
    lists_right, lists_left = permute(lists, to_left), permute(lists, to_right)

    def pack(v):
        return call(
            pack_kernel, [vec(nb)] * 2, [SM, VM], [VM, VM], flops=4 * size, bytes_=8 * size, name="pack"
        )(core, blocked(v))

    def begin(mine, other):
        return call(
            first_kernel,
            [vec(2 * nb), vec(ghosts), vec(ghosts)],
            [SM, SM, VM, VM],
            [VM, VM, VM],
            flops=4 * size,
            bytes_=12 * size,
            name="first",
        )(core, lists, mine, other)

    def exchange(right, left):
        return permute(left, to_left), permute(right, to_right)

    packed = [pack(v) for v in (direction, residual)]
    started = [begin(mine, permute(send, swap)) for mine, send in packed]
    halo = [exchange(right, left) for _, right, left in started]
    p_basis, r_basis = ([own] for own, _, _ in started)

    vals_other = permute(block_vals, swap)
    cols = jnp.stack([block_cols, permute(block_cols, swap)])
    index = call(
        index_kernel,
        sds((2 * nb, slots), jnp.int32),
        [SM] * 5,
        SM,
        scratch=[pltpu.SMEM((nb + 4 * cap,), jnp.int32)],
        flops=1000,
        name="index",
    )(core, lists, lists_right, lists_left, cols)

    def split(vals):
        spec = pl.BlockSpec((1, rows, slots * rows), lambda i: (i, 0, 0))
        return call(
            matrix_kernel,
            [sds((nb, rows, slots * rows), BF16)] * 2,
            [pl.BlockSpec((1, slots, rows, rows), lambda i: (i, 0, 0, 0))],
            [spec, spec],
            grid=(nb,),
            flops=4 * vals.size,
            bytes_=8 * vals.size,
            name="matrix",
        )(vals)

    parts = split(block_vals) + split(vals_other)
    moments = []

    def moment(j):
        now_r = j < STEPS
        args = [p_basis[j]] + ([r_basis[j]] if now_r else [])
        if j:
            args += [p_basis[j - 1], r_basis[j - 1]]
        p, r = 0, 1
        q, s = len(args) - 2, len(args) - 1
        pairs = [
            (p, q) if j else None,
            (p, p),
            (p, s) if j else None,
            (p, r) if now_r else None,
            (r, s) if j and now_r else None,
            (r, r) if now_r else None,
        ]
        moments.append(
            call(
                functools.partial(moment_kernel, pairs),
                sds((8, width), F32),
                [VM] * len(args),
                VM,
                flops=12 * size,
                bytes_=16 * size,
                name="moment",
            )(*args)
        )

    def step(v, halo, last):
        out = [vec(2 * nb)] + ([] if last else [vec(ghosts), vec(ghosts)])
        return call(
            functools.partial(step_kernel, last),
            out,
            [SM] * 3 + [VM] * 7,
            [VM] * len(out),
            scratch=[pltpu.VMEM((2 * nb + 2 * ghosts, rows, width), BF16)],
            flops=2 * 4 * 2 * nb * slots * rows * rows * width,
            bytes_=8 * 2 * nb * slots * rows * rows,
            name="step",
        )(core, lists, index, v, *halo, *parts)

    for j in range(STEPS):
        for which, (basis, count) in enumerate(((p_basis, STEPS), (r_basis, STEPS - 1))):
            if j < count:
                last = j == count - 1
                res = step(basis[-1], halo[which], last)
                basis.append(res[0])
                if not last:
                    halo[which] = exchange(res[1], res[2])
        moment(j)
    moment(STEPS)
    total = reduce_moments(jnp.concatenate(moments, axis=0), devices)
    lanes = 16
    weights = call(
        coefficient_kernel,
        sds((3 * lanes, width), F32),
        [VM],
        VM,
        scratch=[
            pltpu.VMEM((2 * STEPS + 1, lanes, width), F32),
            pltpu.VMEM(total.shape, F32),
        ],
        flops=100000,
        name="coefficients",
    )(total)
    basis = p_basis + r_basis

    def combine(second):
        return call(
            functools.partial(combine_kernel, second),
            vec(3 * nb),
            [VM] * (len(basis) + 1),
            VM,
            flops=6 * len(basis) * size // 2,
            bytes_=4 * (len(basis) + 3) * size // 2,
            name="combine",
        )(*basis, weights)

    other = permute(combine(1), swap)
    outs = call(
        unpack_kernel,
        [sds((nb, rows, width), F32)] * 3,
        [SM, VM, VM, VM],
        [VM] * 3,
        flops=6 * size,
        bytes_=28 * size,
        name="unpack",
    )(core, blocked(start_point), combine(0), other)
    return tuple(o.reshape(start_point.shape) for o in outs)


def reduce_moments(local, devices):
    pairs = devices // 2
    if pairs & (pairs - 1):
        index = lax.axis_index("dom")
        slot = (lax.broadcasted_iota(jnp.int32, (2, 1, 1), 0) == index % 2).astype(F32)
        both = lax.psum(local[None] * slot, "dom")
        return jnp.where(index % 2 == 0, both[0], both[1])
    bit = 2
    while bit < devices:
        masks = [bit, 2 * bit, 3 * bit] if 2 * bit < devices else [bit]
        parts = [lax.ppermute(local, "dom", [(i, i ^ m) for i in range(devices)]) for m in masks]
        for part in parts:
            local = local + part
        bit *= 4
    return local


def solution(mesh):
    devices = mesh.shape["dom"]
    return jax.shard_map(
        functools.partial(shards, devices),
        mesh=mesh,
        in_specs=(
            P("dom", None),
            P("dom", None),
            P("dom", None),
            P("dom", None, None),
            P("dom", None),
            P("dom", None, None, None),
        ),
        out_specs=(P("dom", None), P("dom", None), P("dom", None)),
        check_vma=False,
    )
```

time: 179 us -> 145 us (0.81)
  waiting for transfers between devices: 112 us -> 42.3 us
  starting transfers between devices: 40.4 us -> 68.1 us
  Pallas kernels: 19.5 us -> 29 us
    ppermute x19 -> x30, waiting for transfers between devices: 105 us -> 34.9 us  [shards(): permute = lambda v, pairs: lax.ppermute(v, 'dom', pairs)]
    ppermute x19 -> x30, starting transfers between devices: 31.8 us -> 58.8 us  [shards(): permute = lambda v, pairs: lax.ppermute(v, 'dom', pairs)]
    pallas_call x18 -> x27, Pallas kernels: 18.7 us -> 28.3 us  [the longest x11 22 us: step(): call(functools.partial(step_kernel, last), out, [SM] * 3 + [VM] * 7, [VM]...]
    unnamed x17 -> x15, local copies, waits for them, and re-layouts: 4.12 us -> 4.09 us
  transfers between devices with their start and end apart: 25 -> 36, of which waited for: 19 -> 18; matrix products, arithmetic and copies ran while one was open for 0% -> 1% of each run, Pallas kernels for 3% -> 17%
where the time goes in v3:
time: 145 us
  starting transfers between devices  68.1 us (47%)
  waiting for transfers between devices  42.3 us (29%)
  Pallas kernels  29 us (20%)
  local copies, waits for them, and re-layouts  4.1 us (3%)
    ppermute x30, starting transfers between devices, shards(): permute = lambda v, pairs: lax.ppermute(v, 'dom', pairs)  58.8 us
    ppermute x30, waiting for transfers between devices, shards(): permute = lambda v, pairs: lax.ppermute(v, 'dom', pairs)  34.9 us
    pallas_call x11, Pallas kernels, step(): call(functools.partial(step_kernel, last), out, [SM] * 3 + [VM] * 7, [VM]...  22 us
    ppermute x6, starting transfers between devices, reduce_moments(): lax.ppermute(local, 'dom', [(i, i ^ m) for i in range(devices)])  9.26 us
    ppermute x6, waiting for transfers between devices, reduce_moments(): lax.ppermute(local, 'dom', [(i, i ^ m) for i in range(devices)])  7.39 us
    unnamed x15, local copies, waits for them, and re-layouts  4.09 us
  transfers between devices with their start and end apart: 36, of which 18 were waited for; matrix products, arithmetic and copies ran while one was open for 1% of the time, Pallas kernels for 17%

profile of v3, /device:TPU:0, one launch (start us, length us, event | category | flops | bytes accessed | tf_op | source)
XLA Modules:
  0.0 145.2 jit_solution(8456622400105484199)
XLA Ops:
  1.2 0.9 copy-done.1
  2.4 0.9 copy-done.2
  4.8 1.1 collective-permute-done
  6.6 6.7 %collective-permute-start.5 = (f32[7,64,128]{2,1,0:T(8,128)S(1)}, f32[7,64,128]{2,1,0:T(8,128)S(1)}, u32[]{:S(2)}, u32[]{:S(2)}) collective-permute-start(f32[7,64,128]{2,1,0:T(8,128)S(1)} %get-tuple-element.50), channel_id=1, source_target_pairs={{0,30},{1,31},{2,0},{3,1},{4,2},{5,3},{6,4},{7,5},{8,6},{9,7},{10,... | collective-permute-start | bytes 688136 | tf_op jit(solution)/shard_map/ppermute | solution.py:258
  13.4 5.6 %collective-permute-start.2 = (s32[2,4,3]{2,1,0:T(4,128)S(1)}, s32[2,4,3]{2,1,0:T(4,128)S(1)}, u32[]{:S(2)}, u32[]{:S(2)}) collective-permute-start(s32[2,4,3]{2,1,0:T(4,128)S(1)} %pad_add_fusion.lists), channel_id=1, source_target_pairs={{0,30},{1,31},{2,0},{3,1},{4,2},{5,3},{6,4},{7,5},{8,6},{9,7},{10,... | collective-permute-start | bytes 296 | tf_op jit(solution)/shard_map/ppermute | solution.py:258
  19.7 0.8 collective-permute-done.2.from_right
  20.5 5.7 %collective-permute-start.19 = (f32[7,64,128]{2,1,0:T(8,128)S(1)}, f32[7,64,128]{2,1,0:T(8,128)S(1)}, u32[]{:S(2)}, u32[]{:S(2)}) collective-permute-start(f32[7,64,128]{2,1,0:T(8,128)S(1)} %get-tuple-element.74), channel_id=1, source_target_pairs={{0,30},{1,31},{2,0},{3,1},{4,2},{5,3},{6,4},{7,5},{8,6},{9,7},{10,... | collective-permute-start | bytes 688136 | tf_op jit(solution)/shard_map/ppermute | solution.py:258
  26.1 0.8 collective-permute-done.3.from_left
  27.6 1.4 copy-done
  29.4 1.5 %index.1 = s32[8,6]{1,0:T(8,128)S(1)} custom-call(s32[1]{0:T(128)} %bitcast.core, s32[2,4,3]{2,1,0:T(4,128)S(1)} %pad_add_fusion.lists, s32[2,4,3]{2,1,0:T(4,128)S(1)} %collective-permute-done.2.from_right, s32[2,4,3]{2,1,0:T(4,128)S(1)} %collective-permute-done.3.from_left, s32[2,4,6]{2,1,0:T(4,128)S(1)} %pad_add_fusion.1.cols), custom_call_target="tpu_custom_call" | custom-call | flops 1000 | tf_op jit(solution)/shard_map/index/pallas_call | solution.py:291
  31.4 2.0 %step.11 = (f32[8,64,128]{2,1,0:T(8,128)S(1)}, f32[7,64,128]{2,1,0:T(8,128)S(1)}, f32[7,64,128]{2,1,0:T(8,128)S(1)}) custom-call(s32[1]{0:T(128)} %bitcast.core, s32[2,4,3]{2,1,0:T(4,128)S(1)} %pad_add_fusion.lists, s32[8,6]{1,0:T(8,128)S(1)} %index.1, f32[8,64,128]{2,1,0:T(8,128)S(1)} %get-tuple-element.49.own_ref.refs_0_.refs_2_, ...), custom_call_target="tpu_custom_call" | custom-call | flops 805306368 | bytes 6291456 | tf_op jit(solution)/shard_map/step/pallas_call | solution.py:346
  33.4 5.7 %collective-permute-start.8 = (f32[7,64,128]{2,1,0:T(8,128)S(1)}, f32[7,64,128]{2,1,0:T(8,128)S(1)}, u32[]{:S(2)}, u32[]{:S(2)}) collective-permute-start(f32[7,64,128]{2,1,0:T(8,128)S(1)} %get-tuple-element.57), channel_id=1, source_target_pairs={{0,30},{1,31},{2,0},{3,1},{4,2},{5,3},{6,4},{7,5},{8,6},{9,7},{10,... | collective-permute-start | bytes 688136 | tf_op jit(solution)/shard_map/ppermute | solution.py:258
  39.1 2.0 %step.17 = (f32[8,64,128]{2,1,0:T(8,128)S(1)}, f32[7,64,128]{2,1,0:T(8,128)S(1)}, f32[7,64,128]{2,1,0:T(8,128)S(1)}) custom-call(s32[1]{0:T(128)} %bitcast.core, s32[2,4,3]{2,1,0:T(4,128)S(1)} %pad_add_fusion.lists, s32[8,6]{1,0:T(8,128)S(1)} %index.1, f32[8,64,128]{2,1,0:T(8,128)S(1)} %get-tuple-element.73.own_ref.refs_1_.refs_3_.refs_7_, ...), custom_call_target="tpu_custom_call" | custom-call | flops 805306368 | bytes 6291456 | tf_op jit(solution)/shard_map/step/pallas_call | solution.py:346
  41.1 5.7 %collective-permute-start.21 = (f32[7,64,128]{2,1,0:T(8,128)S(1)}, f32[7,64,128]{2,1,0:T(8,128)S(1)}, u32[]{:S(2)}, u32[]{:S(2)}) collective-permute-start(f32[7,64,128]{2,1,0:T(8,128)S(1)} %get-tuple-element.77), channel_id=1, source_target_pairs={{0,30},{1,31},{2,0},{3,1},{4,2},{5,3},{6,4},{7,5},{8,6},{9,7},{10,... | collective-permute-start | bytes 688136 | tf_op jit(solution)/shard_map/ppermute | solution.py:258
  46.8 2.0 %collective-permute-done.9.fl_ref = f32[7,64,128]{2,1,0:T(8,128)S(1)} collective-permute-done((f32[7,64,128]{2,1,0:T(8,128)S(1)}, f32[7,64,128]{2,1,0:T(8,128)S(1)}, u32[]{:S(2)}, u32[]{:S(2)}) %collective-permute-start.9) | collective-permute-done | bytes 229408 | tf_op jit(solution)/shard_map/ppermute | solution.py:258
  48.8 2.0 %step.12 = (f32[8,64,128]{2,1,0:T(8,128)S(1)}, f32[7,64,128]{2,1,0:T(8,128)S(1)}, f32[7,64,128]{2,1,0:T(8,128)S(1)}) custom-call(s32[1]{0:T(128)} %bitcast.core, s32[2,4,3]{2,1,0:T(4,128)S(1)} %pad_add_fusion.lists, s32[8,6]{1,0:T(8,128)S(1)} %index.1, f32[8,64,128]{2,1,0:T(8,128)S(1)} %get-tuple-element.56.own_ref.refs_0_.refs_2_.refs_1_, ...), custom_call_target="tpu_custom_call" | custom-call | flops 805306368 | bytes 6291456 | tf_op jit(solution)/shard_map/step/pallas_call | solution.py:346
  50.8 3.7 %collective-permute-start.10 = (f32[7,64,128]{2,1,0:T(8,128)S(1)}, f32[7,64,128]{2,1,0:T(8,128)S(1)}, u32[]{:S(2)}, u32[]{:S(2)}) collective-permute-start(f32[7,64,128]{2,1,0:T(8,128)S(1)} %get-tuple-element.60), channel_id=1, source_target_pairs={{0,30},{1,31},{2,0},{3,1},{4,2},{5,3},{6,4},{7,5},{8,6},{9,7},{10,... | collective-permute-start | bytes 688136 | tf_op jit(solution)/shard_map/ppermute | solution.py:258
  54.5 3.2 %collective-permute-done.22.fl_ref = f32[7,64,128]{2,1,0:T(8,128)S(1)} collective-permute-done((f32[7,64,128]{2,1,0:T(8,128)S(1)}, f32[7,64,128]{2,1,0:T(8,128)S(1)}, u32[]{:S(2)}, u32[]{:S(2)}) %collective-permute-start.22) | collective-permute-done | bytes 229408 | tf_op jit(solution)/shard_map/ppermute | solution.py:258
  57.7 2.0 %step.18 = (f32[8,64,128]{2,1,0:T(8,128)S(1)}, f32[7,64,128]{2,1,0:T(8,128)S(1)}, f32[7,64,128]{2,1,0:T(8,128)S(1)}) custom-call(s32[1]{0:T(128)} %bitcast.core, s32[2,4,3]{2,1,0:T(4,128)S(1)} %pad_add_fusion.lists, s32[8,6]{1,0:T(8,128)S(1)} %index.1, f32[8,64,128]{2,1,0:T(8,128)S(1)} %get-tuple-element.76.own_ref.refs_1_.refs_3_.refs_8_, ...), custom_call_target="tpu_custom_call" | custom-call | flops 805306368 | bytes 6291456 | tf_op jit(solution)/shard_map/step/pallas_call | solution.py:346
  59.7 4.1 %collective-permute-start.23 = (f32[7,64,128]{2,1,0:T(8,128)S(1)}, f32[7,64,128]{2,1,0:T(8,128)S(1)}, u32[]{:S(2)}, u32[]{:S(2)}) collective-permute-start(f32[7,64,128]{2,1,0:T(8,128)S(1)} %get-tuple-element.80), channel_id=1, source_target_pairs={{0,30},{1,31},{2,0},{3,1},{4,2},{5,3},{6,4},{7,5},{8,6},{9,7},{10,... | collective-permute-start | bytes 688136 | tf_op jit(solution)/shard_map/ppermute | solution.py:258
  63.9 3.7 %collective-permute-done.11.fl_ref = f32[7,64,128]{2,1,0:T(8,128)S(1)} collective-permute-done((f32[7,64,128]{2,1,0:T(8,128)S(1)}, f32[7,64,128]{2,1,0:T(8,128)S(1)}, u32[]{:S(2)}, u32[]{:S(2)}) %collective-permute-start.11) | collective-permute-done | bytes 229408 | tf_op jit(solution)/shard_map/ppermute | solution.py:258
  67.6 2.0 %step.13 = (f32[8,64,128]{2,1,0:T(8,128)S(1)}, f32[7,64,128]{2,1,0:T(8,128)S(1)}, f32[7,64,128]{2,1,0:T(8,128)S(1)}) custom-call(s32[1]{0:T(128)} %bitcast.core, s32[2,4,3]{2,1,0:T(4,128)S(1)} %pad_add_fusion.lists, s32[8,6]{1,0:T(8,128)S(1)} %index.1, f32[8,64,128]{2,1,0:T(8,128)S(1)} %get-tuple-element.59.own_ref.refs_0_.refs_2_, ...), custom_call_target="tpu_custom_call" | custom-call | flops 805306368 | bytes 6291456 | tf_op jit(solution)/shard_map/step/pallas_call | solution.py:346
  69.6 4.1 %collective-permute-start.12 = (f32[7,64,128]{2,1,0:T(8,128)S(1)}, f32[7,64,128]{2,1,0:T(8,128)S(1)}, u32[]{:S(2)}, u32[]{:S(2)}) collective-permute-start(f32[7,64,128]{2,1,0:T(8,128)S(1)} %get-tuple-element.63), channel_id=1, source_target_pairs={{0,30},{1,31},{2,0},{3,1},{4,2},{5,3},{6,4},{7,5},{8,6},{9,7},{10,... | collective-permute-start | bytes 688136 | tf_op jit(solution)/shard_map/ppermute | solution.py:258
  73.8 3.6 %collective-permute-done.24.fl_ref = f32[7,64,128]{2,1,0:T(8,128)S(1)} collective-permute-done((f32[7,64,128]{2,1,0:T(8,128)S(1)}, f32[7,64,128]{2,1,0:T(8,128)S(1)}, u32[]{:S(2)}, u32[]{:S(2)}) %collective-permute-start.24) | collective-permute-done | bytes 229408 | tf_op jit(solution)/shard_map/ppermute | solution.py:258
  77.4 2.0 %step.19 = (f32[8,64,128]{2,1,0:T(8,128)S(1)}, f32[7,64,128]{2,1,0:T(8,128)S(1)}, f32[7,64,128]{2,1,0:T(8,128)S(1)}) custom-call(s32[1]{0:T(128)} %bitcast.core, s32[2,4,3]{2,1,0:T(4,128)S(1)} %pad_add_fusion.lists, s32[8,6]{1,0:T(8,128)S(1)} %index.1, f32[8,64,128]{2,1,0:T(8,128)S(1)} %get-tuple-element.79.own_ref.refs_1_.refs_3_.refs_9_, ...), custom_call_target="tpu_custom_call" | custom-call | flops 805306368 | bytes 6291456 | tf_op jit(solution)/shard_map/step/pallas_call | solution.py:346
  79.4 4.1 %collective-permute-start.25 = (f32[7,64,128]{2,1,0:T(8,128)S(1)}, f32[7,64,128]{2,1,0:T(8,128)S(1)}, u32[]{:S(2)}, u32[]{:S(2)}) collective-permute-start(f32[7,64,128]{2,1,0:T(8,128)S(1)} %get-tuple-element.83), channel_id=1, source_target_pairs={{0,30},{1,31},{2,0},{3,1},{4,2},{5,3},{6,4},{7,5},{8,6},{9,7},{10,... | collective-permute-start | bytes 688136 | tf_op jit(solution)/shard_map/ppermute | solution.py:258
  83.6 3.6 %collective-permute-done.13.fl_ref = f32[7,64,128]{2,1,0:T(8,128)S(1)} collective-permute-done((f32[7,64,128]{2,1,0:T(8,128)S(1)}, f32[7,64,128]{2,1,0:T(8,128)S(1)}, u32[]{:S(2)}, u32[]{:S(2)}) %collective-permute-start.13) | collective-permute-done | bytes 229408 | tf_op jit(solution)/shard_map/ppermute | solution.py:258
  87.2 2.0 %step.14 = (f32[8,64,128]{2,1,0:T(8,128)S(1)}, f32[7,64,128]{2,1,0:T(8,128)S(1)}, f32[7,64,128]{2,1,0:T(8,128)S(1)}) custom-call(s32[1]{0:T(128)} %bitcast.core, s32[2,4,3]{2,1,0:T(4,128)S(1)} %pad_add_fusion.lists, s32[8,6]{1,0:T(8,128)S(1)} %index.1, f32[8,64,128]{2,1,0:T(8,128)S(1)} %get-tuple-element.62.own_ref.refs_0_.refs_2_.refs_3_, ...), custom_call_target="tpu_custom_call" | custom-call | flops 805306368 | bytes 6291456 | tf_op jit(solution)/shard_map/step/pallas_call | solution.py:346
  89.2 4.1 %collective-permute-start.14 = (f32[7,64,128]{2,1,0:T(8,128)S(1)}, f32[7,64,128]{2,1,0:T(8,128)S(1)}, u32[]{:S(2)}, u32[]{:S(2)}) collective-permute-start(f32[7,64,128]{2,1,0:T(8,128)S(1)} %get-tuple-element.66), channel_id=1, source_target_pairs={{0,30},{1,31},{2,0},{3,1},{4,2},{5,3},{6,4},{7,5},{8,6},{9,7},{10,... | collective-permute-start | bytes 688136 | tf_op jit(solution)/shard_map/ppermute | solution.py:258
  93.5 3.6 %collective-permute-done.26.fl_ref = f32[7,64,128]{2,1,0:T(8,128)S(1)} collective-permute-done((f32[7,64,128]{2,1,0:T(8,128)S(1)}, f32[7,64,128]{2,1,0:T(8,128)S(1)}, u32[]{:S(2)}, u32[]{:S(2)}) %collective-permute-start.26) | collective-permute-done | bytes 229408 | tf_op jit(solution)/shard_map/ppermute | solution.py:258
  97.1 2.0 %step.20 = (f32[8,64,128]{2,1,0:T(8,128)S(1)}, f32[7,64,128]{2,1,0:T(8,128)S(1)}, f32[7,64,128]{2,1,0:T(8,128)S(1)}) custom-call(s32[1]{0:T(128)} %bitcast.core, s32[2,4,3]{2,1,0:T(4,128)S(1)} %pad_add_fusion.lists, s32[8,6]{1,0:T(8,128)S(1)} %index.1, f32[8,64,128]{2,1,0:T(8,128)S(1)} %get-tuple-element.82.own_ref.refs_1_.refs_3_.refs_10_, ...), custom_call_target="tpu_custom_call" | custom-call | flops 805306368 | bytes 6291456 | tf_op jit(solution)/shard_map/step/pallas_call | solution.py:346
  99.1 4.1 %collective-permute-start.27 = (f32[7,64,128]{2,1,0:T(8,128)S(1)}, f32[7,64,128]{2,1,0:T(8,128)S(1)}, u32[]{:S(2)}, u32[]{:S(2)}) collective-permute-start(f32[7,64,128]{2,1,0:T(8,128)S(1)} %get-tuple-element.86), channel_id=1, source_target_pairs={{0,30},{1,31},{2,0},{3,1},{4,2},{5,3},{6,4},{7,5},{8,6},{9,7},{10,... | collective-permute-start | bytes 688136 | tf_op jit(solution)/shard_map/ppermute | solution.py:258
  103.3 3.6 %collective-permute-done.15.fl_ref = f32[7,64,128]{2,1,0:T(8,128)S(1)} collective-permute-done((f32[7,64,128]{2,1,0:T(8,128)S(1)}, f32[7,64,128]{2,1,0:T(8,128)S(1)}, u32[]{:S(2)}, u32[]{:S(2)}) %collective-permute-start.15) | collective-permute-done | bytes 229408 | tf_op jit(solution)/shard_map/ppermute | solution.py:258
  106.9 2.0 %step.15 = (f32[8,64,128]{2,1,0:T(8,128)S(1)}, f32[7,64,128]{2,1,0:T(8,128)S(1)}, f32[7,64,128]{2,1,0:T(8,128)S(1)}) custom-call(s32[1]{0:T(128)} %bitcast.core, s32[2,4,3]{2,1,0:T(4,128)S(1)} %pad_add_fusion.lists, s32[8,6]{1,0:T(8,128)S(1)} %index.1, f32[8,64,128]{2,1,0:T(8,128)S(1)} %get-tuple-element.65.own_ref.refs_0_.refs_2_.refs_4_, ...), custom_call_target="tpu_custom_call" | custom-call | flops 805306368 | bytes 6291456 | tf_op jit(solution)/shard_map/step/pallas_call | solution.py:346
  108.9 4.1 %collective-permute-start.16 = (f32[7,64,128]{2,1,0:T(8,128)S(1)}, f32[7,64,128]{2,1,0:T(8,128)S(1)}, u32[]{:S(2)}, u32[]{:S(2)}) collective-permute-start(f32[7,64,128]{2,1,0:T(8,128)S(1)} %get-tuple-element.69), channel_id=1, source_target_pairs={{0,30},{1,31},{2,0},{3,1},{4,2},{5,3},{6,4},{7,5},{8,6},{9,7},{10,... | collective-permute-start | bytes 688136 | tf_op jit(solution)/shard_map/ppermute | solution.py:258
  113.0 3.7 %collective-permute-done.28.fl_ref = f32[7,64,128]{2,1,0:T(8,128)S(1)} collective-permute-done((f32[7,64,128]{2,1,0:T(8,128)S(1)}, f32[7,64,128]{2,1,0:T(8,128)S(1)}, u32[]{:S(2)}, u32[]{:S(2)}) %collective-permute-start.28) | collective-permute-done | bytes 229408 | tf_op jit(solution)/shard_map/ppermute | solution.py:258
  116.7 2.0 %step.21.refs_1_.refs_2_.refs_12_ = f32[8,64,128]{2,1,0:T(8,128)S(1)} custom-call(s32[1]{0:T(128)} %bitcast.core, s32[2,4,3]{2,1,0:T(4,128)S(1)} %pad_add_fusion.lists, s32[8,6]{1,0:T(8,128)S(1)} %index.1, f32[8,64,128]{2,1,0:T(8,128)S(1)} %get-tuple-element.85.own_ref.refs_1_.refs_3_.refs_11_, f32[7,64,128]{2,1,0:T(8,128)S(1)} %collective-permute-done.27.fr_ref, ...), custom_call_target="tpu_custom_call" | custom-call | flops 805306368 | bytes 6291456 | tf_op jit(solution)/shard_map/step/pallas_call | solution.py:346
  118.9 1.8 %collective-permute-done.16.fr_ref = f32[7,64,128]{2,1,0:T(8,128)S(1)} collective-permute-done((f32[7,64,128]{2,1,0:T(8,128)S(1)}, f32[7,64,128]{2,1,0:T(8,128)S(1)}, u32[]{:S(2)}, u32[]{:S(2)}) %collective-permute-start.16) | collective-permute-done | bytes 229408 | tf_op jit(solution)/shard_map/ppermute | solution.py:258
  120.6 2.1 %collective-permute-done.17.fl_ref = f32[7,64,128]{2,1,0:T(8,128)S(1)} collective-permute-done((f32[7,64,128]{2,1,0:T(8,128)S(1)}, f32[7,64,128]{2,1,0:T(8,128)S(1)}, u32[]{:S(2)}, u32[]{:S(2)}) %collective-permute-start.17) | collective-permute-done | bytes 229408 | tf_op jit(solution)/shard_map/ppermute | solution.py:258
  122.7 2.0 %step.16.refs_0_.refs_6_ = f32[8,64,128]{2,1,0:T(8,128)S(1)} custom-call(s32[1]{0:T(128)} %bitcast.core, s32[2,4,3]{2,1,0:T(4,128)S(1)} %pad_add_fusion.lists, s32[8,6]{1,0:T(8,128)S(1)} %index.1, f32[8,64,128]{2,1,0:T(8,128)S(1)} %get-tuple-element.68.own_ref.refs_0_.refs_1_.refs_5_, f32[7,64,128]{2,1,0:T(8,128)S(1)} %collective-permute-done.16.fr_ref, ...), custom_call_target="tpu_custom_call" | custom-call | flops 805306368 | bytes 6291456 | tf_op jit(solution)/shard_map/step/pallas_call | solution.py:346
  125.3 2.9 %collective-permute-start.30 = (f32[56,128]{1,0:T(8,128)S(1)}, f32[56,128]{1,0:T(8,128)S(1)}, u32[]{:S(2)}, u32[]{:S(2)}) collective-permute-start(f32[56,128]{1,0:T(8,128)S(1)} %constant_dynamic-update-slice_fusion), channel_id=1, source_target_pairs={{0,4},{1,5},{2,6},{3,7},{4,0},{5,1},{6,2},{7,3},{8,12},{9,13},{10,... | collective-permute-start | bytes 86024 | tf_op jit(solution)/shard_map/ppermute | solution.py:417
  128.2 1.4 collective-permute-start.31
  130.0 2.9 %collective-permute-done.31 = f32[56,128]{1,0:T(8,128)S(1)} collective-permute-done((f32[56,128]{1,0:T(8,128)S(1)}, f32[56,128]{1,0:T(8,128)S(1)}, u32[]{:S(2)}, u32[]{:S(2)}) %collective-permute-start.31) | collective-permute-done | bytes 28704 | tf_op jit(solution)/shard_map/ppermute | solution.py:417
  133.2 2.6 %collective-permute-start.33 = (f32[56,128]{1,0:T(8,128)S(1)}, f32[56,128]{1,0:T(8,128)S(1)}, u32[]{:S(2)}, u32[]{:S(2)}) collective-permute-start(f32[56,128]{1,0:T(8,128)S(1)} %add_add_fusion.1), channel_id=1, source_target_pairs={{0,16},{1,17},{2,18},{3,19},{4,20},{5,21},{6,22},{7,23},{8,24},{9,... | collective-permute-start | bytes 86024 | tf_op jit(solution)/shard_map/ppermute | solution.py:417
  135.8 1.7 %collective-permute-start.34 = (f32[56,128]{1,0:T(8,128)S(1)}, f32[56,128]{1,0:T(8,128)S(1)}, u32[]{:S(2)}, u32[]{:S(2)}) collective-permute-start(f32[56,128]{1,0:T(8,128)S(1)} %add_add_fusion.1), channel_id=1, source_target_pairs={{0,24},{1,25},{2,26},{3,27},{4,28},{5,29},{6,30},{7,31},{8,16},{9,... | collective-permute-start | bytes 86024 | tf_op jit(solution)/shard_map/ppermute | solution.py:417
  138.1 3.4 %collective-permute-done.34 = f32[56,128]{1,0:T(8,128)S(1)} collective-permute-done((f32[56,128]{1,0:T(8,128)S(1)}, f32[56,128]{1,0:T(8,128)S(1)}, u32[]{:S(2)}, u32[]{:S(2)}) %collective-permute-start.34) | collective-permute-done | bytes 28704 | tf_op jit(solution)/shard_map/ppermute | solution.py:417
  142.8 1.3 collective-permute-done.35.other_ref
  144.1 1.0 unpack.1
  (73 shorter events, 9.3 us)
Async XLA Ops:
  0.6 30.4 %collective-permute-start.7 = (f32[4,6,128,128]{3,2,1,0:T(8,128)}, f32[4,6,128,128]{3,2,1,0:T(8,128)S(1)}, u32[]{:S(2)}, u32[]{:S(2)}) collective-permute-start(f32[4,6,128,128]{3,2,1,0:T(8,128)} %a_ref.1), channel_id=1, source_target_pairs={{0,1},{1,0},{2,3},{3,2},{4,5},{5,4},{6,7},{7,6},{8,9},{9,8},{10,11... | collective-permute-start | bytes 4718600 | tf_op jit(solution)/shard_map/ppermute | solution.py:258
  1.2 0.9 copy-start.1
  2.3 3.7 %collective-permute-start.1 = (f32[4,64,128]{2,1,0:T(8,128)S(1)}, f32[4,64,128]{2,1,0:T(8,128)S(1)}, u32[]{:S(2)}, u32[]{:S(2)}) collective-permute-start(f32[4,64,128]{2,1,0:T(8,128)S(1)} %get-tuple-element.48), channel_id=1, source_target_pairs={{0,1},{1,0},{2,3},{3,2},{4,5},{5,4},{6,7},{7,6},{8,9},{9,8},{10,11... | collective-permute-start | bytes 393224 | tf_op jit(solution)/shard_map/ppermute | solution.py:258
  2.4 0.9 copy-start.2
  3.5 9.9 %collective-permute-start.18 = (f32[4,64,128]{2,1,0:T(8,128)S(1)}, f32[4,64,128]{2,1,0:T(8,128)S(1)}, u32[]{:S(2)}, u32[]{:S(2)}) collective-permute-start(f32[4,64,128]{2,1,0:T(8,128)S(1)} %get-tuple-element.72), channel_id=1, source_target_pairs={{0,1},{1,0},{2,3},{3,2},{4,5},{5,4},{6,7},{7,6},{8,9},{9,8},{10,11... | collective-permute-start | bytes 393224 | tf_op jit(solution)/shard_map/ppermute | solution.py:258
  4.8 1.2 collective-permute-start
  6.6 24.8 %collective-permute-start.5 = (f32[7,64,128]{2,1,0:T(8,128)S(1)}, f32[7,64,128]{2,1,0:T(8,128)S(1)}, u32[]{:S(2)}, u32[]{:S(2)}) collective-permute-start(f32[7,64,128]{2,1,0:T(8,128)S(1)} %get-tuple-element.50), channel_id=1, source_target_pairs={{0,30},{1,31},{2,0},{3,1},{4,2},{5,3},{6,4},{7,5},{8,6},{9,7},{10,... | collective-permute-start | bytes 688136 | tf_op jit(solution)/shard_map/ppermute | solution.py:258
  13.3 18.1 %collective-permute-start.6 = (f32[7,64,128]{2,1,0:T(8,128)S(1)}, f32[7,64,128]{2,1,0:T(8,128)S(1)}, u32[]{:S(2)}, u32[]{:S(2)}) collective-permute-start(f32[7,64,128]{2,1,0:T(8,128)S(1)} %get-tuple-element.51), channel_id=1, source_target_pairs={{0,2},{1,3},{2,4},{3,5},{4,6},{5,7},{6,8},{7,9},{8,10},{9,11},{10,... | collective-permute-start | bytes 688136 | tf_op jit(solution)/shard_map/ppermute | solution.py:258
  13.3 6.3 %collective-permute-start.4 = (s32[4,6]{1,0:T(4,128)}, s32[4,6]{1,0:T(4,128)S(1)}, u32[]{:S(2)}, u32[]{:S(2)}) collective-permute-start(s32[4,6]{1,0:T(4,128)} %param.10), channel_id=1, source_target_pairs={{0,1},{1,0},{2,3},{3,2},{4,5},{5,4},{6,7},{7,6},{8,9},{9,8},{10,11... | collective-permute-start | bytes 296 | tf_op jit(solution)/shard_map/ppermute | solution.py:258
  13.4 7.1 %collective-permute-start.2 = (s32[2,4,3]{2,1,0:T(4,128)S(1)}, s32[2,4,3]{2,1,0:T(4,128)S(1)}, u32[]{:S(2)}, u32[]{:S(2)}) collective-permute-start(s32[2,4,3]{2,1,0:T(4,128)S(1)} %pad_add_fusion.lists), channel_id=1, source_target_pairs={{0,30},{1,31},{2,0},{3,1},{4,2},{5,3},{6,4},{7,5},{8,6},{9,7},{10,... | collective-permute-start | bytes 296 | tf_op jit(solution)/shard_map/ppermute | solution.py:258
  19.6 7.4 %collective-permute-start.3 = (s32[2,4,3]{2,1,0:T(4,128)S(1)}, s32[2,4,3]{2,1,0:T(4,128)S(1)}, u32[]{:S(2)}, u32[]{:S(2)}) collective-permute-start(s32[2,4,3]{2,1,0:T(4,128)S(1)} %pad_add_fusion.lists), channel_id=1, source_target_pairs={{0,2},{1,3},{2,4},{3,5},{4,6},{5,7},{6,8},{7,9},{8,10},{9,11},{10,... | collective-permute-start | bytes 296 | tf_op jit(solution)/shard_map/ppermute | solution.py:258
  20.5 18.7 %collective-permute-start.19 = (f32[7,64,128]{2,1,0:T(8,128)S(1)}, f32[7,64,128]{2,1,0:T(8,128)S(1)}, u32[]{:S(2)}, u32[]{:S(2)}) collective-permute-start(f32[7,64,128]{2,1,0:T(8,128)S(1)} %get-tuple-element.74), channel_id=1, source_target_pairs={{0,30},{1,31},{2,0},{3,1},{4,2},{5,3},{6,4},{7,5},{8,6},{9,7},{10,... | collective-permute-start | bytes 688136 | tf_op jit(solution)/shard_map/ppermute | solution.py:258
  26.9 12.2 %collective-permute-start.20 = (f32[7,64,128]{2,1,0:T(8,128)S(1)}, f32[7,64,128]{2,1,0:T(8,128)S(1)}, u32[]{:S(2)}, u32[]{:S(2)}) collective-permute-start(f32[7,64,128]{2,1,0:T(8,128)S(1)} %get-tuple-element.75), channel_id=1, source_target_pairs={{0,2},{1,3},{2,4},{3,5},{4,6},{5,7},{6,8},{7,9},{8,10},{9,11},{10,... | collective-permute-start | bytes 688136 | tf_op jit(solution)/shard_map/ppermute | solution.py:258
  27.6 1.4 copy-start
  33.4 13.4 %collective-permute-start.8 = (f32[7,64,128]{2,1,0:T(8,128)S(1)}, f32[7,64,128]{2,1,0:T(8,128)S(1)}, u32[]{:S(2)}, u32[]{:S(2)}) collective-permute-start(f32[7,64,128]{2,1,0:T(8,128)S(1)} %get-tuple-element.57), channel_id=1, source_target_pairs={{0,30},{1,31},{2,0},{3,1},{4,2},{5,3},{6,4},{7,5},{8,6},{9,7},{10,... | collective-permute-start | bytes 688136 | tf_op jit(solution)/shard_map/ppermute | solution.py:258
  39.1 9.7 %collective-permute-start.9 = (f32[7,64,128]{2,1,0:T(8,128)S(1)}, f32[7,64,128]{2,1,0:T(8,128)S(1)}, u32[]{:S(2)}, u32[]{:S(2)}) collective-permute-start(f32[7,64,128]{2,1,0:T(8,128)S(1)} %get-tuple-element.58), channel_id=1, source_target_pairs={{0,2},{1,3},{2,4},{3,5},{4,6},{5,7},{6,8},{7,9},{8,10},{9,11},{10,... | collective-permute-start | bytes 688136 | tf_op jit(solution)/shard_map/ppermute | solution.py:258
  41.1 13.4 %collective-permute-start.21 = (f32[7,64,128]{2,1,0:T(8,128)S(1)}, f32[7,64,128]{2,1,0:T(8,128)S(1)}, u32[]{:S(2)}, u32[]{:S(2)}) collective-permute-start(f32[7,64,128]{2,1,0:T(8,128)S(1)} %get-tuple-element.77), channel_id=1, source_target_pairs={{0,30},{1,31},{2,0},{3,1},{4,2},{5,3},{6,4},{7,5},{8,6},{9,7},{10,... | collective-permute-start | bytes 688136 | tf_op jit(solution)/shard_map/ppermute | solution.py:258
  46.8 10.9 %collective-permute-start.22 = (f32[7,64,128]{2,1,0:T(8,128)S(1)}, f32[7,64,128]{2,1,0:T(8,128)S(1)}, u32[]{:S(2)}, u32[]{:S(2)}) collective-permute-start(f32[7,64,128]{2,1,0:T(8,128)S(1)} %get-tuple-element.78), channel_id=1, source_target_pairs={{0,2},{1,3},{2,4},{3,5},{4,6},{5,7},{6,8},{7,9},{8,10},{9,11},{10,... | collective-permute-start | bytes 688136 | tf_op jit(solution)/shard_map/ppermute | solution.py:258
  50.8 13.0 %collective-permute-start.10 = (f32[7,64,128]{2,1,0:T(8,128)S(1)}, f32[7,64,128]{2,1,0:T(8,128)S(1)}, u32[]{:S(2)}, u32[]{:S(2)}) collective-permute-start(f32[7,64,128]{2,1,0:T(8,128)S(1)} %get-tuple-element.60), channel_id=1, source_target_pairs={{0,30},{1,31},{2,0},{3,1},{4,2},{5,3},{6,4},{7,5},{8,6},{9,7},{10,... | collective-permute-start | bytes 688136 | tf_op jit(solution)/shard_map/ppermute | solution.py:258
  54.5 13.0 %collective-permute-start.11 = (f32[7,64,128]{2,1,0:T(8,128)S(1)}, f32[7,64,128]{2,1,0:T(8,128)S(1)}, u32[]{:S(2)}, u32[]{:S(2)}) collective-permute-start(f32[7,64,128]{2,1,0:T(8,128)S(1)} %get-tuple-element.61), channel_id=1, source_target_pairs={{0,2},{1,3},{2,4},{3,5},{4,6},{5,7},{6,8},{7,9},{8,10},{9,11},{10,... | collective-permute-start | bytes 688136 | tf_op jit(solution)/shard_map/ppermute | solution.py:258
  59.7 14.0 %collective-permute-start.23 = (f32[7,64,128]{2,1,0:T(8,128)S(1)}, f32[7,64,128]{2,1,0:T(8,128)S(1)}, u32[]{:S(2)}, u32[]{:S(2)}) collective-permute-start(f32[7,64,128]{2,1,0:T(8,128)S(1)} %get-tuple-element.80), channel_id=1, source_target_pairs={{0,30},{1,31},{2,0},{3,1},{4,2},{5,3},{6,4},{7,5},{8,6},{9,7},{10,... | collective-permute-start | bytes 688136 | tf_op jit(solution)/shard_map/ppermute | solution.py:258
  63.8 13.6 %collective-permute-start.24 = (f32[7,64,128]{2,1,0:T(8,128)S(1)}, f32[7,64,128]{2,1,0:T(8,128)S(1)}, u32[]{:S(2)}, u32[]{:S(2)}) collective-permute-start(f32[7,64,128]{2,1,0:T(8,128)S(1)} %get-tuple-element.81), channel_id=1, source_target_pairs={{0,2},{1,3},{2,4},{3,5},{4,6},{5,7},{6,8},{7,9},{8,10},{9,11},{10,... | collective-permute-start | bytes 688136 | tf_op jit(solution)/shard_map/ppermute | solution.py:258
  69.6 14.1 %collective-permute-start.12 = (f32[7,64,128]{2,1,0:T(8,128)S(1)}, f32[7,64,128]{2,1,0:T(8,128)S(1)}, u32[]{:S(2)}, u32[]{:S(2)}) collective-permute-start(f32[7,64,128]{2,1,0:T(8,128)S(1)} %get-tuple-element.63), channel_id=1, source_target_pairs={{0,30},{1,31},{2,0},{3,1},{4,2},{5,3},{6,4},{7,5},{8,6},{9,7},{10,... | collective-permute-start | bytes 688136 | tf_op jit(solution)/shard_map/ppermute | solution.py:258
  73.6 13.6 %collective-permute-start.13 = (f32[7,64,128]{2,1,0:T(8,128)S(1)}, f32[7,64,128]{2,1,0:T(8,128)S(1)}, u32[]{:S(2)}, u32[]{:S(2)}) collective-permute-start(f32[7,64,128]{2,1,0:T(8,128)S(1)} %get-tuple-element.64), channel_id=1, source_target_pairs={{0,2},{1,3},{2,4},{3,5},{4,6},{5,7},{6,8},{7,9},{8,10},{9,11},{10,... | collective-permute-start | bytes 688136 | tf_op jit(solution)/shard_map/ppermute | solution.py:258
  79.4 14.1 %collective-permute-start.25 = (f32[7,64,128]{2,1,0:T(8,128)S(1)}, f32[7,64,128]{2,1,0:T(8,128)S(1)}, u32[]{:S(2)}, u32[]{:S(2)}) collective-permute-start(f32[7,64,128]{2,1,0:T(8,128)S(1)} %get-tuple-element.83), channel_id=1, source_target_pairs={{0,30},{1,31},{2,0},{3,1},{4,2},{5,3},{6,4},{7,5},{8,6},{9,7},{10,... | collective-permute-start | bytes 688136 | tf_op jit(solution)/shard_map/ppermute | solution.py:258
  83.5 13.6 %collective-permute-start.26 = (f32[7,64,128]{2,1,0:T(8,128)S(1)}, f32[7,64,128]{2,1,0:T(8,128)S(1)}, u32[]{:S(2)}, u32[]{:S(2)}) collective-permute-start(f32[7,64,128]{2,1,0:T(8,128)S(1)} %get-tuple-element.84), channel_id=1, source_target_pairs={{0,2},{1,3},{2,4},{3,5},{4,6},{5,7},{6,8},{7,9},{8,10},{9,11},{10,... | collective-permute-start | bytes 688136 | tf_op jit(solution)/shard_map/ppermute | solution.py:258
  89.2 14.1 %collective-permute-start.14 = (f32[7,64,128]{2,1,0:T(8,128)S(1)}, f32[7,64,128]{2,1,0:T(8,128)S(1)}, u32[]{:S(2)}, u32[]{:S(2)}) collective-permute-start(f32[7,64,128]{2,1,0:T(8,128)S(1)} %get-tuple-element.66), channel_id=1, source_target_pairs={{0,30},{1,31},{2,0},{3,1},{4,2},{5,3},{6,4},{7,5},{8,6},{9,7},{10,... | collective-permute-start | bytes 688136 | tf_op jit(solution)/shard_map/ppermute | solution.py:258
  93.3 13.6 %collective-permute-start.15 = (f32[7,64,128]{2,1,0:T(8,128)S(1)}, f32[7,64,128]{2,1,0:T(8,128)S(1)}, u32[]{:S(2)}, u32[]{:S(2)}) collective-permute-start(f32[7,64,128]{2,1,0:T(8,128)S(1)} %get-tuple-element.67), channel_id=1, source_target_pairs={{0,2},{1,3},{2,4},{3,5},{4,6},{5,7},{6,8},{7,9},{8,10},{9,11},{10,... | collective-permute-start | bytes 688136 | tf_op jit(solution)/shard_map/ppermute | solution.py:258
  99.1 13.9 %collective-permute-start.27 = (f32[7,64,128]{2,1,0:T(8,128)S(1)}, f32[7,64,128]{2,1,0:T(8,128)S(1)}, u32[]{:S(2)}, u32[]{:S(2)}) collective-permute-start(f32[7,64,128]{2,1,0:T(8,128)S(1)} %get-tuple-element.86), channel_id=1, source_target_pairs={{0,30},{1,31},{2,0},{3,1},{4,2},{5,3},{6,4},{7,5},{8,6},{9,7},{10,... | collective-permute-start | bytes 688136 | tf_op jit(solution)/shard_map/ppermute | solution.py:258
  103.1 13.6 %collective-permute-start.28 = (f32[7,64,128]{2,1,0:T(8,128)S(1)}, f32[7,64,128]{2,1,0:T(8,128)S(1)}, u32[]{:S(2)}, u32[]{:S(2)}) collective-permute-start(f32[7,64,128]{2,1,0:T(8,128)S(1)} %get-tuple-element.87), channel_id=1, source_target_pairs={{0,2},{1,3},{2,4},{3,5},{4,6},{5,7},{6,8},{7,9},{8,10},{9,11},{10,... | collective-permute-start | bytes 688136 | tf_op jit(solution)/shard_map/ppermute | solution.py:258
  108.9 11.7 %collective-permute-start.16 = (f32[7,64,128]{2,1,0:T(8,128)S(1)}, f32[7,64,128]{2,1,0:T(8,128)S(1)}, u32[]{:S(2)}, u32[]{:S(2)}) collective-permute-start(f32[7,64,128]{2,1,0:T(8,128)S(1)} %get-tuple-element.69), channel_id=1, source_target_pairs={{0,30},{1,31},{2,0},{3,1},{4,2},{5,3},{6,4},{7,5},{8,6},{9,7},{10,... | collective-permute-start | bytes 688136 | tf_op jit(solution)/shard_map/ppermute | solution.py:258
  113.0 9.7 %collective-permute-start.17 = (f32[7,64,128]{2,1,0:T(8,128)S(1)}, f32[7,64,128]{2,1,0:T(8,128)S(1)}, u32[]{:S(2)}, u32[]{:S(2)}) collective-permute-start(f32[7,64,128]{2,1,0:T(8,128)S(1)} %get-tuple-element.70), channel_id=1, source_target_pairs={{0,2},{1,3},{2,4},{3,5},{4,6},{5,7},{6,8},{7,9},{8,10},{9,11},{10,... | collective-permute-start | bytes 688136 | tf_op jit(solution)/shard_map/ppermute | solution.py:258
  124.8 4.8 %collective-permute-start.29 = (f32[56,128]{1,0:T(8,128)S(1)}, f32[56,128]{1,0:T(8,128)S(1)}, u32[]{:S(2)}, u32[]{:S(2)}) collective-permute-start(f32[56,128]{1,0:T(8,128)S(1)} %constant_dynamic-update-slice_fusion), channel_id=1, source_target_pairs={{0,2},{1,3},{2,0},{3,1},{4,6},{5,7},{6,4},{7,5},{8,10},{9,11},{10,... | collective-permute-start | bytes 86024 | tf_op jit(solution)/shard_map/ppermute | solution.py:417
  125.3 4.7 %collective-permute-start.30 = (f32[56,128]{1,0:T(8,128)S(1)}, f32[56,128]{1,0:T(8,128)S(1)}, u32[]{:S(2)}, u32[]{:S(2)}) collective-permute-start(f32[56,128]{1,0:T(8,128)S(1)} %constant_dynamic-update-slice_fusion), channel_id=1, source_target_pairs={{0,4},{1,5},{2,6},{3,7},{4,0},{5,1},{6,2},{7,3},{8,12},{9,13},{10,... | collective-permute-start | bytes 86024 | tf_op jit(solution)/shard_map/ppermute | solution.py:417
  128.2 4.8 %collective-permute-start.31 = (f32[56,128]{1,0:T(8,128)S(1)}, f32[56,128]{1,0:T(8,128)S(1)}, u32[]{:S(2)}, u32[]{:S(2)}) collective-permute-start(f32[56,128]{1,0:T(8,128)S(1)} %constant_dynamic-update-slice_fusion), channel_id=1, source_target_pairs={{0,6},{1,7},{2,4},{3,5},{4,2},{5,3},{6,0},{7,1},{8,14},{9,15},{10,... | collective-permute-start | bytes 86024 | tf_op jit(solution)/shard_map/ppermute | solution.py:417
  133.0 4.5 %collective-permute-start.32 = (f32[56,128]{1,0:T(8,128)S(1)}, f32[56,128]{1,0:T(8,128)S(1)}, u32[]{:S(2)}, u32[]{:S(2)}) collective-permute-start(f32[56,128]{1,0:T(8,128)S(1)} %add_add_fusion.1), channel_id=1, source_target_pairs={{0,8},{1,9},{2,10},{3,11},{4,12},{5,13},{6,14},{7,15},{8,0},{9,1},... | collective-permute-start | bytes 86024 | tf_op jit(solution)/shard_map/ppermute | solution.py:417
  133.2 4.9 %collective-permute-start.33 = (f32[56,128]{1,0:T(8,128)S(1)}, f32[56,128]{1,0:T(8,128)S(1)}, u32[]{:S(2)}, u32[]{:S(2)}) collective-permute-start(f32[56,128]{1,0:T(8,128)S(1)} %add_add_fusion.1), channel_id=1, source_target_pairs={{0,16},{1,17},{2,18},{3,19},{4,20},{5,21},{6,22},{7,23},{8,24},{9,... | collective-permute-start | bytes 86024 | tf_op jit(solution)/shard_map/ppermute | solution.py:417
  135.8 5.7 %collective-permute-start.34 = (f32[56,128]{1,0:T(8,128)S(1)}, f32[56,128]{1,0:T(8,128)S(1)}, u32[]{:S(2)}, u32[]{:S(2)}) collective-permute-start(f32[56,128]{1,0:T(8,128)S(1)} %add_add_fusion.1), channel_id=1, source_target_pairs={{0,24},{1,25},{2,26},{3,27},{4,28},{5,29},{6,30},{7,31},{8,16},{9,... | collective-permute-start | bytes 86024 | tf_op jit(solution)/shard_map/ppermute | solution.py:417
  142.3 1.8 %copy-start.3 = (f32[512,128]{1,0:T(8,128)S(1)}, f32[512,128]{1,0:T(8,128)}, u32[]{:S(2)}) copy-start(f32[512,128]{1,0:T(8,128)} %param.6) | copy-start | bytes 786436
  142.3 1.8 %collective-permute-start.35 = (f32[12,64,128]{2,1,0:T(8,128)S(1)}, f32[12,64,128]{2,1,0:T(8,128)S(1)}, u32[]{:S(2)}, u32[]{:S(2)}) collective-permute-start(f32[12,64,128]{2,1,0:T(8,128)S(1)} %combine.3), channel_id=1, source_target_pairs={{0,1},{1,0},{2,3},{3,2},{4,5},{5,4},{6,7},{7,6},{8,9},{9,8},{10,11... | collective-permute-start | bytes 1179656 | tf_op jit(solution)/shard_map/ppermute | solution.py:258
